TPU v7x, 128 devices: a whole 4x4x4 slice. The times are simulated.
128 devices in a mesh: pts: 16 (over z_hi, x, core), wlk: 8 (over z_lo, y).
Axes of the slice: x: 4, y: 4, z: 4 (z_hi: 2, z_lo: 2; z = z_hi * 2 + z_lo), core: 2. Of those that a mesh axis runs over, the one named last changes fastest.
Arguments:
- green_half: bfloat16 [16, 400, 2400], P('wlk'), may hold values from -6 to 6
- collocation: bfloat16 [2400, 9600], P('wlk', 'pts'), may hold values from -0.125 to 0.125
- occupied: bfloat16 [9600, 400], P('pts'), may hold values from -0.0029296875 to 0.0029296875
- kernel: bfloat16 [9600, 9600], P('pts'), may hold values from 0 to 16, as said below
Outputs:
- potential: float32 [16, 9600], P('wlk', 'pts')
- coulomb_energy: float32 [16], P('wlk')
- exchange_energy: float32 [16], P('wlk')
Inputs may be any that keep to these rules, and one draw needn't show every extreme that they name: kernel is symmetric and positive definite: kernel[p, q] equals kernel[q, p].
All inputs are finite; a program needn't handle non-finite values.
Results may differ from a plain program's by a relative error of at most 0.008.
Values may be sent and summed in bfloat16 or wider, within the bound.
No kernel may reach another device: no remote copies, remote signals or barrier semaphores. Data moves between devices by JAX's collectives and lax.ppermute only.
A program may use at most 192 MiB of HBM per device.

v0:
```python
import jax
import jax.numpy as jnp
from jax import lax
from jax.experimental import pallas as pl
from jax.experimental.pallas import tpu as pltpu
from jax.sharding import PartitionSpec as P


F32 = jnp.float32
BF16 = jnp.bfloat16
PLANES, COLS, CORES = 2, 4, 2
ZLO, YS = 2, 4
EXTRA = 8
SLOTS = {
    "left": ((0, 3), (0, 3)),
    "right": ((0, 1), (0, 1)),
    "far": ((0, 2), (0, 2)),
    "side": ((1, 3), (1, 1)),
    "plane": ((1, 0), (1, 0)),
    "side2": ((1, 1), (1, 3)),
    "far2": ((1, 2), (1, 2)),
}
MIB = 1 << 20


def whole():
    return pl.BlockSpec(memory_space=pltpu.VMEM)


def scalars():
    return pl.BlockSpec(memory_space=pltpu.SMEM)


def params(mib):
    return pltpu.CompilerParams(vmem_limit_bytes=mib * MIB)


def pts_id(a, x, c):
    return ((a & (PLANES - 1)) * COLS + (x & (COLS - 1))) * CORES + (c & (CORES - 1))


def from_device(block, source):
    route = []
    for a in range(PLANES):
        for x in range(COLS):
            for c in range(CORES):
                for z in range(ZLO):
                    for y in range(YS):
                        sa, sx, sc, sz, sy = source(a, x, c, z, y)
                        start = pts_id(sa, sx, sc) * ZLO * YS + (sz & 1) * YS + (sy & 3)
                        route.append((start, pts_id(a, x, c) * ZLO * YS + z * YS + y))
    return lax.ppermute(block, ("pts", "wlk"), route)


def from_chip(block, da, dx, dc=0):
    return from_device(block, lambda a, x, c, z, y: (a + da, x + dx, c + dc, z, y))


def from_group(block, dz, dy):
    return from_device(block, lambda a, x, c, z, y: (a, x, c, z + dz, y + dy))


def from_column(block, slot):
    def source(a, x, c, z, y):
        return a, x + SLOTS[slot][(y ^ c) & 1][1], c, z, y

    return from_device(block, source)


def place(ids_ref):
    here = ids_ref[0]
    return here >> 3, (here >> 1) & 3, here & 1, ids_ref[1] & 3


def takes(slot, a, x, c, odd):
    low = jnp.where((x & 3) < COLS // 2, 1, 0)
    return {
        "own": c,
        "left": 0,
        "right": 1,
        "far": 1 - low,
        "side": odd,
        "plane": a,
        "side2": 1 - odd,
        "far2": low,
    }[slot]


def chip_of(slot, a, x, odd):
    (a0, x0), (a1, x1) = SLOTS.get(slot, ((0, 0), (0, 0)))
    return a + jnp.where(odd == 1, a1, a0), x + jnp.where(odd == 1, x1, x0)


def split_columns(array, pieces, steps, mib, room=1):
    rows, cols = array.shape
    width = cols // pieces
    tile = rows // steps

    def body(x_ref, o_ref):
        @pl.loop(0, tile // 40)
        def _(part):
            cut = pl.ds(pl.multiple_of(part * 40, 8), 40)
            for b in range(pieces):
                o_ref[b, cut, :] = x_ref[cut, b * width : (b + 1) * width]

    return pl.pallas_call(
        body,
        grid=(steps,),
        in_specs=[pl.BlockSpec((tile, cols), lambda i: (i, 0))],
        out_specs=pl.BlockSpec((pieces, tile, width), lambda i: (0, i, 0)),
        out_shape=jax.ShapeDtypeStruct((pieces * room, rows, width), array.dtype),
        compiler_params=params(mib),
    )(array)


def pick(ids, takes_second, one, two):
    def body(ids_ref, one_ref, two_ref, o_ref):
        second = takes_second(*place(ids_ref))

        @pl.when(second == 0)
        def _():
            o_ref[...] = one_ref[...]

        @pl.when(second != 0)
        def _():
            o_ref[...] = two_ref[...]

    return pl.pallas_call(
        body,
        in_specs=[scalars(), whole(), whole()],
        out_specs=whole(),
        out_shape=jax.ShapeDtypeStruct(one.shape, one.dtype),
        compiler_params=params(4),
    )(ids, one, two)


def group_block(ids_ref, key):
    zlo, y = ids_ref[1] >> 2, ids_ref[1] & 3
    return ((zlo + key[0]) & (ZLO - 1)) * YS + ((y + key[1]) & (YS - 1))


def theta_part(ids, green_cut, blocks, so_far=None, occ_t=None):
    keys = list(blocks)
    n = len(keys)
    rows = green_cut.shape[1]
    pts = blocks[keys[0]].shape[1]
    flops = 2 * rows * pts * green_cut.shape[2] * n
    cost = pl.CostEstimate(flops=flops, bytes_accessed=flops // 600, transcendentals=0)

    if occ_t is None:

        def part(ids_ref, g_ref, *refs):
            cs, o_ref = refs[:n], refs[-1]
            at = [group_block(ids_ref, key) for key in keys]

            @pl.loop(0, 2)
            def _(half):
                cut = pl.ds(pl.multiple_of(half * (rows // 2), 8), rows // 2)
                total = sum(
                    jnp.dot(g_ref[at[j], cut, :], cs[j][...], preferred_element_type=F32)
                    for j in range(n)
                )
                o_ref[cut, :] = total if so_far is None else refs[n][cut, :] + total

        more = () if so_far is None else (so_far,)
        return pl.pallas_call(
            part,
            in_specs=[scalars()] + [whole()] * (n + 1 + len(more)),
            out_specs=whole(),
            out_shape=jax.ShapeDtypeStruct((rows, pts), F32),
            cost_estimate=cost,
            compiler_params=params(8),
        )(ids, green_cut, *blocks.values(), *more)

    elec = occ_t.shape[0]

    def last(ids_ref, g_ref, *refs):
        cs = refs[:n]
        acc_ref, occ_ref, t0_ref, t1_ref, *pick_refs, dens_ref = refs[n:]
        at = [group_block(ids_ref, key) for key in keys]
        th_refs = (t0_ref, t1_ref)
        occ = occ_ref[...].astype(F32)
        dens = []
        for w in range(2):
            cut = pl.ds(w * elec, elec)
            t = acc_ref[cut, :] + sum(
                jnp.dot(g_ref[at[j], cut, :], cs[j][...], preferred_element_type=F32)
                for j in range(n)
            )
            t = t.astype(BF16)
            th_refs[w][0:elec, :] = t
            dens.append(jnp.sum(t.astype(F32) * occ, axis=0, keepdims=True))
        dens_ref[0:1, :] = dens[0]
        dens_ref[1:2, :] = dens[1]
        row = lax.broadcasted_iota(jnp.int32, (EXTRA, pts), 0)
        tail = jnp.where(row == 0, dens[0], jnp.where(row == 1, dens[1], 0.0)).astype(BF16)
        for w in range(2):
            th_refs[w][elec : elec + EXTRA, :] = tail
        a, x, c, y = place(ids_ref)
        odd = (y ^ c) & 1
        goes = (
            odd,
            1 - odd,
            takes("far", a, x + 2, c, odd),
            takes("own", a, x, 1 - c, odd),
        )
        for w, o_ref in zip(goes, pick_refs):

            @pl.when(w == 0)
            def _():
                o_ref[...] = t0_ref[...]

            @pl.when(w != 0)
            def _():
                o_ref[...] = t1_ref[...]

    slab = jax.ShapeDtypeStruct((elec + EXTRA, pts), BF16)
    return pl.pallas_call(
        last,
        in_specs=[scalars()] + [whole()] * (n + 3),
        out_specs=[whole()] * 7,
        out_shape=[slab] * 6 + [jax.ShapeDtypeStruct((2, pts), F32)],
        cost_estimate=cost,
        compiler_params=params(8),
    )(ids, green_cut, *blocks.values(), so_far, occ_t)


def exchange(jobs, ids, own, kernel_cut, acc=None, density=None):
    n = len(jobs)
    elec, pts = jobs[0][3][0].shape
    contract_last = (((1,), (1,)), ((), ()))
    occ_blocks, occ_first = [], []
    for job in jobs:
        occ_first.append(len(occ_blocks))
        occ_blocks += job[3]
    first = acc is None

    def body(ids_ref, k_ref, *refs):
        refs = list(refs)
        os = [refs.pop(0) for _ in occ_blocks]
        ts = [refs.pop(0) for _ in jobs]
        block_ref, near_ref, far_ref, sem, *flip_ref = refs[-5:] if first else refs[-4:]
        if first:
            ex_ref, pot_ref, own_ref = refs[:3]
            ex_ref[...] = jnp.zeros_like(ex_ref)
            pot_ref[...] = jnp.zeros_like(pot_ref)
        else:
            own_ref = refs[0]
            dens_ref, ex_ref, pot_ref, pot_out, vals_out = (
                (None, *refs[3:5], None, None) if density is None else refs[3:8]
            )
        a, x, c, y = place(ids_ref)

        def of_job(j, values):
            value = values[0]
            for i in range(1, n):
                value = jnp.where(j == i, values[i], value)
            return value

        starts, walkers, occ_at = [], [], []
        for (slot, core, walker, blocks, *_), at in zip(jobs, occ_first):
            odd = (y ^ c ^ core) & 1
            walkers.append(takes(slot, a, x, c, odd) if walker is None else walker)
            starts.append(pts_id(*chip_of(slot, a, x, odd), c + core))
            occ_at.append(at + odd if len(blocks) > 1 else at)

        def copy(j, block):
            return pltpu.make_async_copy(k_ref.at[block], block_ref.at[j], sem.at[j])

        for j in range(n):
            copy(j, starts[j]).start()
        if first:
            for to, block in enumerate((ts[0], ts[1], os[0])):
                flip_ref[0][0:elec, 0:pts] = block[0:elec, :].astype(F32)
                own_ref[to] = flip_ref[0][...].T[0:pts, 0:elec].astype(BF16)

        @pl.loop(0, n)
        def _(j):
            w = of_job(j, walkers)
            at = of_job(j, occ_at)
            occ, theta = os[0][...], ts[0][...]
            for i in range(1, len(os)):
                occ = jnp.where(at == i, os[i][...], occ)
            for i in range(1, n):
                theta = jnp.where(j == i, ts[i][...], theta)
            near_ref[...] = jnp.dot(own_ref[w], occ, preferred_element_type=F32)
            far_ref[...] = jnp.dot(own_ref[2], theta[0:elec, :], preferred_element_type=F32)
            copy(j, 0).wait()
            k = block_ref[j]
            prod = k.astype(F32) * near_ref[...] * far_ref[...]
            weight = of_job(j, [job[5] for job in jobs])
            ex_ref[w] += weight * jnp.sum(prod.reshape(pts // 8, 8, pts), axis=0)
            adds = of_job(j, [1.0 if job[6] else 0.0 for job in jobs])
            pot_ref[...] += adds * lax.dot_general(
                theta[elec : elec + EXTRA, :],
                k,
                contract_last,
                preferred_element_type=F32,
            )

        if density is not None:
            pot = pot_ref[0:2, :]
            pot_out[...] = pot
            lane = lax.broadcasted_iota(jnp.int32, (8, 128), 1)
            vals = jnp.zeros((8, 128), F32)
            for w in range(2):
                coulomb = 0.5 * jnp.sum(dens_ref[w : w + 1, :] * pot[w : w + 1, :])
                vals = jnp.where(lane == w, coulomb, vals)
                vals = jnp.where(lane == 2 + w, -0.5 * jnp.sum(ex_ref[w]), vals)
            vals_out[...] = vals

    shapes = [jax.ShapeDtypeStruct((2, 8, pts), F32), jax.ShapeDtypeStruct((EXTRA, pts), F32)]
    flops = 4 * pts * pts * elec * n
    operands = [ids, kernel_cut] + occ_blocks + [job[4] for job in jobs]
    scratch = [
        pltpu.VMEM((n, pts, pts), BF16),
        pltpu.VMEM((pts, pts), F32),
        pltpu.VMEM((pts, pts), F32),
        pltpu.SemaphoreType.DMA((n,)),
    ]
    alias = {}
    if first:
        shapes += [jax.ShapeDtypeStruct((3, pts, elec), BF16)]
        scratch += [pltpu.VMEM((-(-elec // 128) * 128, -(-pts // 128) * 128), F32)]
    else:
        operands += [own]
        alias = {len(operands): 0, len(operands) + 1: 1}
        operands += acc
    if density is not None:
        operands += [density]
        shapes += [jax.ShapeDtypeStruct((2, pts), F32), jax.ShapeDtypeStruct((8, 128), F32)]
    return pl.pallas_call(
        body,
        in_specs=[scalars(), pl.BlockSpec(memory_space=pl.ANY)]
        + [whole()] * (len(operands) - 2),
        out_specs=[whole()] * len(shapes),
        out_shape=shapes,
        scratch_shapes=scratch,
        input_output_aliases=alias,
        cost_estimate=pl.CostEstimate(flops=flops, bytes_accessed=flops // 300, transcendentals=0),
        compiler_params=params(9),
    )(*operands)


def everyone_total(v):
    v = v + from_chip(v, 0, 0, 1)
    r1, r2, r3 = (from_chip(v, 0, dx) for dx in (1, 2, 3))
    v = (v + r2) + (r1 + r3)
    return v + from_chip(v, 1, 0)


def local(green_half, collocation, occupied, kernel):
    walkers, elec, orb = green_half.shape
    groups = ZLO * YS
    ids = jnp.stack([lax.axis_index("pts"), lax.axis_index("wlk")]).astype(jnp.int32)
    occ_t = occupied.T

    coll = {(0, 0): collocation}
    coll[1, 0] = from_group(collocation, 1, 0)
    for dy in (2, 1, 3):
        coll[0, dy] = from_group(collocation, 0, dy)
    for dy in (1, 3):
        coll[1, dy] = from_group(coll[1, 0], 0, dy)
    coll[1, 2] = from_group(coll[0, 2], 1, 0)
    occ_left = from_column(occ_t, "left")
    occ_right = from_column(occ_t, "right")
    occ_plane = from_chip(occ_t, 1, 0)
    occ_side = from_column(occ_plane, "side")
    occ_pick = pick(ids, lambda a, x, c, y: (y ^ c) & 1, occ_t, occ_plane)
    occ_far = from_column(occ_pick, "far")

    def from_y(block):
        return from_device(block, lambda a, x, c, z, y: (a, x, c, z, y ^ 1))

    occ_side2 = from_y(occ_side)
    occ_far2 = from_y(occ_far)
    occ = {"own": [occ_t], "left": [occ_left], "right": [occ_right], "far": [occ_far, occ_far2]}
    occ |= {"side": [occ_side], "plane": [occ_plane], "side2": [occ_side2]}

    green_cut = split_columns(green_half.reshape(walkers * elec, orb), groups, 4, 8)

    kernel_cut = split_columns(kernel, PLANES * COLS * CORES, 15, 6, 5)

    def some(keys):
        return {k: coll[k] for k in keys}

    so_far = theta_part(ids, green_cut, some([(0, 0), (1, 0), (0, 2)]))
    so_far = theta_part(ids, green_cut, some([(0, 1), (0, 3), (1, 1), (1, 3)]), so_far)
    t0, t1, t_first, t_second, t_far, t_sib, density = theta_part(
        ids, green_cut, some([(1, 2)]), so_far, occ_t
    )
    first = from_chip(t_first, 1, 0)
    second = from_chip(t_second, 1, 0)
    plane = pick(ids, lambda a, x, c, y: a ^ (y ^ c) & 1, first, second)
    far2 = pick(ids, lambda a, x, c, y: x >> 1 ^ (y ^ c) & 1, first, second)
    theta = {
        "left": from_column(t0, "left"),
        "right": from_column(t1, "right"),
        "far": from_column(t_far, "far"),
        "side": from_column(first, "side"),
        "plane": plane,
        "side2": from_column(second, "side2"),
        "far2": from_column(far2, "far2"),
    }
    theta_sib = {"own": from_chip(t_sib, 0, 0, 1)}
    occ_sib = {slot: [from_chip(block, 0, 0, 1) for block in occ[slot][:1]] for slot in occ}
    occ_sib["far"] += [from_chip(occ_far2, 0, 0, 1)]
    for known in (occ, occ_sib):
        known["far2"] = known["far"][::-1]
    *acc, own = exchange(
        [
            ("own", 0, 0, [occ_t], t0, 1.0, True),
            ("own", 0, 1, [occ_t], t1, 1.0, False),
            ("own", 1, None, occ_sib["own"], theta_sib["own"], 2.0, True),
        ],
        ids,
        None,
        kernel_cut,
    )
    for slot in SLOTS:
        theta_sib[slot] = from_chip(theta[slot], 0, 0, 1)
        same = (slot, 0, None, occ[slot], theta[slot], 2.0, True)
        sib = (slot, 1, None, occ_sib[slot], theta_sib[slot], 2.0, True)
        if slot == list(SLOTS)[-1]:
            acc = exchange([same], ids, own, kernel_cut, acc)
            acc = exchange([sib], ids, own, kernel_cut, acc, density)
        else:
            acc = exchange([same, sib], ids, own, kernel_cut, acc)
    _, _, potential, energies = acc
    energies = everyone_total(energies)
    return potential, energies[0, :walkers], energies[0, walkers : 2 * walkers]


def solution(mesh):
    placed = (P("wlk", None, None), P("wlk", "pts"), P("pts", None), P("pts", None))

    return jax.shard_map(
        local,
        mesh=mesh,
        in_specs=placed,
        out_specs=(P("wlk", "pts"), P("wlk"), P("wlk")),
        check_vma=False,
    )
```

profile of v0, /device:TPU:1, one launch (start us, length us, event | category | flops | bytes accessed | tf_op | source)
XLA Modules:
  0.0 174.2 jit_solution(7894738810404803857)
XLA Ops:
  0.6 2.5 %collective-permute-start.9 = (bf16[300,600]{1,0:T(8,128)(2,1)}, bf16[300,600]{1,0:T(8,128)(2,1)S(1)}, u32[]{:S(2)}, u32[]{:S(2)}) collective-permute-start(bf16[300,600]{1,0:T(8,128)(2,1)} %refs_0_.1), channel_id=1, source_target_pairs={{4,0},{5,1},{6,2},{7,3},{0,4},{1,5},{2,6},{3,7},{12,8},{13,9},{14,... | collective-permute-start | bytes 1080008 | tf_op jit(solution)/shard_map/ppermute | solution.py:52
  3.2 2.9 %collective-permute-start.5 = (bf16[300,600]{1,0:T(8,128)(2,1)}, bf16[300,600]{1,0:T(8,128)(2,1)}, u32[]{:S(2)}, u32[]{:S(2)}) collective-permute-start(bf16[300,600]{1,0:T(8,128)(2,1)} %refs_0_.1), channel_id=1, source_target_pairs={{2,0},{3,1},{0,2},{1,3},{6,4},{7,5},{4,6},{5,7},{10,8},{11,9},{8,1... | collective-permute-start | bytes 1080008 | tf_op jit(solution)/shard_map/ppermute | solution.py:52
  6.1 0.8 collective-permute-start.7
  6.9 1.2 collective-permute-start.34
  8.1 1.5 collective-permute-start.30
  9.5 2.7 %collective-permute-done.9.refs_1_ = bf16[300,600]{1,0:T(8,128)(2,1)S(1)} collective-permute-done((bf16[300,600]{1,0:T(8,128)(2,1)}, bf16[300,600]{1,0:T(8,128)(2,1)S(1)}, u32[]{:S(2)}, u32[]{:S(2)}) %collective-permute-start.9) | collective-permute-done | bytes 360032 | tf_op jit(solution)/shard_map/ppermute | solution.py:52
  12.2 3.1 %collective-permute-start = (bf16[400,600]{1,0:T(8,128)(2,1)}, bf16[400,600]{1,0:T(8,128)(2,1)S(1)}, u32[]{:S(2)}, u32[]{:S(2)}) collective-permute-start(bf16[400,600]{1,0:T(8,128)(2,1)} %bitcast.12), channel_id=1, source_target_pairs={{64,0},{65,1},{66,2},{67,3},{68,4},{69,5},{70,6},{71,7},{72,8},{73... | collective-permute-start | bytes 1440008 | tf_op jit(solution)/shard_map/ppermute | solution.py:52
  15.4 1.3 collective-permute-start.8
  16.7 6.9 %collective-permute-done.7.refs_0_ = bf16[300,600]{1,0:T(8,128)(2,1)S(1)} collective-permute-done((bf16[300,600]{1,0:T(8,128)(2,1)}, bf16[300,600]{1,0:T(8,128)(2,1)S(1)}, u32[]{:S(2)}, u32[]{:S(2)}) %collective-permute-start.7) | collective-permute-done | bytes 360032 | tf_op jit(solution)/shard_map/ppermute | solution.py:52
  23.6 0.7 copy-done.3
  24.3 3.3 %collective-permute-start.10 = (bf16[300,600]{1,0:T(8,128)(2,1)S(1)}, bf16[300,600]{1,0:T(8,128)(2,1)S(1)}, u32[]{:S(2)}, u32[]{:S(2)}) collective-permute-start(bf16[300,600]{1,0:T(8,128)(2,1)S(1)} %collective-permute-done.9.refs_1_), channel_id=1, source_target_pairs={{1,0},{2,1},{3,2},{0,3},{5,4},{6,5},{7,6},{4,7},{9,8},{10,9},{11,1... | collective-permute-start | bytes 1080008 | tf_op jit(solution)/shard_map/ppermute | solution.py:52
  27.6 0.8 copy-done.5
  28.5 1.9 %collective-permute-start.16 = (bf16[400,600]{1,0:T(8,128)(2,1)}, bf16[400,600]{1,0:T(8,128)(2,1)S(1)}, u32[]{:S(2)}, u32[]{:S(2)}) collective-permute-start(bf16[400,600]{1,0:T(8,128)(2,1)} %bitcast.13), channel_id=1, source_target_pairs={{8,0},{9,1},{10,2},{11,3},{12,4},{13,5},{14,6},{15,7},{0,8},{1,9},... | collective-permute-start | bytes 1440008 | tf_op jit(solution)/shard_map/ppermute | solution.py:52
  30.5 5.1 %collective-permute-done.10.refs_2_ = bf16[300,600]{1,0:T(8,128)(2,1)S(1)} collective-permute-done((bf16[300,600]{1,0:T(8,128)(2,1)S(1)}, bf16[300,600]{1,0:T(8,128)(2,1)S(1)}, u32[]{:S(2)}, u32[]{:S(2)}) %collective-permute-start.10) | collective-permute-done | bytes 360032 | tf_op jit(solution)/shard_map/ppermute | solution.py:52
  35.5 0.8 copy-done.7
  36.3 1.3 collective-permute-start.31
  37.6 2.1 %copy-done.1 = bf16[2,400,2400]{2,1,0:T(8,128)(2,1)S(1)} copy-done((bf16[2,400,2400]{2,1,0:T(8,128)(2,1)S(1)}, bf16[2,400,2400]{2,1,0:T(8,128)(2,1)}, u32[]{:S(2)}) %copy-start.1) | copy-done | bytes 3840024
  39.7 3.4 %shard_map.69.g_ref = bf16[8,800,300]{2,1,0:T(8,128)(2,1)S(1)} custom-call(bf16[800,2400]{1,0:T(8,128)(2,1)S(1)} %bitcast.18), custom_call_target="tpu_custom_call" | custom-call | tf_op jit(solution)/shard_map/pallas_call | solution.py:106
  43.3 0.6 shard_map.68
  43.9 2.8 %collective-permute-start.1 = (bf16[400,600]{1,0:T(8,128)(2,1)S(1)}, bf16[400,600]{1,0:T(8,128)(2,1)S(1)}, u32[]{:S(2)}, u32[]{:S(2)}) collective-permute-start(bf16[400,600]{1,0:T(8,128)(2,1)S(1)} %shard_map.68), channel_id=1, source_target_pairs={{32,0},{33,1},{34,2},{35,3},{36,4},{37,5},{38,6},{39,7},{40,8},{41... | collective-permute-start | bytes 1440008 | tf_op jit(solution)/shard_map/ppermute | solution.py:52
  46.7 0.9 collective-permute-start.18
  47.6 3.4 %shard_map.70.refs_4_ = f32[800,600]{1,0:T(8,128)S(1)} custom-call(s32[2]{0:T(128)S(1)} %pad_add_fusion.ids_ref, bf16[8,800,300]{2,1,0:T(8,128)(2,1)S(1)} %shard_map.69.g_ref, bf16[300,600]{1,0:T(8,128)(2,1)S(1)} %copy-done.2, bf16[300,600]{1,0:T(8,128)(2,1)S(1)} %collective-permute-done.9.refs_1_, bf16[300,600]{1,0:T(8,128)(2,1)} %collective-permute-done.5.refs_2_), custom_call_target="tpu_custom_call" | custom-call | flops 864000000 | bytes 1440000 | tf_op jit(solution)/shard_map/pallas_call | solution.py:166
  51.0 4.0 %shard_map.71.refs_1_ = f32[800,600]{1,0:T(8,128)S(1)} custom-call(s32[2]{0:T(128)S(1)} %pad_add_fusion.ids_ref, bf16[8,800,300]{2,1,0:T(8,128)(2,1)S(1)} %shard_map.69.g_ref, bf16[300,600]{1,0:T(8,128)(2,1)S(1)} %copy-done.4, bf16[300,600]{1,0:T(8,128)(2,1)S(1)} %copy-done.6, bf16[300,600]{1,0:T(8,128)(2,1)S(1)} %copy-done.8, ...), custom_call_target="tpu_custom_call" | custom-call | flops 1152000000 | bytes 1920000 | tf_op jit(solution)/shard_map/pallas_call | solution.py:166
  55.1 2.2 %shard_map.72 = (bf16[408,600]{1,0:T(8,128)(2,1)S(1)}, bf16[408,600]{1,0:T(8,128)(2,1)S(1)}, bf16[408,600]{1,0:T(8,128)(2,1)S(1)}, bf16[408,600]{1,0:T(8,128)(2,...) custom-call(s32[2]{0:T(128)S(1)} %pad_add_fusion.ids_ref, ...), custom_call_target="tpu_custom_call" | custom-call | flops 288000000 | bytes 480000 | tf_op jit(solution)/shard_map/pallas_call | solution.py:218
  57.4 0.7 collective-permute-start.36
  58.1 2.1 %collective-permute-start.32 = (bf16[408,600]{1,0:T(8,128)(2,1)S(1)}, bf16[408,600]{1,0:T(8,128)(2,1)S(1)}, u32[]{:S(2)}, u32[]{:S(2)}) collective-permute-start(bf16[408,600]{1,0:T(8,128)(2,1)S(1)} %get-tuple-element.32.refs_4_), channel_id=1, source_target_pairs={{16,0},{17,1},{18,2},{19,3},{20,4},{21,5},{22,6},{23,7},{24,8},{25... | collective-permute-start | bytes 1468808 | tf_op jit(solution)/shard_map/ppermute | solution.py:52
  60.2 1.3 collective-permute-start.28
  61.5 6.1 %collective-permute-done.18.refs_0_ = bf16[400,600]{1,0:T(8,128)(2,1)S(1)} collective-permute-done((bf16[400,600]{1,0:T(8,128)(2,1)S(1)}, bf16[400,600]{1,0:T(8,128)(2,1)S(1)}, u32[]{:S(2)}, u32[]{:S(2)}) %collective-permute-start.18) | collective-permute-done | bytes 480032 | tf_op jit(solution)/shard_map/ppermute | solution.py:52
  67.6 3.3 %collective-permute-start.12 = (bf16[408,600]{1,0:T(8,128)(2,1)S(1)}, bf16[408,600]{1,0:T(8,128)(2,1)S(1)}, u32[]{:S(2)}, u32[]{:S(2)}) collective-permute-start(bf16[408,600]{1,0:T(8,128)(2,1)S(1)} %get-tuple-element.29), channel_id=1, source_target_pairs={{64,0},{65,1},{66,2},{67,3},{68,4},{69,5},{70,6},{71,7},{72,8},{73... | collective-permute-start | bytes 1468808 | tf_op jit(solution)/shard_map/ppermute | solution.py:52
  70.9 1.7 collective-permute-done.36.refs_2_
  72.6 7.2 %collective-permute-start.2 = (bf16[400,600]{1,0:T(8,128)(2,1)S(1)}, bf16[400,600]{1,0:T(8,128)(2,1)S(1)}, u32[]{:S(2)}, u32[]{:S(2)}) collective-permute-start(bf16[400,600]{1,0:T(8,128)(2,1)S(1)} %collective-permute-done.1.refs_0_.refs_1_), channel_id=1, source_target_pairs={{1,0},{0,1},{3,2},{2,3},{5,4},{4,5},{7,6},{6,7},{9,8},{8,9},{11,10... | collective-permute-start | bytes 1440008 | tf_op jit(solution)/shard_map/ppermute | solution.py:52
  79.8 0.7 collective-permute-start.4
  80.4 4.1 %collective-permute-done.28.refs_4_ = bf16[408,600]{1,0:T(8,128)(2,1)S(1)} collective-permute-done((bf16[408,600]{1,0:T(8,128)(2,1)S(1)}, bf16[408,600]{1,0:T(8,128)(2,1)S(1)}, u32[]{:S(2)}, u32[]{:S(2)}) %collective-permute-start.28) | collective-permute-done | bytes 489632 | tf_op jit(solution)/shard_map/ppermute | solution.py:52
  84.5 2.9 %collective-permute-start.25 = (bf16[400,600]{1,0:T(8,128)(2,1)S(1)}, bf16[400,600]{1,0:T(8,128)(2,1)S(1)}, u32[]{:S(2)}, u32[]{:S(2)}) collective-permute-start(bf16[400,600]{1,0:T(8,128)(2,1)S(1)} %collective-permute-done.18.refs_0_), channel_id=1, source_target_pairs={{8,0},{9,1},{10,2},{11,3},{12,4},{13,5},{14,6},{15,7},{0,8},{1,9},... | collective-permute-start | bytes 1440008 | tf_op jit(solution)/shard_map/ppermute | solution.py:52
  87.8 4.8 %collective-permute-done.13.two_ref = bf16[408,600]{1,0:T(8,128)(2,1)S(1)} collective-permute-done((bf16[408,600]{1,0:T(8,128)(2,1)S(1)}, bf16[408,600]{1,0:T(8,128)(2,1)S(1)}, u32[]{:S(2)}, u32[]{:S(2)}) %collective-permute-start.13) | collective-permute-done | bytes 489632 | tf_op jit(solution)/shard_map/ppermute | solution.py:52
  92.7 2.2 %collective-permute-start.37 = (bf16[408,600]{1,0:T(8,128)(2,1)S(1)}, bf16[408,600]{1,0:T(8,128)(2,1)S(1)}, u32[]{:S(2)}, u32[]{:S(2)}) collective-permute-start(bf16[408,600]{1,0:T(8,128)(2,1)S(1)} %collective-permute-done.36.refs_2_), channel_id=1, source_target_pairs={{8,0},{9,1},{10,2},{11,3},{12,4},{13,5},{14,6},{15,7},{0,8},{1,9},... | collective-permute-start | bytes 1468808 | tf_op jit(solution)/shard_map/ppermute | solution.py:52
  95.2 2.2 %collective-permute-start.29 = (bf16[408,600]{1,0:T(8,128)(2,1)S(1)}, bf16[408,600]{1,0:T(8,128)(2,1)S(1)}, u32[]{:S(2)}, u32[]{:S(2)}) collective-permute-start(bf16[408,600]{1,0:T(8,128)(2,1)S(1)} %collective-permute-done.28.refs_4_), channel_id=1, source_target_pairs={{8,0},{9,1},{10,2},{11,3},{12,4},{13,5},{14,6},{15,7},{0,8},{1,9},... | collective-permute-start | bytes 1468808 | tf_op jit(solution)/shard_map/ppermute | solution.py:52
  97.5 3.9 %collective-permute-done.19.refs_0_ = bf16[400,600]{1,0:T(8,128)(2,1)S(1)} collective-permute-done((bf16[400,600]{1,0:T(8,128)(2,1)S(1)}, bf16[400,600]{1,0:T(8,128)(2,1)S(1)}, u32[]{:S(2)}, u32[]{:S(2)}) %collective-permute-start.19) | collective-permute-done | bytes 480032 | tf_op jit(solution)/shard_map/ppermute | solution.py:52
  101.4 2.2 %collective-permute-start.21 = (bf16[408,600]{1,0:T(8,128)(2,1)S(1)}, bf16[408,600]{1,0:T(8,128)(2,1)S(1)}, u32[]{:S(2)}, u32[]{:S(2)}) collective-permute-start(bf16[408,600]{1,0:T(8,128)(2,1)S(1)} %collective-permute-done.13.two_ref), channel_id=1, source_target_pairs={{16,0},{49,1},{18,2},{51,3},{20,4},{53,5},{22,6},{55,7},{56,8},{25... | collective-permute-start | bytes 1468808 | tf_op jit(solution)/shard_map/ppermute | solution.py:52
  103.6 0.6 shard_map.73
  104.6 4.0 %collective-permute-start.3 = (bf16[400,600]{1,0:T(8,128)(2,1)S(1)}, bf16[400,600]{1,0:T(8,128)(2,1)S(1)}, u32[]{:S(2)}, u32[]{:S(2)}) collective-permute-start(bf16[400,600]{1,0:T(8,128)(2,1)S(1)} %collective-permute-done.2.refs_1_.refs_0_), channel_id=1, source_target_pairs={{8,0},{9,1},{10,2},{11,3},{12,4},{13,5},{14,6},{15,7},{0,8},{1,9},... | collective-permute-start | bytes 1440008 | tf_op jit(solution)/shard_map/ppermute | solution.py:52
  108.7 9.8 %shard_map.67.k_ref = bf16[80,600,600]{2,1,0:T(8,128)(2,1)} custom-call(bf16[600,9600]{1,0:T(8,128)(2,1)S(1)} %bitcast.9), custom_call_target="tpu_custom_call" | custom-call | tf_op jit(solution)/shard_map/pallas_call | solution.py:106
  118.6 0.6 shard_map.75.refs_2_
  119.2 0.5 collective-permute-start.23
  119.7 2.2 %collective-permute-done.21.refs_2_ = bf16[408,600]{1,0:T(8,128)(2,1)S(1)} collective-permute-done((bf16[408,600]{1,0:T(8,128)(2,1)S(1)}, bf16[408,600]{1,0:T(8,128)(2,1)S(1)}, u32[]{:S(2)}, u32[]{:S(2)}) %collective-permute-start.21) | collective-permute-done | bytes 489632 | tf_op jit(solution)/shard_map/ppermute | solution.py:52
  121.9 6.1 %shard_map.74 = (f32[2,8,600]{2,1,0:T(8,128)S(1)}, f32[8,600]{1,0:T(8,128)S(1)}, bf16[3,600,400]{2,1,0:T(8,128)(2,1)S(1)}) custom-call(s32[2]{0:T(128)S(1)} %pad_add_fusion.ids_ref, bf16[80,600,600]{2,1,0:T(8,128)(2,1)} %shard_map.67.k_ref, bf16[400,600]{1,0:T(8,128)(2,1)S(1)} %bitcast.16, bf16[400,600]{1,0:T(8,128)(2,1)S(1)} %bitcast.17, ...), custom_call_target="tpu_custom_call" | custom-call | flops 1728000000 | bytes 5760000 | tf_op jit(solution)/shard_map/pallas_call | solution.py:332
  128.0 0.6 collective-permute-start.20
  128.7 3.7 %shard_map.76 = (f32[2,8,600]{2,1,0:T(8,128)S(1)}, f32[8,600]{1,0:T(8,128)S(1)}) custom-call(s32[2]{0:T(128)S(1)} %pad_add_fusion.ids_ref, bf16[80,600,600]{2,1,0:T(8,128)(2,1)} %shard_map.67.k_ref, bf16[400,600]{1,0:T(8,128)(2,1)S(1)} %collective-permute-done.34.refs_0_, ...), custom_call_target="tpu_custom_call", output_to_operand_aliasing={{0}: (7, {}), {1}: (8, {})} | custom-call | flops 1152000000 | bytes 3840000 | tf_op jit(solution)/shard_map/pallas_call | solution.py:332
  132.4 0.7 collective-permute-start.15
  133.1 3.7 %shard_map.77 = (f32[2,8,600]{2,1,0:T(8,128)S(1)}, f32[8,600]{1,0:T(8,128)S(1)}) custom-call(s32[2]{0:T(128)S(1)} %pad_add_fusion.ids_ref, bf16[80,600,600]{2,1,0:T(8,128)(2,1)} %shard_map.67.k_ref, bf16[400,600]{1,0:T(8,128)(2,1)S(1)} %collective-permute-done.30.refs_0_, ...), custom_call_target="tpu_custom_call", output_to_operand_aliasing={{0}: (7, {}), {1}: (8, {})} | custom-call | flops 1152000000 | bytes 3840000 | tf_op jit(solution)/shard_map/pallas_call | solution.py:332
  136.9 3.7 %shard_map.78 = (f32[2,8,600]{2,1,0:T(8,128)S(1)}, f32[8,600]{1,0:T(8,128)S(1)}) custom-call(s32[2]{0:T(128)S(1)} %pad_add_fusion.ids_ref, bf16[80,600,600]{2,1,0:T(8,128)(2,1)} %shard_map.67.k_ref, bf16[400,600]{1,0:T(8,128)(2,1)S(1)} %collective-permute-done.1.refs_0_.refs_1_, ...), custom_call_target="tpu_custom_call", output_to_operand_aliasing={{0}: (9, {}), {1}: (10, {})} | custom-call | flops 1152000000 | bytes 3840000 | tf_op jit(solution)/shard_map/pallas_call | solution.py:332
  140.6 3.7 %shard_map.79 = (f32[2,8,600]{2,1,0:T(8,128)S(1)}, f32[8,600]{1,0:T(8,128)S(1)}) custom-call(s32[2]{0:T(128)S(1)} %pad_add_fusion.ids_ref, bf16[80,600,600]{2,1,0:T(8,128)(2,1)} %shard_map.67.k_ref, bf16[400,600]{1,0:T(8,128)(2,1)S(1)} %collective-permute-done.18.refs_0_, ...), custom_call_target="tpu_custom_call", output_to_operand_aliasing={{0}: (7, {}), {1}: (8, {})} | custom-call | flops 1152000000 | bytes 3840000 | tf_op jit(solution)/shard_map/pallas_call | solution.py:332
  144.3 3.7 %shard_map.80 = (f32[2,8,600]{2,1,0:T(8,128)S(1)}, f32[8,600]{1,0:T(8,128)S(1)}) custom-call(s32[2]{0:T(128)S(1)} %pad_add_fusion.ids_ref, bf16[80,600,600]{2,1,0:T(8,128)(2,1)} %shard_map.67.k_ref, bf16[400,600]{1,0:T(8,128)(2,1)S(1)} %collective-permute-done.two_ref.refs_0_, ...), custom_call_target="tpu_custom_call", output_to_operand_aliasing={{0}: (7, {}), {1}: (8, {})} | custom-call | flops 1152000000 | bytes 3840000 | tf_op jit(solution)/shard_map/pallas_call | solution.py:332
  148.0 3.7 %shard_map.81 = (f32[2,8,600]{2,1,0:T(8,128)S(1)}, f32[8,600]{1,0:T(8,128)S(1)}) custom-call(s32[2]{0:T(128)S(1)} %pad_add_fusion.ids_ref, bf16[80,600,600]{2,1,0:T(8,128)(2,1)} %shard_map.67.k_ref, bf16[400,600]{1,0:T(8,128)(2,1)S(1)} %collective-permute-done.19.refs_0_, ...), custom_call_target="tpu_custom_call", output_to_operand_aliasing={{0}: (7, {}), {1}: (8, {})} | custom-call | flops 1152000000 | bytes 3840000 | tf_op jit(solution)/shard_map/pallas_call | solution.py:332
  151.7 3.1 %shard_map.82 = (f32[2,8,600]{2,1,0:T(8,128)S(1)}, f32[8,600]{1,0:T(8,128)S(1)}) custom-call(s32[2]{0:T(128)S(1)} %pad_add_fusion.ids_ref, bf16[80,600,600]{2,1,0:T(8,128)(2,1)} %shard_map.67.k_ref, bf16[400,600]{1,0:T(8,128)(2,1)S(1)} %collective-permute-done.2.refs_1_.refs_0_, ...), custom_call_target="tpu_custom_call", output_to_operand_aliasing={{0}: (6, {}), {1}: (7, {})} | custom-call | flops 576000000 | bytes 1920000 | tf_op jit(solution)/shard_map/pallas_call | solution.py:332
  154.8 3.7 %shard_map.83 = (f32[2,8,600]{2,1,0:T(8,128)S(1)}, f32[8,600]{1,0:T(8,128)S(1)}, f32[2,600]{1,0:T(2,128)}, f32[8,128]{1,0:T(8,128)S(1)}) custom-call(s32[2]{0:T(128)S(1)} %pad_add_fusion.ids_ref, bf16[80,600,600]{2,1,0:T(8,128)(2,1)} %shard_map.67.k_ref, ...), custom_call_target="tpu_custom_call", output_to_operand_aliasing={{0}: (6, {}), {1}: (7, {})} | custom-call | flops 576000000 | bytes 1920000 | tf_op jit(solution)/shard_map/pallas_call | solution.py:332
  158.7 1.1 collective-permute-done.38
  159.8 3.1 %collective-permute-start.39 = (f32[8,128]{1,0:T(8,128)S(1)}, f32[8,128]{1,0:T(8,128)S(1)}, u32[]{:S(2)}, u32[]{:S(2)}) collective-permute-start(f32[8,128]{1,0:T(8,128)S(1)} %add.15), channel_id=1, source_target_pairs={{32,0},{33,1},{34,2},{35,3},{36,4},{37,5},{38,6},{39,7},{40,8},{41... | collective-permute-start | bytes 12296 | tf_op jit(solution)/shard_map/ppermute | solution.py:52
  162.9 2.8 %collective-permute-start.40 = (f32[8,128]{1,0:T(8,128)S(1)}, f32[8,128]{1,0:T(8,128)S(1)}, u32[]{:S(2)}, u32[]{:S(2)}) collective-permute-start(f32[8,128]{1,0:T(8,128)S(1)} %add.15), channel_id=1, source_target_pairs={{16,0},{17,1},{18,2},{19,3},{20,4},{21,5},{22,6},{23,7},{24,8},{25... | collective-permute-start | bytes 12296 | tf_op jit(solution)/shard_map/ppermute | solution.py:52
  165.7 0.7 collective-permute-done.40
  166.4 2.9 %collective-permute-done.41 = f32[8,128]{1,0:T(8,128)S(1)} collective-permute-done((f32[8,128]{1,0:T(8,128)S(1)}, f32[8,128]{1,0:T(8,128)S(1)}, u32[]{:S(2)}, u32[]{:S(2)}) %collective-permute-start.41) | collective-permute-done | bytes 4128 | tf_op jit(solution)/shard_map/ppermute | solution.py:52
  169.4 3.3 %collective-permute-start.42 = (f32[8,128]{1,0:T(8,128)S(1)}, f32[8,128]{1,0:T(8,128)S(1)}, u32[]{:S(2)}, u32[]{:S(2)}) collective-permute-start(f32[8,128]{1,0:T(8,128)S(1)} %add_add_fusion), channel_id=1, source_target_pairs={{64,0},{65,1},{66,2},{67,3},{68,4},{69,5},{70,6},{71,7},{72,8},{73... | collective-permute-start | bytes 12296 | tf_op jit(solution)/shard_map/ppermute | solution.py:52
  172.7 1.0 collective-permute-done.42
  173.7 0.6 slice_bitcast_fusion
  (69 shorter events, 1.9 us)
Async XLA Ops:
  0.6 11.6 %collective-permute-start.9 = (bf16[300,600]{1,0:T(8,128)(2,1)}, bf16[300,600]{1,0:T(8,128)(2,1)S(1)}, u32[]{:S(2)}, u32[]{:S(2)}) collective-permute-start(bf16[300,600]{1,0:T(8,128)(2,1)} %refs_0_.1), channel_id=1, source_target_pairs={{4,0},{5,1},{6,2},{7,3},{0,4},{1,5},{2,6},{3,7},{12,8},{13,9},{14,... | collective-permute-start | bytes 1080008 | tf_op jit(solution)/shard_map/ppermute | solution.py:52
  3.2 12.2 %collective-permute-start.5 = (bf16[300,600]{1,0:T(8,128)(2,1)}, bf16[300,600]{1,0:T(8,128)(2,1)}, u32[]{:S(2)}, u32[]{:S(2)}) collective-permute-start(bf16[300,600]{1,0:T(8,128)(2,1)} %refs_0_.1), channel_id=1, source_target_pairs={{2,0},{3,1},{0,2},{1,3},{6,4},{7,5},{4,6},{5,7},{10,8},{11,9},{8,1... | collective-permute-start | bytes 1080008 | tf_op jit(solution)/shard_map/ppermute | solution.py:52
  6.1 17.5 %collective-permute-start.7 = (bf16[300,600]{1,0:T(8,128)(2,1)}, bf16[300,600]{1,0:T(8,128)(2,1)S(1)}, u32[]{:S(2)}, u32[]{:S(2)}) collective-permute-start(bf16[300,600]{1,0:T(8,128)(2,1)} %refs_0_.1), channel_id=1, source_target_pairs={{1,0},{2,1},{3,2},{0,3},{5,4},{6,5},{7,6},{4,7},{9,8},{10,9},{11,1... | collective-permute-start | bytes 1080008 | tf_op jit(solution)/shard_map/ppermute | solution.py:52
  6.9 21.6 %collective-permute-start.34 = (bf16[400,600]{1,0:T(8,128)(2,1)}, bf16[400,600]{1,0:T(8,128)(2,1)S(1)}, u32[]{:S(2)}, u32[]{:S(2)}) collective-permute-start(bf16[400,600]{1,0:T(8,128)(2,1)} %bitcast.10), channel_id=1, source_target_pairs={{48,0},{49,1},{50,2},{51,3},{52,4},{53,5},{54,6},{55,7},{56,8},{57... | collective-permute-start | bytes 1440008 | tf_op jit(solution)/shard_map/ppermute | solution.py:52
  8.1 20.4 %collective-permute-start.30 = (bf16[400,600]{1,0:T(8,128)(2,1)}, bf16[400,600]{1,0:T(8,128)(2,1)S(1)}, u32[]{:S(2)}, u32[]{:S(2)}) collective-permute-start(bf16[400,600]{1,0:T(8,128)(2,1)} %bitcast.11), channel_id=1, source_target_pairs={{16,0},{17,1},{18,2},{19,3},{20,4},{21,5},{22,6},{23,7},{24,8},{25... | collective-permute-start | bytes 1440008 | tf_op jit(solution)/shard_map/ppermute | solution.py:52
  12.2 18.2 %collective-permute-start = (bf16[400,600]{1,0:T(8,128)(2,1)}, bf16[400,600]{1,0:T(8,128)(2,1)S(1)}, u32[]{:S(2)}, u32[]{:S(2)}) collective-permute-start(bf16[400,600]{1,0:T(8,128)(2,1)} %bitcast.12), channel_id=1, source_target_pairs={{64,0},{65,1},{66,2},{67,3},{68,4},{69,5},{70,6},{71,7},{72,8},{73... | collective-permute-start | bytes 1440008 | tf_op jit(solution)/shard_map/ppermute | solution.py:52
  15.4 12.3 %collective-permute-start.8 = (bf16[300,600]{1,0:T(8,128)(2,1)}, bf16[300,600]{1,0:T(8,128)(2,1)S(1)}, u32[]{:S(2)}, u32[]{:S(2)}) collective-permute-start(bf16[300,600]{1,0:T(8,128)(2,1)} %refs_0_.1), channel_id=1, source_target_pairs={{3,0},{0,1},{1,2},{2,3},{7,4},{4,5},{5,6},{6,7},{11,8},{8,9},{9,10... | collective-permute-start | bytes 1080008 | tf_op jit(solution)/shard_map/ppermute | solution.py:52
  23.6 0.7 copy-start.3
  24.3 11.2 %collective-permute-start.10 = (bf16[300,600]{1,0:T(8,128)(2,1)S(1)}, bf16[300,600]{1,0:T(8,128)(2,1)S(1)}, u32[]{:S(2)}, u32[]{:S(2)}) collective-permute-start(bf16[300,600]{1,0:T(8,128)(2,1)S(1)} %collective-permute-done.9.refs_1_), channel_id=1, source_target_pairs={{1,0},{2,1},{3,2},{0,3},{5,4},{6,5},{7,6},{4,7},{9,8},{10,9},{11,1... | collective-permute-start | bytes 1080008 | tf_op jit(solution)/shard_map/ppermute | solution.py:52
  27.6 0.8 copy-start.5
  28.4 15.5 %collective-permute-start.11 = (bf16[300,600]{1,0:T(8,128)(2,1)S(1)}, bf16[300,600]{1,0:T(8,128)(2,1)}, u32[]{:S(2)}, u32[]{:S(2)}) collective-permute-start(bf16[300,600]{1,0:T(8,128)(2,1)S(1)} %collective-permute-done.9.refs_1_), channel_id=1, source_target_pairs={{3,0},{0,1},{1,2},{2,3},{7,4},{4,5},{5,6},{6,7},{11,8},{8,9},{9,10... | collective-permute-start | bytes 1080008 | tf_op jit(solution)/shard_map/ppermute | solution.py:52
  28.4 18.3 %collective-permute-start.6 = (bf16[300,600]{1,0:T(8,128)(2,1)}, bf16[300,600]{1,0:T(8,128)(2,1)}, u32[]{:S(2)}, u32[]{:S(2)}) collective-permute-start(bf16[300,600]{1,0:T(8,128)(2,1)} %collective-permute-done.5.refs_2_), channel_id=1, source_target_pairs={{4,0},{5,1},{6,2},{7,3},{0,4},{1,5},{2,6},{3,7},{12,8},{13,9},{14,... | collective-permute-start | bytes 1080008 | tf_op jit(solution)/shard_map/ppermute | solution.py:52
  28.5 28.8 %collective-permute-start.16 = (bf16[400,600]{1,0:T(8,128)(2,1)}, bf16[400,600]{1,0:T(8,128)(2,1)S(1)}, u32[]{:S(2)}, u32[]{:S(2)}) collective-permute-start(bf16[400,600]{1,0:T(8,128)(2,1)} %bitcast.13), channel_id=1, source_target_pairs={{8,0},{9,1},{10,2},{11,3},{12,4},{13,5},{14,6},{15,7},{0,8},{1,9},... | collective-permute-start | bytes 1440008 | tf_op jit(solution)/shard_map/ppermute | solution.py:52
  30.4 27.0 %collective-permute-start.35 = (bf16[400,600]{1,0:T(8,128)(2,1)S(1)}, bf16[400,600]{1,0:T(8,128)(2,1)S(1)}, u32[]{:S(2)}, u32[]{:S(2)}) collective-permute-start(bf16[400,600]{1,0:T(8,128)(2,1)S(1)} %collective-permute-done.34.refs_0_), channel_id=1, source_target_pairs={{8,0},{9,1},{10,2},{11,3},{12,4},{13,5},{14,6},{15,7},{0,8},{1,9},... | collective-permute-start | bytes 1440008 | tf_op jit(solution)/shard_map/ppermute | solution.py:52
  35.5 0.8 copy-start.7
  36.3 21.8 %collective-permute-start.31 = (bf16[400,600]{1,0:T(8,128)(2,1)S(1)}, bf16[400,600]{1,0:T(8,128)(2,1)S(1)}, u32[]{:S(2)}, u32[]{:S(2)}) collective-permute-start(bf16[400,600]{1,0:T(8,128)(2,1)S(1)} %collective-permute-done.30.refs_0_), channel_id=1, source_target_pairs={{8,0},{9,1},{10,2},{11,3},{12,4},{13,5},{14,6},{15,7},{0,8},{1,9},... | collective-permute-start | bytes 1440008 | tf_op jit(solution)/shard_map/ppermute | solution.py:52
  37.6 2.1 %copy-start.1 = (bf16[2,400,2400]{2,1,0:T(8,128)(2,1)S(1)}, bf16[2,400,2400]{2,1,0:T(8,128)(2,1)}, u32[]{:S(2)}) copy-start(bf16[2,400,2400]{2,1,0:T(8,128)(2,1)} %param.4) | copy-start | bytes 11520004
  39.7 3.5 %copy-start = (bf16[600,400]{0,1:T(8,128)(2,1)S(1)}, bf16[600,400]{0,1:T(8,128)(2,1)}, u32[]{:S(2)}) copy-start(bf16[600,400]{0,1:T(8,128)(2,1)} %param.6) | copy-start | bytes 1440004
  39.7 7.8 %copy-start.2 = (bf16[300,600]{1,0:T(8,128)(2,1)S(1)}, bf16[300,600]{1,0:T(8,128)(2,1)}, u32[]{:S(2)}) copy-start(bf16[300,600]{1,0:T(8,128)(2,1)} %refs_0_.1) | copy-start | bytes 1080004
  43.8 7.1 %copy-start.4 = (bf16[300,600]{1,0:T(8,128)(2,1)S(1)}, bf16[300,600]{1,0:T(8,128)(2,1)}, u32[]{:S(2)}) copy-start(bf16[300,600]{1,0:T(8,128)(2,1)} %copy-done.3) | copy-start | bytes 1080004
  43.9 7.1 %copy-start.6 = (bf16[300,600]{1,0:T(8,128)(2,1)S(1)}, bf16[300,600]{1,0:T(8,128)(2,1)}, u32[]{:S(2)}) copy-start(bf16[300,600]{1,0:T(8,128)(2,1)} %copy-done.5) | copy-start | bytes 1080004
  43.9 7.1 %copy-start.8 = (bf16[300,600]{1,0:T(8,128)(2,1)S(1)}, bf16[300,600]{1,0:T(8,128)(2,1)}, u32[]{:S(2)}) copy-start(bf16[300,600]{1,0:T(8,128)(2,1)} %copy-done.7) | copy-start | bytes 1080004
  43.9 16.3 %collective-permute-start.1 = (bf16[400,600]{1,0:T(8,128)(2,1)S(1)}, bf16[400,600]{1,0:T(8,128)(2,1)S(1)}, u32[]{:S(2)}, u32[]{:S(2)}) collective-permute-start(bf16[400,600]{1,0:T(8,128)(2,1)S(1)} %shard_map.68), channel_id=1, source_target_pairs={{32,0},{33,1},{34,2},{35,3},{36,4},{37,5},{38,6},{39,7},{40,8},{41... | collective-permute-start | bytes 1440008 | tf_op jit(solution)/shard_map/ppermute | solution.py:52
  46.7 20.9 %collective-permute-start.18 = (bf16[400,600]{1,0:T(8,128)(2,1)S(1)}, bf16[400,600]{1,0:T(8,128)(2,1)S(1)}, u32[]{:S(2)}, u32[]{:S(2)}) collective-permute-start(bf16[400,600]{1,0:T(8,128)(2,1)S(1)} %collective-permute-done.two_ref.refs_0_), channel_id=1, source_target_pairs={{48,0},{17,1},{50,2},{19,3},{52,4},{21,5},{54,6},{23,7},{24,8},{57... | collective-permute-start | bytes 1440008 | tf_op jit(solution)/shard_map/ppermute | solution.py:52
  47.6 61.1 %slice-start = ((s8[11520000]{0:T(1024)(128)(4,1)}), s8[4194304]{0:T(1024)(128)(4,1)S(1)}, s32[]{:S(2)}) async-start(s8[11520000]{0:T(1024)(128)(4,1)} %bitcast.8), calls=%async_computation | async-start | bytes 8388608
  51.0 57.7 %slice-start.1 = ((s8[11520000]{0:T(1024)(128)(4,1)}), s8[4194304]{0:T(1024)(128)(4,1)S(1)}, s32[]{:S(2)}) async-start(s8[11520000]{0:T(1024)(128)(4,1)} %bitcast.8), calls=%async_computation.1 | async-start | bytes 8388608
  55.0 53.7 %slice-start.2 = ((s8[11520000]{0:T(1024)(128)(4,1)}), s8[3131392]{0:T(1024)(128)(4,1)S(1)}, s32[]{:S(2)}) async-start(s8[11520000]{0:T(1024)(128)(4,1)} %bitcast.8), calls=%async_computation.2 | async-start | bytes 6262784
  57.3 13.6 %collective-permute-start.17 = (bf16[408,600]{1,0:T(8,128)(2,1)S(1)}, bf16[408,600]{1,0:T(8,128)(2,1)S(1)}, u32[]{:S(2)}, u32[]{:S(2)}) collective-permute-start(bf16[408,600]{1,0:T(8,128)(2,1)S(1)} %get-tuple-element.33), channel_id=1, source_target_pairs={{8,0},{9,1},{10,2},{11,3},{12,4},{13,5},{14,6},{15,7},{0,8},{1,9},... | collective-permute-start | bytes 1468808 | tf_op jit(solution)/shard_map/ppermute | solution.py:52
  57.4 15.2 %collective-permute-start.36 = (bf16[408,600]{1,0:T(8,128)(2,1)S(1)}, bf16[408,600]{1,0:T(8,128)(2,1)S(1)}, u32[]{:S(2)}, u32[]{:S(2)}) collective-permute-start(bf16[408,600]{1,0:T(8,128)(2,1)S(1)} %get-tuple-element.31.refs_3_), channel_id=1, source_target_pairs={{48,0},{49,1},{50,2},{51,3},{52,4},{53,5},{54,6},{55,7},{56,8},{57... | collective-permute-start | bytes 1468808 | tf_op jit(solution)/shard_map/ppermute | solution.py:52
  58.1 21.7 %collective-permute-start.32 = (bf16[408,600]{1,0:T(8,128)(2,1)S(1)}, bf16[408,600]{1,0:T(8,128)(2,1)S(1)}, u32[]{:S(2)}, u32[]{:S(2)}) collective-permute-start(bf16[408,600]{1,0:T(8,128)(2,1)S(1)} %get-tuple-element.32.refs_4_), channel_id=1, source_target_pairs={{16,0},{17,1},{18,2},{19,3},{20,4},{21,5},{22,6},{23,7},{24,8},{25... | collective-permute-start | bytes 1468808 | tf_op jit(solution)/shard_map/ppermute | solution.py:52
  60.2 24.4 %collective-permute-start.28 = (bf16[408,600]{1,0:T(8,128)(2,1)S(1)}, bf16[408,600]{1,0:T(8,128)(2,1)S(1)}, u32[]{:S(2)}, u32[]{:S(2)}) collective-permute-start(bf16[408,600]{1,0:T(8,128)(2,1)S(1)} %get-tuple-element.35), channel_id=1, source_target_pairs={{32,0},{33,1},{34,2},{35,3},{36,4},{37,5},{38,6},{39,7},{40,8},{41... | collective-permute-start | bytes 1468808 | tf_op jit(solution)/shard_map/ppermute | solution.py:52
  67.6 19.9 %collective-permute-start.12 = (bf16[408,600]{1,0:T(8,128)(2,1)S(1)}, bf16[408,600]{1,0:T(8,128)(2,1)S(1)}, u32[]{:S(2)}, u32[]{:S(2)}) collective-permute-start(bf16[408,600]{1,0:T(8,128)(2,1)S(1)} %get-tuple-element.29), channel_id=1, source_target_pairs={{64,0},{65,1},{66,2},{67,3},{68,4},{69,5},{70,6},{71,7},{72,8},{73... | collective-permute-start | bytes 1468808 | tf_op jit(solution)/shard_map/ppermute | solution.py:52
  70.9 21.8 %collective-permute-start.13 = (bf16[408,600]{1,0:T(8,128)(2,1)S(1)}, bf16[408,600]{1,0:T(8,128)(2,1)S(1)}, u32[]{:S(2)}, u32[]{:S(2)}) collective-permute-start(bf16[408,600]{1,0:T(8,128)(2,1)S(1)} %get-tuple-element.30), channel_id=1, source_target_pairs={{64,0},{65,1},{66,2},{67,3},{68,4},{69,5},{70,6},{71,7},{72,8},{73... | collective-permute-start | bytes 1468808 | tf_op jit(solution)/shard_map/ppermute | solution.py:52
  72.6 22.3 %collective-permute-start.2 = (bf16[400,600]{1,0:T(8,128)(2,1)S(1)}, bf16[400,600]{1,0:T(8,128)(2,1)S(1)}, u32[]{:S(2)}, u32[]{:S(2)}) collective-permute-start(bf16[400,600]{1,0:T(8,128)(2,1)S(1)} %collective-permute-done.1.refs_0_.refs_1_), channel_id=1, source_target_pairs={{1,0},{0,1},{3,2},{2,3},{5,4},{4,5},{7,6},{6,7},{9,8},{8,9},{11,10... | collective-permute-start | bytes 1440008 | tf_op jit(solution)/shard_map/ppermute | solution.py:52
  79.8 15.1 %collective-permute-start.4 = (bf16[400,600]{1,0:T(8,128)(2,1)S(1)}, bf16[400,600]{1,0:T(8,128)(2,1)S(1)}, u32[]{:S(2)}, u32[]{:S(2)}) collective-permute-start(bf16[400,600]{1,0:T(8,128)(2,1)S(1)} %collective-permute-done.1.refs_0_.refs_1_), channel_id=1, source_target_pairs={{8,0},{9,1},{10,2},{11,3},{12,4},{13,5},{14,6},{15,7},{0,8},{1,9},... | collective-permute-start | bytes 1440008 | tf_op jit(solution)/shard_map/ppermute | solution.py:52
  84.5 10.7 %collective-permute-start.25 = (bf16[400,600]{1,0:T(8,128)(2,1)S(1)}, bf16[400,600]{1,0:T(8,128)(2,1)S(1)}, u32[]{:S(2)}, u32[]{:S(2)}) collective-permute-start(bf16[400,600]{1,0:T(8,128)(2,1)S(1)} %collective-permute-done.18.refs_0_), channel_id=1, source_target_pairs={{8,0},{9,1},{10,2},{11,3},{12,4},{13,5},{14,6},{15,7},{0,8},{1,9},... | collective-permute-start | bytes 1440008 | tf_op jit(solution)/shard_map/ppermute | solution.py:52
  87.5 13.9 %collective-permute-start.19 = (bf16[400,600]{1,0:T(8,128)(2,1)S(1)}, bf16[400,600]{1,0:T(8,128)(2,1)S(1)}, u32[]{:S(2)}, u32[]{:S(2)}) collective-permute-start(bf16[400,600]{1,0:T(8,128)(2,1)S(1)} %collective-permute-done.18.refs_0_), channel_id=1, source_target_pairs={{1,0},{0,1},{3,2},{2,3},{5,4},{4,5},{7,6},{6,7},{9,8},{8,9},{11,10... | collective-permute-start | bytes 1440008 | tf_op jit(solution)/shard_map/ppermute | solution.py:52
  92.7 11.5 %collective-permute-start.37 = (bf16[408,600]{1,0:T(8,128)(2,1)S(1)}, bf16[408,600]{1,0:T(8,128)(2,1)S(1)}, u32[]{:S(2)}, u32[]{:S(2)}) collective-permute-start(bf16[408,600]{1,0:T(8,128)(2,1)S(1)} %collective-permute-done.36.refs_2_), channel_id=1, source_target_pairs={{8,0},{9,1},{10,2},{11,3},{12,4},{13,5},{14,6},{15,7},{0,8},{1,9},... | collective-permute-start | bytes 1468808 | tf_op jit(solution)/shard_map/ppermute | solution.py:52
  94.9 9.7 %collective-permute-start.33 = (bf16[408,600]{1,0:T(8,128)(2,1)S(1)}, bf16[408,600]{1,0:T(8,128)(2,1)S(1)}, u32[]{:S(2)}, u32[]{:S(2)}) collective-permute-start(bf16[408,600]{1,0:T(8,128)(2,1)S(1)} %collective-permute-done.32.refs_2_), channel_id=1, source_target_pairs={{8,0},{9,1},{10,2},{11,3},{12,4},{13,5},{14,6},{15,7},{0,8},{1,9},... | collective-permute-start | bytes 1468808 | tf_op jit(solution)/shard_map/ppermute | solution.py:52
  94.9 13.7 %collective-permute-start.26 = (bf16[408,600]{1,0:T(8,128)(2,1)S(1)}, bf16[408,600]{1,0:T(8,128)(2,1)S(1)}, u32[]{:S(2)}, u32[]{:S(2)}) collective-permute-start(bf16[408,600]{1,0:T(8,128)(2,1)S(1)} %collective-permute-done.12.one_ref), channel_id=1, source_target_pairs={{48,0},{17,1},{50,2},{19,3},{52,4},{21,5},{54,6},{23,7},{24,8},{57... | collective-permute-start | bytes 1468808 | tf_op jit(solution)/shard_map/ppermute | solution.py:52
  95.2 23.9 %collective-permute-start.29 = (bf16[408,600]{1,0:T(8,128)(2,1)S(1)}, bf16[408,600]{1,0:T(8,128)(2,1)S(1)}, u32[]{:S(2)}, u32[]{:S(2)}) collective-permute-start(bf16[408,600]{1,0:T(8,128)(2,1)S(1)} %collective-permute-done.28.refs_4_), channel_id=1, source_target_pairs={{8,0},{9,1},{10,2},{11,3},{12,4},{13,5},{14,6},{15,7},{0,8},{1,9},... | collective-permute-start | bytes 1468808 | tf_op jit(solution)/shard_map/ppermute | solution.py:52
  101.4 20.5 %collective-permute-start.21 = (bf16[408,600]{1,0:T(8,128)(2,1)S(1)}, bf16[408,600]{1,0:T(8,128)(2,1)S(1)}, u32[]{:S(2)}, u32[]{:S(2)}) collective-permute-start(bf16[408,600]{1,0:T(8,128)(2,1)S(1)} %collective-permute-done.13.two_ref), channel_id=1, source_target_pairs={{16,0},{49,1},{18,2},{51,3},{20,4},{53,5},{22,6},{55,7},{56,8},{25... | collective-permute-start | bytes 1468808 | tf_op jit(solution)/shard_map/ppermute | solution.py:52
  104.2 23.8 %collective-permute-start.14 = (bf16[408,600]{1,0:T(8,128)(2,1)S(1)}, bf16[408,600]{1,0:T(8,128)(2,1)S(1)}, u32[]{:S(2)}, u32[]{:S(2)}) collective-permute-start(bf16[408,600]{1,0:T(8,128)(2,1)S(1)} %shard_map.73), channel_id=1, source_target_pairs={{32,0},{33,1},{34,2},{35,3},{36,4},{37,5},{38,6},{39,7},{40,8},{41... | collective-permute-start | bytes 1468808 | tf_op jit(solution)/shard_map/ppermute | solution.py:52
  104.6 24.0 %collective-permute-start.3 = (bf16[400,600]{1,0:T(8,128)(2,1)S(1)}, bf16[400,600]{1,0:T(8,128)(2,1)S(1)}, u32[]{:S(2)}, u32[]{:S(2)}) collective-permute-start(bf16[400,600]{1,0:T(8,128)(2,1)S(1)} %collective-permute-done.2.refs_1_.refs_0_), channel_id=1, source_target_pairs={{8,0},{9,1},{10,2},{11,3},{12,4},{13,5},{14,6},{15,7},{0,8},{1,9},... | collective-permute-start | bytes 1440008 | tf_op jit(solution)/shard_map/ppermute | solution.py:52
  108.6 23.8 %collective-permute-start.27 = (bf16[408,600]{1,0:T(8,128)(2,1)S(1)}, bf16[408,600]{1,0:T(8,128)(2,1)S(1)}, u32[]{:S(2)}, u32[]{:S(2)}) collective-permute-start(bf16[408,600]{1,0:T(8,128)(2,1)S(1)} %collective-permute-done.26.refs_2_), channel_id=1, source_target_pairs={{8,0},{9,1},{10,2},{11,3},{12,4},{13,5},{14,6},{15,7},{0,8},{1,9},... | collective-permute-start | bytes 1468808 | tf_op jit(solution)/shard_map/ppermute | solution.py:52
  119.2 25.1 %collective-permute-start.23 = (bf16[400,600]{1,0:T(8,128)(2,1)S(1)}, bf16[400,600]{1,0:T(8,128)(2,1)S(1)}, u32[]{:S(2)}, u32[]{:S(2)}) collective-permute-start(bf16[400,600]{1,0:T(8,128)(2,1)S(1)} %collective-permute-done.two_ref.refs_0_), channel_id=1, source_target_pairs={{8,0},{9,1},{10,2},{11,3},{12,4},{13,5},{14,6},{15,7},{0,8},{1,9},... | collective-permute-start | bytes 1440008 | tf_op jit(solution)/shard_map/ppermute | solution.py:52
  121.9 22.4 %collective-permute-start.24 = (bf16[408,600]{1,0:T(8,128)(2,1)S(1)}, bf16[408,600]{1,0:T(8,128)(2,1)S(1)}, u32[]{:S(2)}, u32[]{:S(2)}) collective-permute-start(bf16[408,600]{1,0:T(8,128)(2,1)S(1)} %shard_map.75.refs_2_), channel_id=1, source_target_pairs={{8,0},{9,1},{10,2},{11,3},{12,4},{13,5},{14,6},{15,7},{0,8},{1,9},... | collective-permute-start | bytes 1468808 | tf_op jit(solution)/shard_map/ppermute | solution.py:52
  128.0 20.0 %collective-permute-start.20 = (bf16[400,600]{1,0:T(8,128)(2,1)S(1)}, bf16[400,600]{1,0:T(8,128)(2,1)S(1)}, u32[]{:S(2)}, u32[]{:S(2)}) collective-permute-start(bf16[400,600]{1,0:T(8,128)(2,1)S(1)} %collective-permute-done.19.refs_0_), channel_id=1, source_target_pairs={{8,0},{9,1},{10,2},{11,3},{12,4},{13,5},{14,6},{15,7},{0,8},{1,9},... | collective-permute-start | bytes 1440008 | tf_op jit(solution)/shard_map/ppermute | solution.py:52
  128.6 19.4 %collective-permute-start.22 = (bf16[408,600]{1,0:T(8,128)(2,1)S(1)}, bf16[408,600]{1,0:T(8,128)(2,1)S(1)}, u32[]{:S(2)}, u32[]{:S(2)}) collective-permute-start(bf16[408,600]{1,0:T(8,128)(2,1)S(1)} %collective-permute-done.21.refs_2_), channel_id=1, source_target_pairs={{8,0},{9,1},{10,2},{11,3},{12,4},{13,5},{14,6},{15,7},{0,8},{1,9},... | collective-permute-start | bytes 1468808 | tf_op jit(solution)/shard_map/ppermute | solution.py:52
  132.4 22.4 %collective-permute-start.15 = (bf16[408,600]{1,0:T(8,128)(2,1)S(1)}, bf16[408,600]{1,0:T(8,128)(2,1)S(1)}, u32[]{:S(2)}, u32[]{:S(2)}) collective-permute-start(bf16[408,600]{1,0:T(8,128)(2,1)S(1)} %collective-permute-done.14.refs_2_), channel_id=1, source_target_pairs={{8,0},{9,1},{10,2},{11,3},{12,4},{13,5},{14,6},{15,7},{0,8},{1,9},... | collective-permute-start | bytes 1468808 | tf_op jit(solution)/shard_map/ppermute | solution.py:52
  158.5 1.2 collective-permute-start.38
  159.8 5.9 %collective-permute-start.39 = (f32[8,128]{1,0:T(8,128)S(1)}, f32[8,128]{1,0:T(8,128)S(1)}, u32[]{:S(2)}, u32[]{:S(2)}) collective-permute-start(f32[8,128]{1,0:T(8,128)S(1)} %add.15), channel_id=1, source_target_pairs={{32,0},{33,1},{34,2},{35,3},{36,4},{37,5},{38,6},{39,7},{40,8},{41... | collective-permute-start | bytes 12296 | tf_op jit(solution)/shard_map/ppermute | solution.py:52
  162.9 3.6 %collective-permute-start.40 = (f32[8,128]{1,0:T(8,128)S(1)}, f32[8,128]{1,0:T(8,128)S(1)}, u32[]{:S(2)}, u32[]{:S(2)}) collective-permute-start(f32[8,128]{1,0:T(8,128)S(1)} %add.15), channel_id=1, source_target_pairs={{16,0},{17,1},{18,2},{19,3},{20,4},{21,5},{22,6},{23,7},{24,8},{25... | collective-permute-start | bytes 12296 | tf_op jit(solution)/shard_map/ppermute | solution.py:52
  165.7 3.7 %collective-permute-start.41 = (f32[8,128]{1,0:T(8,128)S(1)}, f32[8,128]{1,0:T(8,128)S(1)}, u32[]{:S(2)}, u32[]{:S(2)}) collective-permute-start(f32[8,128]{1,0:T(8,128)S(1)} %add.15), channel_id=1, source_target_pairs={{48,0},{49,1},{50,2},{51,3},{52,4},{53,5},{54,6},{55,7},{56,8},{57... | collective-permute-start | bytes 12296 | tf_op jit(solution)/shard_map/ppermute | solution.py:52
  169.4 4.3 %collective-permute-start.42 = (f32[8,128]{1,0:T(8,128)S(1)}, f32[8,128]{1,0:T(8,128)S(1)}, u32[]{:S(2)}, u32[]{:S(2)}) collective-permute-start(f32[8,128]{1,0:T(8,128)S(1)} %add_add_fusion), channel_id=1, source_target_pairs={{64,0},{65,1},{66,2},{67,3},{68,4},{69,5},{70,6},{71,7},{72,8},{73... | collective-permute-start | bytes 12296 | tf_op jit(solution)/shard_map/ppermute | solution.py:52
where the time goes:
time: 177 us; the launch traced here: 174 us
  starting transfers between devices  65.1 us (37%)
  Pallas kernels  59.7 us (34%)
  waiting for transfers between devices  43.4 us (25%)
  local copies, waits for them, and re-layouts  4.98 us (3%)
    ppermute x43, starting transfers between devices, from_device(): return lax.ppermute(block, ('pts', 'wlk'), route)  65.1 us
    ppermute x43, waiting for transfers between devices, from_device(): return lax.ppermute(block, ('pts', 'wlk'), route)  43.4 us
    pallas_call x9, Pallas kernels, exchange(): pl.pallas_call(body, in_specs=[scalars(), pl.BlockSpec(memory_space=pl.AN...  35 us
    pallas_call x2, Pallas kernels, split_columns(): pl.pallas_call(body, grid=(steps,), in_specs=[pl.BlockSpec((tile, cols),...  13.3 us
    pallas_call x2, Pallas kernels, theta_part(): pl.pallas_call(part, in_specs=[scalars()] + [whole()] * (n + 1 + len(more...  7.4 us
    unnamed x24, local copies, waits for them, and re-layouts  4.4 us
  transfers between devices with their start and end apart: 43, of which 13 were waited for; matrix products, arithmetic and copies ran while one was open for 0% of the time, Pallas kernels for 32%

commit v1 on v0

v1 whole, which is shorter than its diff:
```python
import jax
import jax.numpy as jnp
from jax import lax
from jax.experimental import pallas as pl
from jax.experimental.pallas import tpu as pltpu
from jax.sharding import PartitionSpec as P


F32 = jnp.float32
BF16 = jnp.bfloat16
PLANES, COLS, CORES = 2, 4, 2
ZLO, YS = 2, 4
EXTRA = 8
OWN, LEFT, RIGHT, SIDE, PLANE, FAR, SIDE2, FAR2 = "olrspfgh"
SLOTS = {
    LEFT: ((0, 3), (0, 3)),
    RIGHT: ((0, 1), (0, 1)),
    SIDE: ((1, 3), (1, 1)),
    PLANE: ((1, 0), (1, 0)),
    FAR: ((0, 2), (0, 2)),
    SIDE2: ((1, 1), (1, 3)),
    FAR2: ((1, 2), (1, 2)),
}
AXES = ("pts", "wlk")


def whole():
    return pl.BlockSpec(memory_space=pltpu.VMEM)


def scalars():
    return pl.BlockSpec(memory_space=pltpu.SMEM)


def call(body, shapes, operands, mib, flops=0, **more):
    return pl.pallas_call(
        body,
        in_specs=[scalars()] + [whole()] * (len(operands) - 1),
        out_specs=jax.tree.map(lambda _: whole(), shapes),
        out_shape=shapes,
        cost_estimate=pl.CostEstimate(flops=flops, bytes_accessed=flops // 300, transcendentals=0),
        compiler_params=pltpu.CompilerParams(vmem_limit_bytes=mib << 20),
        **more,
    )(*operands)


def pts_id(a, x, c):
    return ((a & (PLANES - 1)) * COLS + (x & (COLS - 1))) * CORES + (c & (CORES - 1))


def from_device(block, source):
    route = []
    for a in range(PLANES):
        for x in range(COLS):
            for c in range(CORES):
                for z in range(ZLO):
                    for y in range(YS):
                        sa, sx, sc, sz, sy = source(a, x, c, z, y)
                        start = pts_id(sa, sx, sc) * ZLO * YS + (sz & 1) * YS + (sy & 3)
                        route.append((start, pts_id(a, x, c) * ZLO * YS + z * YS + y))
    return lax.ppermute(block, AXES, route)


def from_chip(block, da, dx, dc=0):
    return from_device(block, lambda a, x, c, z, y: (a + da, x + dx, c + dc, z, y))


def from_group(block, dz, dy):
    return from_device(block, lambda a, x, c, z, y: (a, x, c, z + dz, y + dy))


def from_column(block, slot):
    def source(a, x, c, z, y):
        return a, x + SLOTS[slot][(y ^ c) & 1][1], c, z, y

    return from_device(block, source)


def place(ids_ref):
    here = ids_ref[0]
    return here >> 3, (here >> 1) & 3, here & 1, ids_ref[1] & 3


def takes(slot, a, x, c, odd):
    low = jnp.where((x & 3) < COLS // 2, 1, 0)
    return {
        OWN: c,
        LEFT: 0,
        RIGHT: 1,
        SIDE: odd,
        PLANE: a,
        FAR: 1 - low,
        SIDE2: 1 - odd,
        FAR2: low,
    }[slot]


def chip_of(slot, a, x, odd):
    (a0, x0), (a1, x1) = SLOTS.get(slot, ((0, 0), (0, 0)))
    return a + jnp.where(odd == 1, a1, a0), x + jnp.where(odd == 1, x1, x0)


def split_columns(array, pieces, steps, mib):
    rows, cols = array.shape
    width = cols // pieces
    tile = rows // steps

    def body(x_ref, o_ref):
        @pl.loop(0, tile // 40)
        def _(part):
            cut = pl.ds(pl.multiple_of(part * 40, 8), 40)
            for b in range(pieces):
                o_ref[b, cut, :] = x_ref[cut, b * width : (b + 1) * width]

    return pl.pallas_call(
        body,
        grid=(steps,),
        in_specs=[pl.BlockSpec((tile, cols), lambda i: (i, 0))],
        out_specs=pl.BlockSpec((pieces, tile, width), lambda i: (0, i, 0)),
        out_shape=jax.ShapeDtypeStruct((pieces, rows, width), array.dtype),
        compiler_params=pltpu.CompilerParams(vmem_limit_bytes=mib << 20),
    )(array)


def pick(ids, takes_second, one, two):
    def body(ids_ref, one_ref, two_ref, o_ref):
        second = takes_second(*place(ids_ref))

        @pl.when(second == 0)
        def _():
            o_ref[...] = one_ref[...]

        @pl.when(second != 0)
        def _():
            o_ref[...] = two_ref[...]

    return call(body, jax.ShapeDtypeStruct(one.shape, one.dtype), [ids, one, two], 4)


def group_block(ids_ref, key):
    zlo, y = ids_ref[1] >> 2, ids_ref[1] & 3
    return ((zlo + key[0]) & (ZLO - 1)) * YS + ((y + key[1]) & (YS - 1))


def theta_part(ids, green_cut, blocks, so_far=None, occ_t=None):
    keys = list(blocks)
    n = len(keys)
    rows = green_cut.shape[1]
    pts = blocks[keys[0]].shape[1]
    flops = 2 * rows * pts * green_cut.shape[2] * n
    operands = [ids, green_cut, *blocks.values()]
    if so_far is not None:
        operands.append(so_far)

    if occ_t is None:

        def part(ids_ref, g_ref, *refs):
            cs, o_ref = refs[:n], refs[-1]
            at = [group_block(ids_ref, key) for key in keys]

            @pl.loop(0, 2)
            def _(half):
                cut = pl.ds(pl.multiple_of(half * (rows // 2), 8), rows // 2)
                total = sum(
                    jnp.dot(g_ref[at[j], cut, :], cs[j][...], preferred_element_type=F32)
                    for j in range(n)
                )
                o_ref[cut, :] = total if so_far is None else refs[n][cut, :] + total

        return call(part, jax.ShapeDtypeStruct((rows, pts), F32), operands, 8, flops)

    elec = occ_t.shape[0]

    def last(ids_ref, g_ref, *refs):
        cs = refs[:n]
        acc_ref, occ_ref, t0_ref, t1_ref, *pick_refs, dens_ref = refs[n:]
        at = [group_block(ids_ref, key) for key in keys]
        th_refs = (t0_ref, t1_ref)
        occ = occ_ref[...].astype(F32)
        dens = []
        for w in range(2):
            cut = pl.ds(w * elec, elec)
            t = acc_ref[cut, :] + sum(
                jnp.dot(g_ref[at[j], cut, :], cs[j][...], preferred_element_type=F32)
                for j in range(n)
            )
            t = t.astype(BF16)
            th_refs[w][0:elec, :] = t
            dens.append(jnp.sum(t.astype(F32) * occ, axis=0, keepdims=True))
        dens_ref[0:1, :] = dens[0]
        dens_ref[1:2, :] = dens[1]
        row = lax.broadcasted_iota(jnp.int32, (EXTRA, pts), 0)
        tail = jnp.where(row == 0, dens[0], jnp.where(row == 1, dens[1], 0.0)).astype(BF16)
        for w in range(2):
            th_refs[w][elec : elec + EXTRA, :] = tail
        a, x, c, y = place(ids_ref)
        odd = (y ^ c) & 1
        goes = (
            odd,
            1 - odd,
            takes(FAR, a, x + 2, c, odd),
            takes(OWN, a, x, 1 - c, odd),
        )
        for w, o_ref in zip(goes, pick_refs):

            @pl.when(w == 0)
            def _():
                o_ref[...] = t0_ref[...]

            @pl.when(w != 0)
            def _():
                o_ref[...] = t1_ref[...]

    slab = jax.ShapeDtypeStruct((elec + EXTRA, pts), BF16)
    shapes = [slab] * 6 + [jax.ShapeDtypeStruct((2, pts), F32)]
    return call(last, shapes, operands + [occ_t], 8, flops)


def exchange(jobs, ids, own, kernel_cut, acc=None, density=None):
    n = len(jobs)
    elec, pts = jobs[0][3][0].shape
    contract_last = (((1,), (1,)), ((), ()))
    occ_blocks = [block for job in jobs for block in job[3]]
    n_occ = len(occ_blocks)
    first = acc is None

    def body(ids_ref, k_ref, *refs):
        os, ts, refs = refs[:n_occ], refs[n_occ : n_occ + n], refs[n_occ + n :]
        a, x, c, y = place(ids_ref)
        if first:
            ex_ref, pot_ref, own_ref, flip_ref = refs
            ex_ref[...] = jnp.zeros_like(ex_ref)
            pot_ref[...] = jnp.zeros_like(pot_ref)
            for to, block in enumerate((ts[0], ts[1], os[0])):
                flip_ref[0:elec, 0:pts] = block[0:elec, :].astype(F32)
                own_ref[to] = flip_ref[...].T[0:pts, 0:elec].astype(BF16)
        elif density is None:
            own_ref, _, _, ex_ref, pot_ref = refs
        else:
            own_ref, _, _, dens_ref, ex_ref, pot_ref, pot_out, vals_out = refs
        for j, (slot, core, walker, blocks, _, weight, adds) in enumerate(jobs):
            odd = (y ^ c ^ core) & 1
            w = takes(slot, a, x, c, odd) if walker is None else walker
            k = k_ref[pts_id(*chip_of(slot, a, x, odd), c + core)]
            if len(blocks) > 1:
                occ = jnp.where(odd == 0, os[0][...], os[1][...])
            else:
                occ = os[j][...]
            near = jnp.dot(own_ref[w], occ, preferred_element_type=F32)
            far = jnp.dot(own_ref[2], ts[j][0:elec, :], preferred_element_type=F32)
            prod = k.astype(F32) * near * far
            ex_ref[w] += weight * jnp.sum(prod.reshape(pts // 8, 8, pts), axis=0)
            if adds:
                dens = ts[j][elec : elec + EXTRA, :]
                pot_ref[...] += lax.dot_general(
                    dens, k, contract_last, preferred_element_type=F32
                )
        if density is not None:
            pot = pot_ref[0:2, :]
            pot_out[...] = pot
            lane = lax.broadcasted_iota(jnp.int32, (8, 128), 1)
            vals = jnp.zeros((8, 128), F32)
            for w in range(2):
                coulomb = 0.5 * jnp.sum(dens_ref[w : w + 1, :] * pot[w : w + 1, :])
                vals = jnp.where(lane == w, coulomb, vals)
                vals = jnp.where(lane == 2 + w, -0.5 * jnp.sum(ex_ref[w]), vals)
            vals_out[...] = vals

    shapes = [jax.ShapeDtypeStruct((2, 8, pts), F32), jax.ShapeDtypeStruct((EXTRA, pts), F32)]
    operands = [ids, kernel_cut] + occ_blocks + [job[4] for job in jobs]
    scratch, alias = [], {}
    if first:
        shapes += [jax.ShapeDtypeStruct((3, pts, elec), BF16)]
        scratch = [pltpu.VMEM((-(-elec // 128) * 128, -(-pts // 128) * 128), F32)]
    else:
        operands += [own]
        alias = {len(operands): 0, len(operands) + 1: 1}
        operands += acc
    if density is not None:
        operands += [density]
        shapes += [jax.ShapeDtypeStruct((2, pts), F32), jax.ShapeDtypeStruct((8, 128), F32)]
    flops = 4 * pts * pts * elec * n
    return call(
        body, shapes, operands, 8, flops, scratch_shapes=scratch, input_output_aliases=alias
    )


def everyone_total(v):
    v = v + from_chip(v, 0, 0, 1)
    r1, r2, r3 = (from_chip(v, 0, dx) for dx in (1, 2, 3))
    v = (v + r2) + (r1 + r3)
    return v + from_chip(v, 1, 0)


def local(green_half, collocation, occupied, kernel):
    walkers, elec, orb = green_half.shape
    ids = jnp.stack([lax.axis_index(axis) for axis in AXES]).astype(jnp.int32)
    occ_t = occupied.T

    coll = {(0, 0): collocation}
    coll[1, 0] = from_group(collocation, 1, 0)
    for dy in (2, 1, 3):
        coll[0, dy] = from_group(collocation, 0, dy)
    for dy in (1, 3):
        coll[1, dy] = from_group(coll[1, 0], 0, dy)
    coll[1, 2] = from_group(coll[0, 2], 1, 0)
    occ_left = from_column(occ_t, LEFT)
    occ_right = from_column(occ_t, RIGHT)
    occ_plane = from_chip(occ_t, 1, 0)
    occ_side = from_column(occ_plane, SIDE)
    occ_pick = pick(ids, lambda a, x, c, y: (y ^ c) & 1, occ_t, occ_plane)
    occ_far = from_column(occ_pick, FAR)

    def from_y(block):
        return from_device(block, lambda a, x, c, z, y: (a, x, c, z, y ^ 1))

    occ_side2 = from_y(occ_side)
    occ_far2 = from_y(occ_far)
    occ = {OWN: [occ_t], LEFT: [occ_left], RIGHT: [occ_right], FAR: [occ_far, occ_far2]}
    occ |= {SIDE: [occ_side], PLANE: [occ_plane], SIDE2: [occ_side2]}

    green = green_half.reshape(walkers * elec, orb)
    green_cut = split_columns(green, ZLO * YS, 4, 8)
    kernel_cut = split_columns(kernel, PLANES * COLS * CORES, 5, 12)

    def some(keys):
        return {k: coll[k] for k in keys}

    so_far = theta_part(ids, green_cut, some([(0, 0), (1, 0), (0, 2)]))
    middle = some([(0, 1), (0, 3), (1, 1), (1, 3)])
    so_far = theta_part(ids, green_cut, middle, so_far)
    t0, t1, t_first, t_second, t_far, t_sib, density = theta_part(
        ids, green_cut, some([(1, 2)]), so_far, occ_t
    )
    first = from_chip(t_first, 1, 0)
    second = from_chip(t_second, 1, 0)
    plane = pick(ids, lambda a, x, c, y: a ^ (y ^ c) & 1, first, second)
    far2 = pick(ids, lambda a, x, c, y: x >> 1 ^ (y ^ c) & 1, first, second)
    sends = {LEFT: t0, RIGHT: t1, FAR: t_far, SIDE: first, SIDE2: second, FAR2: far2}
    theta = {slot: from_column(sends[slot], slot) for slot in sends}
    theta |= {OWN: t_sib, PLANE: plane}
    theta_sib = {slot: from_chip(theta[slot], 0, 0, 1) for slot in theta}
    occ_sib = {slot: [from_chip(occ[slot][0], 0, 0, 1)] for slot in occ}
    occ_sib[FAR] += [from_chip(occ_far2, 0, 0, 1)]
    for known in (occ, occ_sib):
        known[FAR2] = known[FAR][::-1]

    own_jobs = [(OWN, 0, w, [occ_t], t, 1.0, w == 0) for w, t in enumerate((t0, t1))]
    *acc, own = exchange(own_jobs, ids, None, kernel_cut)

    for slot in (OWN, *SLOTS):
        if slot != OWN:
            same = (slot, 0, None, occ[slot], theta[slot], 2.0, True)
            acc = exchange([same], ids, own, kernel_cut, acc)
        sib = (slot, 1, None, occ_sib[slot], theta_sib[slot], 2.0, True)
        ending = density if slot == FAR2 else None
        acc = exchange([sib], ids, own, kernel_cut, acc, ending)
    _, _, potential, energies = acc
    energies = everyone_total(energies)
    return potential, energies[0, :walkers], energies[0, walkers : 2 * walkers]


def solution(mesh):
    split = P("wlk", "pts")
    placed = (P("wlk", None, None), split, P("pts", None), P("pts", None))

    return jax.shard_map(
        local,
        mesh=mesh,
        in_specs=placed,
        out_specs=(split, P("wlk"), P("wlk")),
        check_vma=False,
    )
```

time: 177 us -> 175 us (0.989)
  waiting for transfers between devices: 43.4 us -> 58.2 us
  Pallas kernels: 59.7 us -> 51.9 us
  starting transfers between devices: 65.1 us -> 58.9 us
    ppermute x43, waiting for transfers between devices: 43.4 us -> 58.2 us  [from_device(): return lax.ppermute(block, AXES, route)]
    ppermute x43, starting transfers between devices: 65.1 us -> 58.9 us  [from_device(): return lax.ppermute(block, AXES, route)]
    pallas_call x2, Pallas kernels: 13.3 us -> 9.18 us  [split_columns(): pl.pallas_call(body, grid=(steps,), in_specs=[pl.BlockSpec((tile, cols),...]
    pallas_call x15 -> x22, Pallas kernels: 46.4 us -> 42.7 us  [call(): pl.pallas_call(body, in_specs=[scalars()] + [whole()] * (len(operands) -...]
    unnamed x24 -> x16, local copies, waits for them, and re-layouts: 4.4 us -> 2.88 us
  transfers between devices with their start and end apart: 43 -> 43, of which waited for: 13 -> 14; matrix products, arithmetic and copies ran while one was open for 0% -> 0% of each run, Pallas kernels for 32% -> 28%
where the time goes in v1:
time: 175 us; the launch traced here: 174 us
  starting transfers between devices  58.9 us (34%)
  waiting for transfers between devices  58.2 us (33%)
  Pallas kernels  51.9 us (30%)
  local copies, waits for them, and re-layouts  3.47 us (2%)
    ppermute x43, starting transfers between devices, from_device(): return lax.ppermute(block, AXES, route)  58.9 us
    ppermute x43, waiting for transfers between devices, from_device(): return lax.ppermute(block, AXES, route)  58.2 us
    pallas_call x22, Pallas kernels, call(): pl.pallas_call(body, in_specs=[scalars()] + [whole()] * (len(operands) -...  42.7 us
    pallas_call x2, Pallas kernels, split_columns(): pl.pallas_call(body, grid=(steps,), in_specs=[pl.BlockSpec((tile, cols),...  9.18 us
  transfers between devices with their start and end apart: 43, of which 14 were waited for; matrix products, arithmetic and copies ran while one was open for 0% of the time, Pallas kernels for 28%

profile of v1, /device:TPU:1, one launch (start us, length us, event | category | flops | bytes accessed | tf_op | source)
XLA Modules:
  0.0 173.6 jit_solution(12778469188722193576)
XLA Ops:
  0.6 2.5 %collective-permute-start.9 = (bf16[300,600]{1,0:T(8,128)(2,1)}, bf16[300,600]{1,0:T(8,128)(2,1)}, u32[]{:S(2)}, u32[]{:S(2)}) collective-permute-start(bf16[300,600]{1,0:T(8,128)(2,1)} %refs_0_.1), channel_id=1, source_target_pairs={{4,0},{5,1},{6,2},{7,3},{0,4},{1,5},{2,6},{3,7},{12,8},{13,9},{14,... | collective-permute-start | bytes 1080008 | tf_op jit(solution)/shard_map/ppermute | solution.py:61
  3.2 2.9 %collective-permute-start.5 = (bf16[300,600]{1,0:T(8,128)(2,1)}, bf16[300,600]{1,0:T(8,128)(2,1)}, u32[]{:S(2)}, u32[]{:S(2)}) collective-permute-start(bf16[300,600]{1,0:T(8,128)(2,1)} %refs_0_.1), channel_id=1, source_target_pairs={{2,0},{3,1},{0,2},{1,3},{6,4},{7,5},{4,6},{5,7},{10,8},{11,9},{8,1... | collective-permute-start | bytes 1080008 | tf_op jit(solution)/shard_map/ppermute | solution.py:61
  6.1 0.8 collective-permute-start.7
  6.9 1.5 collective-permute-start.36
  8.4 1.2 collective-permute-start.32
  9.6 2.6 %collective-permute-done.9.refs_1_ = bf16[300,600]{1,0:T(8,128)(2,1)} collective-permute-done((bf16[300,600]{1,0:T(8,128)(2,1)}, bf16[300,600]{1,0:T(8,128)(2,1)}, u32[]{:S(2)}, u32[]{:S(2)}) %collective-permute-start.9) | collective-permute-done | bytes 360032 | tf_op jit(solution)/shard_map/ppermute | solution.py:61
  12.2 2.4 %collective-permute-start.28 = (bf16[400,600]{1,0:T(8,128)(2,1)}, bf16[400,600]{1,0:T(8,128)(2,1)S(1)}, u32[]{:S(2)}, u32[]{:S(2)}) collective-permute-start(bf16[400,600]{1,0:T(8,128)(2,1)} %bitcast.12), channel_id=1, source_target_pairs={{16,0},{17,1},{18,2},{19,3},{20,4},{21,5},{22,6},{23,7},{24,8},{25... | collective-permute-start | bytes 1440008 | tf_op jit(solution)/shard_map/ppermute | solution.py:61
  14.7 1.3 collective-permute-start.8
  16.0 7.6 %collective-permute-done.7.refs_0_ = bf16[300,600]{1,0:T(8,128)(2,1)S(1)} collective-permute-done((bf16[300,600]{1,0:T(8,128)(2,1)}, bf16[300,600]{1,0:T(8,128)(2,1)S(1)}, u32[]{:S(2)}, u32[]{:S(2)}) %collective-permute-start.7) | collective-permute-done | bytes 360032 | tf_op jit(solution)/shard_map/ppermute | solution.py:61
  23.6 3.3 %collective-permute-start = (bf16[400,600]{1,0:T(8,128)(2,1)}, bf16[400,600]{1,0:T(8,128)(2,1)S(1)}, u32[]{:S(2)}, u32[]{:S(2)}) collective-permute-start(bf16[400,600]{1,0:T(8,128)(2,1)} %bitcast.13), channel_id=1, source_target_pairs={{64,0},{65,1},{66,2},{67,3},{68,4},{69,5},{70,6},{71,7},{72,8},{73... | collective-permute-start | bytes 1440008 | tf_op jit(solution)/shard_map/ppermute | solution.py:61
  26.9 0.8 copy-done.3
  27.7 3.3 %collective-permute-start.10 = (bf16[300,600]{1,0:T(8,128)(2,1)}, bf16[300,600]{1,0:T(8,128)(2,1)}, u32[]{:S(2)}, u32[]{:S(2)}) collective-permute-start(bf16[300,600]{1,0:T(8,128)(2,1)} %collective-permute-done.9.refs_1_), channel_id=1, source_target_pairs={{1,0},{2,1},{3,2},{0,3},{5,4},{6,5},{7,6},{4,7},{9,8},{10,9},{11,1... | collective-permute-start | bytes 1080008 | tf_op jit(solution)/shard_map/ppermute | solution.py:61
  31.1 1.1 collective-permute-start.33
  32.2 5.5 %collective-permute-done.two_ref.refs_0_ = bf16[400,600]{1,0:T(8,128)(2,1)S(1)} collective-permute-done((bf16[400,600]{1,0:T(8,128)(2,1)}, bf16[400,600]{1,0:T(8,128)(2,1)S(1)}, u32[]{:S(2)}, u32[]{:S(2)}) %collective-permute-start) | collective-permute-done | bytes 480032 | tf_op jit(solution)/shard_map/ppermute | solution.py:61
  37.7 3.7 %collective-permute-start.29 = (bf16[400,600]{1,0:T(8,128)(2,1)S(1)}, bf16[400,600]{1,0:T(8,128)(2,1)S(1)}, u32[]{:S(2)}, u32[]{:S(2)}) collective-permute-start(bf16[400,600]{1,0:T(8,128)(2,1)S(1)} %collective-permute-done.28.refs_0_), channel_id=1, source_target_pairs={{8,0},{9,1},{10,2},{11,3},{12,4},{13,5},{14,6},{15,7},{0,8},{1,9},... | collective-permute-start | bytes 1440008 | tf_op jit(solution)/shard_map/ppermute | solution.py:61
  41.4 2.1 %copy-done.1 = bf16[2,400,2400]{2,1,0:T(8,128)(2,1)S(1)} copy-done((bf16[2,400,2400]{2,1,0:T(8,128)(2,1)S(1)}, bf16[2,400,2400]{2,1,0:T(8,128)(2,1)}, u32[]{:S(2)}) %copy-start.1) | copy-done | bytes 3840024
  43.5 3.4 %shard_map.69.g_ref = bf16[8,800,300]{2,1,0:T(8,128)(2,1)S(1)} custom-call(bf16[800,2400]{1,0:T(8,128)(2,1)S(1)} %bitcast.18), custom_call_target="tpu_custom_call" | custom-call | tf_op jit(solution)/shard_map/pallas_call | solution.py:115
  47.0 2.5 %collective-permute-start.16 = (bf16[400,600]{1,0:T(8,128)(2,1)S(1)}, bf16[400,600]{1,0:T(8,128)(2,1)S(1)}, u32[]{:S(2)}, u32[]{:S(2)}) collective-permute-start(bf16[400,600]{1,0:T(8,128)(2,1)S(1)} %collective-permute-done.two_ref.refs_0_), channel_id=1, source_target_pairs={{48,0},{17,1},{50,2},{19,3},{52,4},{21,5},{54,6},{23,7},{24,8},{57... | collective-permute-start | bytes 1440008 | tf_op jit(solution)/shard_map/ppermute | solution.py:61
  49.5 3.3 %shard_map.70.refs_4_ = f32[800,600]{1,0:T(8,128)S(1)} custom-call(s32[2]{0:T(128)S(1)} %pad_add_fusion.ids_ref, bf16[8,800,300]{2,1,0:T(8,128)(2,1)S(1)} %shard_map.69.g_ref, bf16[300,600]{1,0:T(8,128)(2,1)S(1)} %copy-done.2, bf16[300,600]{1,0:T(8,128)(2,1)} %collective-permute-done.9.refs_1_, bf16[300,600]{1,0:T(8,128)(2,1)} %collective-permute-done.5.refs_2_), custom_call_target="tpu_custom_call" | custom-call | flops 864000000 | bytes 2880000 | tf_op jit(solution)/shard_map/pallas_call | solution.py:36
  52.9 0.6 shard_map.68
  53.5 0.6 collective-permute-start.1
  54.1 1.2 collective-permute-start.23
  55.3 4.2 %shard_map.71.refs_1_ = f32[800,600]{1,0:T(8,128)S(1)} custom-call(s32[2]{0:T(128)S(1)} %pad_add_fusion.ids_ref, bf16[8,800,300]{2,1,0:T(8,128)(2,1)S(1)} %shard_map.69.g_ref, bf16[300,600]{1,0:T(8,128)(2,1)S(1)} %collective-permute-done.7.refs_0_, bf16[300,600]{1,0:T(8,128)(2,1)S(1)} %copy-done.4, bf16[300,600]{1,0:T(8,128)(2,1)} %collective-permute-done.10.refs_2_, ...), custom_call_target="tpu_custom_call" | custom-call | flops 1152000000 | bytes 3840000 | tf_op jit(solution)/shard_map/pallas_call | solution.py:36
  59.5 2.2 %shard_map.72 = (bf16[408,600]{1,0:T(8,128)(2,1)S(1)}, bf16[408,600]{1,0:T(8,128)(2,1)S(1)}, bf16[408,600]{1,0:T(8,128)(2,1)S(1)}, bf16[408,600]{1,0:T(8,128)(2,...) custom-call(s32[2]{0:T(128)S(1)} %pad_add_fusion.ids_ref, ...), custom_call_target="tpu_custom_call" | custom-call | flops 288000000 | bytes 960000 | tf_op jit(solution)/shard_map/pallas_call | solution.py:36
  61.9 4.6 %collective-permute-done.16.refs_0_ = bf16[400,600]{1,0:T(8,128)(2,1)S(1)} collective-permute-done((bf16[400,600]{1,0:T(8,128)(2,1)S(1)}, bf16[400,600]{1,0:T(8,128)(2,1)S(1)}, u32[]{:S(2)}, u32[]{:S(2)}) %collective-permute-start.16) | collective-permute-done | bytes 480032 | tf_op jit(solution)/shard_map/ppermute | solution.py:61
  66.6 3.6 %collective-permute-start.30 = (bf16[408,600]{1,0:T(8,128)(2,1)S(1)}, bf16[408,600]{1,0:T(8,128)(2,1)S(1)}, u32[]{:S(2)}, u32[]{:S(2)}) collective-permute-start(bf16[408,600]{1,0:T(8,128)(2,1)S(1)} %get-tuple-element.46.refs_3_), channel_id=1, source_target_pairs={{16,0},{17,1},{18,2},{19,3},{20,4},{21,5},{22,6},{23,7},{24,8},{25... | collective-permute-start | bytes 1468808 | tf_op jit(solution)/shard_map/ppermute | solution.py:61
  70.1 3.2 %collective-permute-start.12 = (bf16[408,600]{1,0:T(8,128)(2,1)S(1)}, bf16[408,600]{1,0:T(8,128)(2,1)S(1)}, u32[]{:S(2)}, u32[]{:S(2)}) collective-permute-start(bf16[408,600]{1,0:T(8,128)(2,1)S(1)} %get-tuple-element.43), channel_id=1, source_target_pairs={{64,0},{65,1},{66,2},{67,3},{68,4},{69,5},{70,6},{71,7},{72,8},{73... | collective-permute-start | bytes 1468808 | tf_op jit(solution)/shard_map/ppermute | solution.py:61
  73.5 6.5 %collective-permute-done.34.refs_1_ = bf16[408,600]{1,0:T(8,128)(2,1)S(1)} collective-permute-done((bf16[408,600]{1,0:T(8,128)(2,1)S(1)}, bf16[408,600]{1,0:T(8,128)(2,1)S(1)}, u32[]{:S(2)}, u32[]{:S(2)}) %collective-permute-start.34) | collective-permute-done | bytes 489632 | tf_op jit(solution)/shard_map/ppermute | solution.py:61
  80.5 8.3 %collective-permute-done.30.refs_1_ = bf16[408,600]{1,0:T(8,128)(2,1)S(1)} collective-permute-done((bf16[408,600]{1,0:T(8,128)(2,1)S(1)}, bf16[408,600]{1,0:T(8,128)(2,1)S(1)}, u32[]{:S(2)}, u32[]{:S(2)}) %collective-permute-start.30) | collective-permute-done | bytes 489632 | tf_op jit(solution)/shard_map/ppermute | solution.py:61
  88.9 2.1 %collective-permute-start.4 = (bf16[400,600]{1,0:T(8,128)(2,1)S(1)}, bf16[400,600]{1,0:T(8,128)(2,1)S(1)}, u32[]{:S(2)}, u32[]{:S(2)}) collective-permute-start(bf16[400,600]{1,0:T(8,128)(2,1)S(1)} %collective-permute-done.1.refs_0_.refs_1_), channel_id=1, source_target_pairs={{8,0},{9,1},{10,2},{11,3},{12,4},{13,5},{14,6},{15,7},{0,8},{1,9},... | collective-permute-start | bytes 1440008 | tf_op jit(solution)/shard_map/ppermute | solution.py:61
  90.9 1.4 collective-permute-done.13.two_ref
  92.9 1.8 %collective-permute-start.26 = (bf16[408,600]{1,0:T(8,128)(2,1)S(1)}, bf16[408,600]{1,0:T(8,128)(2,1)S(1)}, u32[]{:S(2)}, u32[]{:S(2)}) collective-permute-start(bf16[408,600]{1,0:T(8,128)(2,1)S(1)} %collective-permute-done.12.one_ref), channel_id=1, source_target_pairs={{48,0},{17,1},{50,2},{19,3},{52,4},{21,5},{54,6},{23,7},{24,8},{57... | collective-permute-start | bytes 1468808 | tf_op jit(solution)/shard_map/ppermute | solution.py:61
  94.7 7.3 %collective-permute-done.2.refs_1_.refs_0_ = bf16[400,600]{1,0:T(8,128)(2,1)S(1)} collective-permute-done((bf16[400,600]{1,0:T(8,128)(2,1)S(1)}, bf16[400,600]{1,0:T(8,128)(2,1)S(1)}, u32[]{:S(2)}, u32[]{:S(2)}) %collective-permute-start.2) | collective-permute-done | bytes 480032 | tf_op jit(solution)/shard_map/ppermute | solution.py:61
  102.0 1.4 collective-permute-start.31
  103.4 0.6 shard_map.75.refs_1_
  104.1 8.8 %collective-permute-done.17.refs_0_ = bf16[400,600]{1,0:T(8,128)(2,1)S(1)} collective-permute-done((bf16[400,600]{1,0:T(8,128)(2,1)S(1)}, bf16[400,600]{1,0:T(8,128)(2,1)S(1)}, u32[]{:S(2)}, u32[]{:S(2)}) %collective-permute-start.17) | collective-permute-done | bytes 480032 | tf_op jit(solution)/shard_map/ppermute | solution.py:61
  113.0 0.6 shard_map.73
  113.6 4.1 %collective-permute-start.14 = (bf16[408,600]{1,0:T(8,128)(2,1)S(1)}, bf16[408,600]{1,0:T(8,128)(2,1)S(1)}, u32[]{:S(2)}, u32[]{:S(2)}) collective-permute-start(bf16[408,600]{1,0:T(8,128)(2,1)S(1)} %shard_map.73), channel_id=1, source_target_pairs={{32,0},{33,1},{34,2},{35,3},{36,4},{37,5},{38,6},{39,7},{40,8},{41... | collective-permute-start | bytes 1468808 | tf_op jit(solution)/shard_map/ppermute | solution.py:61
  118.1 5.8 %shard_map.67.k_ref = bf16[16,600,600]{2,1,0:T(8,128)(2,1)S(1)} custom-call(bf16[600,9600]{1,0:T(8,128)(2,1)S(1)} %bitcast.9), custom_call_target="tpu_custom_call" | custom-call | tf_op jit(solution)/shard_map/pallas_call | solution.py:115
  123.9 3.0 %shard_map.74 = (f32[2,8,600]{2,1,0:T(8,128)S(1)}, f32[8,600]{1,0:T(8,128)S(1)}, bf16[3,600,400]{2,1,0:T(8,128)(2,1)S(1)}) custom-call(s32[2]{0:T(128)S(1)} %pad_add_fusion.ids_ref, bf16[16,600,600]{2,1,0:T(8,128)(2,1)S(1)} %shard_map.67.k_ref, bf16[400,600]{1,0:T(8,128)(2,1)S(1)} %bitcast.16, bf16[400,600]{1,0:T(8,128)(2,1)S(1)} %bitcast.17, ...), custom_call_target="tpu_custom_call" | custom-call | flops 1152000000 | bytes 3840000 | tf_op jit(solution)/shard_map/pallas_call | solution.py:36
  127.1 1.8 %shard_map.76 = (f32[2,8,600]{2,1,0:T(8,128)S(1)}, f32[8,600]{1,0:T(8,128)S(1)}) custom-call(s32[2]{0:T(128)S(1)} %pad_add_fusion.ids_ref, bf16[16,600,600]{2,1,0:T(8,128)(2,1)S(1)} %shard_map.67.k_ref, bf16[400,600]{1,0:T(8,128)(2,1)S(1)} %collective-permute-done.36.refs_0_, ...), custom_call_target="tpu_custom_call", output_to_operand_aliasing={{0}: (5, {}), {1}: (6, {})} | custom-call | flops 576000000 | bytes 1920000 | tf_op jit(solution)/shard_map/pallas_call | solution.py:36
  129.4 1.8 %shard_map.77 = (f32[2,8,600]{2,1,0:T(8,128)S(1)}, f32[8,600]{1,0:T(8,128)S(1)}) custom-call(s32[2]{0:T(128)S(1)} %pad_add_fusion.ids_ref, bf16[16,600,600]{2,1,0:T(8,128)(2,1)S(1)} %shard_map.67.k_ref, bf16[400,600]{1,0:T(8,128)(2,1)S(1)} %collective-permute-done.32.refs_0_, ...), custom_call_target="tpu_custom_call", output_to_operand_aliasing={{0}: (5, {}), {1}: (6, {})} | custom-call | flops 576000000 | bytes 1920000 | tf_op jit(solution)/shard_map/pallas_call | solution.py:36
  131.2 3.6 %collective-permute-start.20 = (bf16[408,600]{1,0:T(8,128)(2,1)S(1)}, bf16[408,600]{1,0:T(8,128)(2,1)S(1)}, u32[]{:S(2)}, u32[]{:S(2)}) collective-permute-start(bf16[408,600]{1,0:T(8,128)(2,1)S(1)} %collective-permute-done.19.refs_1_), channel_id=1, source_target_pairs={{8,0},{9,1},{10,2},{11,3},{12,4},{13,5},{14,6},{15,7},{0,8},{1,9},... | collective-permute-start | bytes 1468808 | tf_op jit(solution)/shard_map/ppermute | solution.py:61
  134.8 1.8 %shard_map.78 = (f32[2,8,600]{2,1,0:T(8,128)S(1)}, f32[8,600]{1,0:T(8,128)S(1)}) custom-call(s32[2]{0:T(128)S(1)} %pad_add_fusion.ids_ref, bf16[16,600,600]{2,1,0:T(8,128)(2,1)S(1)} %shard_map.67.k_ref, bf16[400,600]{1,0:T(8,128)(2,1)S(1)} %collective-permute-done.33.refs_0_, ...), custom_call_target="tpu_custom_call", output_to_operand_aliasing={{0}: (5, {}), {1}: (6, {})} | custom-call | flops 576000000 | bytes 1920000 | tf_op jit(solution)/shard_map/pallas_call | solution.py:36
  136.7 1.8 %shard_map.79 = (f32[2,8,600]{2,1,0:T(8,128)S(1)}, f32[8,600]{1,0:T(8,128)S(1)}) custom-call(s32[2]{0:T(128)S(1)} %pad_add_fusion.ids_ref, bf16[16,600,600]{2,1,0:T(8,128)(2,1)S(1)} %shard_map.67.k_ref, bf16[400,600]{1,0:T(8,128)(2,1)S(1)} %collective-permute-done.28.refs_0_, ...), custom_call_target="tpu_custom_call", output_to_operand_aliasing={{0}: (5, {}), {1}: (6, {})} | custom-call | flops 576000000 | bytes 1920000 | tf_op jit(solution)/shard_map/pallas_call | solution.py:36
  138.6 0.8 collective-permute-start.15
  139.4 1.8 %shard_map.80 = (f32[2,8,600]{2,1,0:T(8,128)S(1)}, f32[8,600]{1,0:T(8,128)S(1)}) custom-call(s32[2]{0:T(128)S(1)} %pad_add_fusion.ids_ref, bf16[16,600,600]{2,1,0:T(8,128)(2,1)S(1)} %shard_map.67.k_ref, bf16[400,600]{1,0:T(8,128)(2,1)S(1)} %collective-permute-done.29.refs_0_, ...), custom_call_target="tpu_custom_call", output_to_operand_aliasing={{0}: (5, {}), {1}: (6, {})} | custom-call | flops 576000000 | bytes 1920000 | tf_op jit(solution)/shard_map/pallas_call | solution.py:36
  141.2 1.9 %shard_map.81 = (f32[2,8,600]{2,1,0:T(8,128)S(1)}, f32[8,600]{1,0:T(8,128)S(1)}) custom-call(s32[2]{0:T(128)S(1)} %pad_add_fusion.ids_ref, bf16[16,600,600]{2,1,0:T(8,128)(2,1)S(1)} %shard_map.67.k_ref, bf16[400,600]{1,0:T(8,128)(2,1)S(1)} %collective-permute-done.16.refs_0_, ...), custom_call_target="tpu_custom_call", output_to_operand_aliasing={{0}: (5, {}), {1}: (6, {})} | custom-call | flops 576000000 | bytes 1920000 | tf_op jit(solution)/shard_map/pallas_call | solution.py:36
  143.0 1.8 %shard_map.82 = (f32[2,8,600]{2,1,0:T(8,128)S(1)}, f32[8,600]{1,0:T(8,128)S(1)}) custom-call(s32[2]{0:T(128)S(1)} %pad_add_fusion.ids_ref, bf16[16,600,600]{2,1,0:T(8,128)(2,1)S(1)} %shard_map.67.k_ref, bf16[400,600]{1,0:T(8,128)(2,1)S(1)} %collective-permute-done.25.refs_0_, ...), custom_call_target="tpu_custom_call", output_to_operand_aliasing={{0}: (5, {}), {1}: (6, {})} | custom-call | flops 576000000 | bytes 1920000 | tf_op jit(solution)/shard_map/pallas_call | solution.py:36
  144.9 1.9 %shard_map.83 = (f32[2,8,600]{2,1,0:T(8,128)S(1)}, f32[8,600]{1,0:T(8,128)S(1)}) custom-call(s32[2]{0:T(128)S(1)} %pad_add_fusion.ids_ref, bf16[16,600,600]{2,1,0:T(8,128)(2,1)S(1)} %shard_map.67.k_ref, bf16[400,600]{1,0:T(8,128)(2,1)S(1)} %collective-permute-done.two_ref.refs_0_, ...), custom_call_target="tpu_custom_call", output_to_operand_aliasing={{0}: (5, {}), {1}: (6, {})} | custom-call | flops 576000000 | bytes 1920000 | tf_op jit(solution)/shard_map/pallas_call | solution.py:36
  146.7 1.9 %shard_map.84 = (f32[2,8,600]{2,1,0:T(8,128)S(1)}, f32[8,600]{1,0:T(8,128)S(1)}) custom-call(s32[2]{0:T(128)S(1)} %pad_add_fusion.ids_ref, bf16[16,600,600]{2,1,0:T(8,128)(2,1)S(1)} %shard_map.67.k_ref, bf16[400,600]{1,0:T(8,128)(2,1)S(1)} %collective-permute-done.23.refs_0_, ...), custom_call_target="tpu_custom_call", output_to_operand_aliasing={{0}: (5, {}), {1}: (6, {})} | custom-call | flops 576000000 | bytes 1920000 | tf_op jit(solution)/shard_map/pallas_call | solution.py:36
  148.6 1.9 %shard_map.85 = (f32[2,8,600]{2,1,0:T(8,128)S(1)}, f32[8,600]{1,0:T(8,128)S(1)}) custom-call(s32[2]{0:T(128)S(1)} %pad_add_fusion.ids_ref, bf16[16,600,600]{2,1,0:T(8,128)(2,1)S(1)} %shard_map.67.k_ref, bf16[400,600]{1,0:T(8,128)(2,1)S(1)} %collective-permute-done.1.refs_0_.refs_1_, ...), custom_call_target="tpu_custom_call", output_to_operand_aliasing={{0}: (6, {}), {1}: (7, {})} | custom-call | flops 576000000 | bytes 1920000 | tf_op jit(solution)/shard_map/pallas_call | solution.py:36
  150.5 1.8 %shard_map.86 = (f32[2,8,600]{2,1,0:T(8,128)S(1)}, f32[8,600]{1,0:T(8,128)S(1)}) custom-call(s32[2]{0:T(128)S(1)} %pad_add_fusion.ids_ref, bf16[16,600,600]{2,1,0:T(8,128)(2,1)S(1)} %shard_map.67.k_ref, bf16[400,600]{1,0:T(8,128)(2,1)S(1)} %collective-permute-done.4.refs_0_.refs_1_, ...), custom_call_target="tpu_custom_call", output_to_operand_aliasing={{0}: (6, {}), {1}: (7, {})} | custom-call | flops 576000000 | bytes 1920000 | tf_op jit(solution)/shard_map/pallas_call | solution.py:36
  152.4 1.8 %shard_map.87 = (f32[2,8,600]{2,1,0:T(8,128)S(1)}, f32[8,600]{1,0:T(8,128)S(1)}) custom-call(s32[2]{0:T(128)S(1)} %pad_add_fusion.ids_ref, bf16[16,600,600]{2,1,0:T(8,128)(2,1)S(1)} %shard_map.67.k_ref, bf16[400,600]{1,0:T(8,128)(2,1)S(1)} %collective-permute-done.17.refs_0_, ...), custom_call_target="tpu_custom_call", output_to_operand_aliasing={{0}: (5, {}), {1}: (6, {})} | custom-call | flops 576000000 | bytes 1920000 | tf_op jit(solution)/shard_map/pallas_call | solution.py:36
  154.2 1.8 %shard_map.88 = (f32[2,8,600]{2,1,0:T(8,128)S(1)}, f32[8,600]{1,0:T(8,128)S(1)}) custom-call(s32[2]{0:T(128)S(1)} %pad_add_fusion.ids_ref, bf16[16,600,600]{2,1,0:T(8,128)(2,1)S(1)} %shard_map.67.k_ref, bf16[400,600]{1,0:T(8,128)(2,1)S(1)} %collective-permute-done.18.refs_0_, ...), custom_call_target="tpu_custom_call", output_to_operand_aliasing={{0}: (5, {}), {1}: (6, {})} | custom-call | flops 576000000 | bytes 1920000 | tf_op jit(solution)/shard_map/pallas_call | solution.py:36
  156.1 1.9 %shard_map.89 = (f32[2,8,600]{2,1,0:T(8,128)S(1)}, f32[8,600]{1,0:T(8,128)S(1)}) custom-call(s32[2]{0:T(128)S(1)} %pad_add_fusion.ids_ref, bf16[16,600,600]{2,1,0:T(8,128)(2,1)S(1)} %shard_map.67.k_ref, bf16[400,600]{1,0:T(8,128)(2,1)S(1)} %collective-permute-done.2.refs_1_.refs_0_, ...), custom_call_target="tpu_custom_call", output_to_operand_aliasing={{0}: (6, {}), {1}: (7, {})} | custom-call | flops 576000000 | bytes 1920000 | tf_op jit(solution)/shard_map/pallas_call | solution.py:36
  158.0 2.5 %shard_map.90 = (f32[2,8,600]{2,1,0:T(8,128)S(1)}, f32[8,600]{1,0:T(8,128)S(1)}, f32[2,600]{1,0:T(2,128)}, f32[8,128]{1,0:T(8,128)S(1)}) custom-call(s32[2]{0:T(128)S(1)} %pad_add_fusion.ids_ref, bf16[16,600,600]{2,1,0:T(8,128)(2,1)S(1)} %shard_map.67.k_ref, ...), custom_call_target="tpu_custom_call", output_to_operand_aliasing={{0}: (6, {}), {1}: (7, {})} | custom-call | flops 576000000 | bytes 1920000 | tf_op jit(solution)/shard_map/pallas_call | solution.py:36
  160.5 1.1 collective-permute-done.38
  161.6 3.4 %collective-permute-start.40 = (f32[8,128]{1,0:T(8,128)S(1)}, f32[8,128]{1,0:T(8,128)S(1)}, u32[]{:S(2)}, u32[]{:S(2)}) collective-permute-start(f32[8,128]{1,0:T(8,128)S(1)} %add.15), channel_id=1, source_target_pairs={{16,0},{17,1},{18,2},{19,3},{20,4},{21,5},{22,6},{23,7},{24,8},{25... | collective-permute-start | bytes 12296 | tf_op jit(solution)/shard_map/ppermute | solution.py:61
  165.7 1.0 collective-permute-done.40
  166.7 2.1 %collective-permute-done.41 = f32[8,128]{1,0:T(8,128)S(1)} collective-permute-done((f32[8,128]{1,0:T(8,128)S(1)}, f32[8,128]{1,0:T(8,128)S(1)}, u32[]{:S(2)}, u32[]{:S(2)}) %collective-permute-start.41) | collective-permute-done | bytes 4128 | tf_op jit(solution)/shard_map/ppermute | solution.py:61
  168.7 3.2 %collective-permute-start.42 = (f32[8,128]{1,0:T(8,128)S(1)}, f32[8,128]{1,0:T(8,128)S(1)}, u32[]{:S(2)}, u32[]{:S(2)}) collective-permute-start(f32[8,128]{1,0:T(8,128)S(1)} %add_add_fusion), channel_id=1, source_target_pairs={{64,0},{65,1},{66,2},{67,3},{68,4},{69,5},{70,6},{71,7},{72,8},{73... | collective-permute-start | bytes 12296 | tf_op jit(solution)/shard_map/ppermute | solution.py:61
  172.0 1.0 collective-permute-done.42
  173.0 0.6 slice_bitcast_fusion
  (68 shorter events, 3.6 us)
Async XLA Ops:
  0.6 11.6 %collective-permute-start.9 = (bf16[300,600]{1,0:T(8,128)(2,1)}, bf16[300,600]{1,0:T(8,128)(2,1)}, u32[]{:S(2)}, u32[]{:S(2)}) collective-permute-start(bf16[300,600]{1,0:T(8,128)(2,1)} %refs_0_.1), channel_id=1, source_target_pairs={{4,0},{5,1},{6,2},{7,3},{0,4},{1,5},{2,6},{3,7},{12,8},{13,9},{14,... | collective-permute-start | bytes 1080008 | tf_op jit(solution)/shard_map/ppermute | solution.py:61
  3.2 11.5 %collective-permute-start.5 = (bf16[300,600]{1,0:T(8,128)(2,1)}, bf16[300,600]{1,0:T(8,128)(2,1)}, u32[]{:S(2)}, u32[]{:S(2)}) collective-permute-start(bf16[300,600]{1,0:T(8,128)(2,1)} %refs_0_.1), channel_id=1, source_target_pairs={{2,0},{3,1},{0,2},{1,3},{6,4},{7,5},{4,6},{5,7},{10,8},{11,9},{8,1... | collective-permute-start | bytes 1080008 | tf_op jit(solution)/shard_map/ppermute | solution.py:61
  6.1 17.5 %collective-permute-start.7 = (bf16[300,600]{1,0:T(8,128)(2,1)}, bf16[300,600]{1,0:T(8,128)(2,1)S(1)}, u32[]{:S(2)}, u32[]{:S(2)}) collective-permute-start(bf16[300,600]{1,0:T(8,128)(2,1)} %refs_0_.1), channel_id=1, source_target_pairs={{1,0},{2,1},{3,2},{0,3},{5,4},{6,5},{7,6},{4,7},{9,8},{10,9},{11,1... | collective-permute-start | bytes 1080008 | tf_op jit(solution)/shard_map/ppermute | solution.py:61
  6.9 24.1 %collective-permute-start.36 = (bf16[400,600]{1,0:T(8,128)(2,1)}, bf16[400,600]{1,0:T(8,128)(2,1)S(1)}, u32[]{:S(2)}, u32[]{:S(2)}) collective-permute-start(bf16[400,600]{1,0:T(8,128)(2,1)} %bitcast.10), channel_id=1, source_target_pairs={{8,0},{9,1},{10,2},{11,3},{12,4},{13,5},{14,6},{15,7},{0,8},{1,9},... | collective-permute-start | bytes 1440008 | tf_op jit(solution)/shard_map/ppermute | solution.py:61
  8.4 22.6 %collective-permute-start.32 = (bf16[400,600]{1,0:T(8,128)(2,1)}, bf16[400,600]{1,0:T(8,128)(2,1)S(1)}, u32[]{:S(2)}, u32[]{:S(2)}) collective-permute-start(bf16[400,600]{1,0:T(8,128)(2,1)} %bitcast.11), channel_id=1, source_target_pairs={{48,0},{49,1},{50,2},{51,3},{52,4},{53,5},{54,6},{55,7},{56,8},{57... | collective-permute-start | bytes 1440008 | tf_op jit(solution)/shard_map/ppermute | solution.py:61
  12.2 18.9 %collective-permute-start.28 = (bf16[400,600]{1,0:T(8,128)(2,1)}, bf16[400,600]{1,0:T(8,128)(2,1)S(1)}, u32[]{:S(2)}, u32[]{:S(2)}) collective-permute-start(bf16[400,600]{1,0:T(8,128)(2,1)} %bitcast.12), channel_id=1, source_target_pairs={{16,0},{17,1},{18,2},{19,3},{20,4},{21,5},{22,6},{23,7},{24,8},{25... | collective-permute-start | bytes 1440008 | tf_op jit(solution)/shard_map/ppermute | solution.py:61
  14.7 12.3 %collective-permute-start.8 = (bf16[300,600]{1,0:T(8,128)(2,1)}, bf16[300,600]{1,0:T(8,128)(2,1)S(1)}, u32[]{:S(2)}, u32[]{:S(2)}) collective-permute-start(bf16[300,600]{1,0:T(8,128)(2,1)} %refs_0_.1), channel_id=1, source_target_pairs={{3,0},{0,1},{1,2},{2,3},{7,4},{4,5},{5,6},{6,7},{11,8},{8,9},{9,10... | collective-permute-start | bytes 1080008 | tf_op jit(solution)/shard_map/ppermute | solution.py:61
  23.6 14.1 %collective-permute-start = (bf16[400,600]{1,0:T(8,128)(2,1)}, bf16[400,600]{1,0:T(8,128)(2,1)S(1)}, u32[]{:S(2)}, u32[]{:S(2)}) collective-permute-start(bf16[400,600]{1,0:T(8,128)(2,1)} %bitcast.13), channel_id=1, source_target_pairs={{64,0},{65,1},{66,2},{67,3},{68,4},{69,5},{70,6},{71,7},{72,8},{73... | collective-permute-start | bytes 1440008 | tf_op jit(solution)/shard_map/ppermute | solution.py:61
  26.9 0.8 copy-start.3
  27.7 19.3 %collective-permute-start.10 = (bf16[300,600]{1,0:T(8,128)(2,1)}, bf16[300,600]{1,0:T(8,128)(2,1)}, u32[]{:S(2)}, u32[]{:S(2)}) collective-permute-start(bf16[300,600]{1,0:T(8,128)(2,1)} %collective-permute-done.9.refs_1_), channel_id=1, source_target_pairs={{1,0},{2,1},{3,2},{0,3},{5,4},{6,5},{7,6},{4,7},{9,8},{10,9},{11,1... | collective-permute-start | bytes 1080008 | tf_op jit(solution)/shard_map/ppermute | solution.py:61
  31.0 22.5 %collective-permute-start.11 = (bf16[300,600]{1,0:T(8,128)(2,1)}, bf16[300,600]{1,0:T(8,128)(2,1)}, u32[]{:S(2)}, u32[]{:S(2)}) collective-permute-start(bf16[300,600]{1,0:T(8,128)(2,1)} %collective-permute-done.9.refs_1_), channel_id=1, source_target_pairs={{3,0},{0,1},{1,2},{2,3},{7,4},{4,5},{5,6},{6,7},{11,8},{8,9},{9,10... | collective-permute-start | bytes 1080008 | tf_op jit(solution)/shard_map/ppermute | solution.py:61
  31.0 23.1 %collective-permute-start.6 = (bf16[300,600]{1,0:T(8,128)(2,1)}, bf16[300,600]{1,0:T(8,128)(2,1)}, u32[]{:S(2)}, u32[]{:S(2)}) collective-permute-start(bf16[300,600]{1,0:T(8,128)(2,1)} %collective-permute-done.5.refs_2_), channel_id=1, source_target_pairs={{4,0},{5,1},{6,2},{7,3},{0,4},{1,5},{2,6},{3,7},{12,8},{13,9},{14,... | collective-permute-start | bytes 1080008 | tf_op jit(solution)/shard_map/ppermute | solution.py:61
  31.1 30.6 %collective-permute-start.33 = (bf16[400,600]{1,0:T(8,128)(2,1)S(1)}, bf16[400,600]{1,0:T(8,128)(2,1)S(1)}, u32[]{:S(2)}, u32[]{:S(2)}) collective-permute-start(bf16[400,600]{1,0:T(8,128)(2,1)S(1)} %collective-permute-done.32.refs_0_), channel_id=1, source_target_pairs={{8,0},{9,1},{10,2},{11,3},{12,4},{13,5},{14,6},{15,7},{0,8},{1,9},... | collective-permute-start | bytes 1440008 | tf_op jit(solution)/shard_map/ppermute | solution.py:61
  37.7 24.1 %collective-permute-start.29 = (bf16[400,600]{1,0:T(8,128)(2,1)S(1)}, bf16[400,600]{1,0:T(8,128)(2,1)S(1)}, u32[]{:S(2)}, u32[]{:S(2)}) collective-permute-start(bf16[400,600]{1,0:T(8,128)(2,1)S(1)} %collective-permute-done.28.refs_0_), channel_id=1, source_target_pairs={{8,0},{9,1},{10,2},{11,3},{12,4},{13,5},{14,6},{15,7},{0,8},{1,9},... | collective-permute-start | bytes 1440008 | tf_op jit(solution)/shard_map/ppermute | solution.py:61
  41.4 2.1 %copy-start.1 = (bf16[2,400,2400]{2,1,0:T(8,128)(2,1)S(1)}, bf16[2,400,2400]{2,1,0:T(8,128)(2,1)}, u32[]{:S(2)}) copy-start(bf16[2,400,2400]{2,1,0:T(8,128)(2,1)} %param.4) | copy-start | bytes 11520004
  43.5 6.0 %copy-start.2 = (bf16[300,600]{1,0:T(8,128)(2,1)S(1)}, bf16[300,600]{1,0:T(8,128)(2,1)}, u32[]{:S(2)}) copy-start(bf16[300,600]{1,0:T(8,128)(2,1)} %refs_0_.1) | copy-start | bytes 1080004
  47.0 5.9 %copy-start = (bf16[600,400]{0,1:T(8,128)(2,1)S(1)}, bf16[600,400]{0,1:T(8,128)(2,1)}, u32[]{:S(2)}) copy-start(bf16[600,400]{0,1:T(8,128)(2,1)} %param.6) | copy-start | bytes 1440004
  47.0 8.3 %copy-start.4 = (bf16[300,600]{1,0:T(8,128)(2,1)S(1)}, bf16[300,600]{1,0:T(8,128)(2,1)}, u32[]{:S(2)}) copy-start(bf16[300,600]{1,0:T(8,128)(2,1)} %copy-done.3) | copy-start | bytes 1080004
  47.0 19.6 %collective-permute-start.16 = (bf16[400,600]{1,0:T(8,128)(2,1)S(1)}, bf16[400,600]{1,0:T(8,128)(2,1)S(1)}, u32[]{:S(2)}, u32[]{:S(2)}) collective-permute-start(bf16[400,600]{1,0:T(8,128)(2,1)S(1)} %collective-permute-done.two_ref.refs_0_), channel_id=1, source_target_pairs={{48,0},{17,1},{50,2},{19,3},{52,4},{21,5},{54,6},{23,7},{24,8},{57... | collective-permute-start | bytes 1440008 | tf_op jit(solution)/shard_map/ppermute | solution.py:61
  53.5 19.9 %collective-permute-start.1 = (bf16[400,600]{1,0:T(8,128)(2,1)S(1)}, bf16[400,600]{1,0:T(8,128)(2,1)S(1)}, u32[]{:S(2)}, u32[]{:S(2)}) collective-permute-start(bf16[400,600]{1,0:T(8,128)(2,1)S(1)} %shard_map.68), channel_id=1, source_target_pairs={{32,0},{33,1},{34,2},{35,3},{36,4},{37,5},{38,6},{39,7},{40,8},{41... | collective-permute-start | bytes 1440008 | tf_op jit(solution)/shard_map/ppermute | solution.py:61
  54.1 16.0 %collective-permute-start.23 = (bf16[400,600]{1,0:T(8,128)(2,1)S(1)}, bf16[400,600]{1,0:T(8,128)(2,1)S(1)}, u32[]{:S(2)}, u32[]{:S(2)}) collective-permute-start(bf16[400,600]{1,0:T(8,128)(2,1)S(1)} %collective-permute-done.two_ref.refs_0_), channel_id=1, source_target_pairs={{8,0},{9,1},{10,2},{11,3},{12,4},{13,5},{14,6},{15,7},{0,8},{1,9},... | collective-permute-start | bytes 1440008 | tf_op jit(solution)/shard_map/ppermute | solution.py:61
  55.3 62.8 %slice-start = ((s8[11520000]{0:T(1024)(128)(4,1)}), s8[4194304]{0:T(1024)(128)(4,1)S(1)}, s32[]{:S(2)}) async-start(s8[11520000]{0:T(1024)(128)(4,1)} %bitcast.8), calls=%async_computation | async-start | bytes 8388608
  55.3 62.8 %slice-start.1 = ((s8[11520000]{0:T(1024)(128)(4,1)}), s8[4194304]{0:T(1024)(128)(4,1)S(1)}, s32[]{:S(2)}) async-start(s8[11520000]{0:T(1024)(128)(4,1)} %bitcast.8), calls=%async_computation.1 | async-start | bytes 8388608
  59.5 58.6 %slice-start.2 = ((s8[11520000]{0:T(1024)(128)(4,1)}), s8[3131392]{0:T(1024)(128)(4,1)S(1)}, s32[]{:S(2)}) async-start(s8[11520000]{0:T(1024)(128)(4,1)} %bitcast.8), calls=%async_computation.2 | async-start | bytes 6262784
  61.7 11.7 %collective-permute-start.37 = (bf16[408,600]{1,0:T(8,128)(2,1)S(1)}, bf16[408,600]{1,0:T(8,128)(2,1)S(1)}, u32[]{:S(2)}, u32[]{:S(2)}) collective-permute-start(bf16[408,600]{1,0:T(8,128)(2,1)S(1)} %get-tuple-element.49), channel_id=1, source_target_pairs={{8,0},{9,1},{10,2},{11,3},{12,4},{13,5},{14,6},{15,7},{0,8},{1,9},... | collective-permute-start | bytes 1468808 | tf_op jit(solution)/shard_map/ppermute | solution.py:61
  61.8 18.1 %collective-permute-start.34 = (bf16[408,600]{1,0:T(8,128)(2,1)S(1)}, bf16[408,600]{1,0:T(8,128)(2,1)S(1)}, u32[]{:S(2)}, u32[]{:S(2)}) collective-permute-start(bf16[408,600]{1,0:T(8,128)(2,1)S(1)} %get-tuple-element.45.refs_2_), channel_id=1, source_target_pairs={{48,0},{49,1},{50,2},{51,3},{52,4},{53,5},{54,6},{55,7},{56,8},{57... | collective-permute-start | bytes 1468808 | tf_op jit(solution)/shard_map/ppermute | solution.py:61
  66.6 22.3 %collective-permute-start.30 = (bf16[408,600]{1,0:T(8,128)(2,1)S(1)}, bf16[408,600]{1,0:T(8,128)(2,1)S(1)}, u32[]{:S(2)}, u32[]{:S(2)}) collective-permute-start(bf16[408,600]{1,0:T(8,128)(2,1)S(1)} %get-tuple-element.46.refs_3_), channel_id=1, source_target_pairs={{16,0},{17,1},{18,2},{19,3},{20,4},{21,5},{22,6},{23,7},{24,8},{25... | collective-permute-start | bytes 1468808 | tf_op jit(solution)/shard_map/ppermute | solution.py:61
  70.1 18.8 %collective-permute-start.12 = (bf16[408,600]{1,0:T(8,128)(2,1)S(1)}, bf16[408,600]{1,0:T(8,128)(2,1)S(1)}, u32[]{:S(2)}, u32[]{:S(2)}) collective-permute-start(bf16[408,600]{1,0:T(8,128)(2,1)S(1)} %get-tuple-element.43), channel_id=1, source_target_pairs={{64,0},{65,1},{66,2},{67,3},{68,4},{69,5},{70,6},{71,7},{72,8},{73... | collective-permute-start | bytes 1468808 | tf_op jit(solution)/shard_map/ppermute | solution.py:61
  73.4 19.0 %collective-permute-start.13 = (bf16[408,600]{1,0:T(8,128)(2,1)S(1)}, bf16[408,600]{1,0:T(8,128)(2,1)S(1)}, u32[]{:S(2)}, u32[]{:S(2)}) collective-permute-start(bf16[408,600]{1,0:T(8,128)(2,1)S(1)} %get-tuple-element.44), channel_id=1, source_target_pairs={{64,0},{65,1},{66,2},{67,3},{68,4},{69,5},{70,6},{71,7},{72,8},{73... | collective-permute-start | bytes 1468808 | tf_op jit(solution)/shard_map/ppermute | solution.py:61
  73.4 18.9 %collective-permute-start.21 = (bf16[408,600]{1,0:T(8,128)(2,1)S(1)}, bf16[408,600]{1,0:T(8,128)(2,1)S(1)}, u32[]{:S(2)}, u32[]{:S(2)}) collective-permute-start(bf16[408,600]{1,0:T(8,128)(2,1)S(1)} %get-tuple-element.48), channel_id=1, source_target_pairs={{32,0},{33,1},{34,2},{35,3},{36,4},{37,5},{38,6},{39,7},{40,8},{41... | collective-permute-start | bytes 1468808 | tf_op jit(solution)/shard_map/ppermute | solution.py:61
  80.0 12.9 %collective-permute-start.25 = (bf16[400,600]{1,0:T(8,128)(2,1)S(1)}, bf16[400,600]{1,0:T(8,128)(2,1)S(1)}, u32[]{:S(2)}, u32[]{:S(2)}) collective-permute-start(bf16[400,600]{1,0:T(8,128)(2,1)S(1)} %collective-permute-done.16.refs_0_), channel_id=1, source_target_pairs={{8,0},{9,1},{10,2},{11,3},{12,4},{13,5},{14,6},{15,7},{0,8},{1,9},... | collective-permute-start | bytes 1440008 | tf_op jit(solution)/shard_map/ppermute | solution.py:61
  88.9 13.2 %collective-permute-start.2 = (bf16[400,600]{1,0:T(8,128)(2,1)S(1)}, bf16[400,600]{1,0:T(8,128)(2,1)S(1)}, u32[]{:S(2)}, u32[]{:S(2)}) collective-permute-start(bf16[400,600]{1,0:T(8,128)(2,1)S(1)} %collective-permute-done.1.refs_0_.refs_1_), channel_id=1, source_target_pairs={{1,0},{0,1},{3,2},{2,3},{5,4},{4,5},{7,6},{6,7},{9,8},{8,9},{11,10... | collective-permute-start | bytes 1440008 | tf_op jit(solution)/shard_map/ppermute | solution.py:61
  88.9 15.2 %collective-permute-start.4 = (bf16[400,600]{1,0:T(8,128)(2,1)S(1)}, bf16[400,600]{1,0:T(8,128)(2,1)S(1)}, u32[]{:S(2)}, u32[]{:S(2)}) collective-permute-start(bf16[400,600]{1,0:T(8,128)(2,1)S(1)} %collective-permute-done.1.refs_0_.refs_1_), channel_id=1, source_target_pairs={{8,0},{9,1},{10,2},{11,3},{12,4},{13,5},{14,6},{15,7},{0,8},{1,9},... | collective-permute-start | bytes 1440008 | tf_op jit(solution)/shard_map/ppermute | solution.py:61
  92.3 20.7 %collective-permute-start.17 = (bf16[400,600]{1,0:T(8,128)(2,1)S(1)}, bf16[400,600]{1,0:T(8,128)(2,1)S(1)}, u32[]{:S(2)}, u32[]{:S(2)}) collective-permute-start(bf16[400,600]{1,0:T(8,128)(2,1)S(1)} %collective-permute-done.16.refs_0_), channel_id=1, source_target_pairs={{1,0},{0,1},{3,2},{2,3},{5,4},{4,5},{7,6},{6,7},{9,8},{8,9},{11,10... | collective-permute-start | bytes 1440008 | tf_op jit(solution)/shard_map/ppermute | solution.py:61
  92.3 21.3 %collective-permute-start.35 = (bf16[408,600]{1,0:T(8,128)(2,1)S(1)}, bf16[408,600]{1,0:T(8,128)(2,1)S(1)}, u32[]{:S(2)}, u32[]{:S(2)}) collective-permute-start(bf16[408,600]{1,0:T(8,128)(2,1)S(1)} %collective-permute-done.34.refs_1_), channel_id=1, source_target_pairs={{8,0},{9,1},{10,2},{11,3},{12,4},{13,5},{14,6},{15,7},{0,8},{1,9},... | collective-permute-start | bytes 1468808 | tf_op jit(solution)/shard_map/ppermute | solution.py:61
  92.9 24.8 %collective-permute-start.26 = (bf16[408,600]{1,0:T(8,128)(2,1)S(1)}, bf16[408,600]{1,0:T(8,128)(2,1)S(1)}, u32[]{:S(2)}, u32[]{:S(2)}) collective-permute-start(bf16[408,600]{1,0:T(8,128)(2,1)S(1)} %collective-permute-done.12.one_ref), channel_id=1, source_target_pairs={{48,0},{17,1},{50,2},{19,3},{52,4},{21,5},{54,6},{23,7},{24,8},{57... | collective-permute-start | bytes 1468808 | tf_op jit(solution)/shard_map/ppermute | solution.py:61
  102.0 24.9 %collective-permute-start.31 = (bf16[408,600]{1,0:T(8,128)(2,1)S(1)}, bf16[408,600]{1,0:T(8,128)(2,1)S(1)}, u32[]{:S(2)}, u32[]{:S(2)}) collective-permute-start(bf16[408,600]{1,0:T(8,128)(2,1)S(1)} %collective-permute-done.30.refs_1_), channel_id=1, source_target_pairs={{8,0},{9,1},{10,2},{11,3},{12,4},{13,5},{14,6},{15,7},{0,8},{1,9},... | collective-permute-start | bytes 1468808 | tf_op jit(solution)/shard_map/ppermute | solution.py:61
  104.0 24.9 %collective-permute-start.24 = (bf16[408,600]{1,0:T(8,128)(2,1)S(1)}, bf16[408,600]{1,0:T(8,128)(2,1)S(1)}, u32[]{:S(2)}, u32[]{:S(2)}) collective-permute-start(bf16[408,600]{1,0:T(8,128)(2,1)S(1)} %shard_map.75.refs_1_), channel_id=1, source_target_pairs={{8,0},{9,1},{10,2},{11,3},{12,4},{13,5},{14,6},{15,7},{0,8},{1,9},... | collective-permute-start | bytes 1468808 | tf_op jit(solution)/shard_map/ppermute | solution.py:61
  113.0 18.2 %collective-permute-start.19 = (bf16[408,600]{1,0:T(8,128)(2,1)S(1)}, bf16[408,600]{1,0:T(8,128)(2,1)S(1)}, u32[]{:S(2)}, u32[]{:S(2)}) collective-permute-start(bf16[408,600]{1,0:T(8,128)(2,1)S(1)} %collective-permute-done.13.two_ref), channel_id=1, source_target_pairs={{16,0},{49,1},{18,2},{51,3},{20,4},{53,5},{22,6},{55,7},{56,8},{25... | collective-permute-start | bytes 1468808 | tf_op jit(solution)/shard_map/ppermute | solution.py:61
  113.6 23.0 %collective-permute-start.14 = (bf16[408,600]{1,0:T(8,128)(2,1)S(1)}, bf16[408,600]{1,0:T(8,128)(2,1)S(1)}, u32[]{:S(2)}, u32[]{:S(2)}) collective-permute-start(bf16[408,600]{1,0:T(8,128)(2,1)S(1)} %shard_map.73), channel_id=1, source_target_pairs={{32,0},{33,1},{34,2},{35,3},{36,4},{37,5},{38,6},{39,7},{40,8},{41... | collective-permute-start | bytes 1468808 | tf_op jit(solution)/shard_map/ppermute | solution.py:61
  117.7 20.8 %collective-permute-start.27 = (bf16[408,600]{1,0:T(8,128)(2,1)S(1)}, bf16[408,600]{1,0:T(8,128)(2,1)S(1)}, u32[]{:S(2)}, u32[]{:S(2)}) collective-permute-start(bf16[408,600]{1,0:T(8,128)(2,1)S(1)} %collective-permute-done.26.refs_1_), channel_id=1, source_target_pairs={{8,0},{9,1},{10,2},{11,3},{12,4},{13,5},{14,6},{15,7},{0,8},{1,9},... | collective-permute-start | bytes 1468808 | tf_op jit(solution)/shard_map/ppermute | solution.py:61
  126.9 23.6 %collective-permute-start.22 = (bf16[408,600]{1,0:T(8,128)(2,1)S(1)}, bf16[408,600]{1,0:T(8,128)(2,1)S(1)}, u32[]{:S(2)}, u32[]{:S(2)}) collective-permute-start(bf16[408,600]{1,0:T(8,128)(2,1)S(1)} %collective-permute-done.21.refs_2_), channel_id=1, source_target_pairs={{8,0},{9,1},{10,2},{11,3},{12,4},{13,5},{14,6},{15,7},{0,8},{1,9},... | collective-permute-start | bytes 1468808 | tf_op jit(solution)/shard_map/ppermute | solution.py:61
  129.0 21.5 %collective-permute-start.3 = (bf16[400,600]{1,0:T(8,128)(2,1)S(1)}, bf16[400,600]{1,0:T(8,128)(2,1)S(1)}, u32[]{:S(2)}, u32[]{:S(2)}) collective-permute-start(bf16[400,600]{1,0:T(8,128)(2,1)S(1)} %collective-permute-done.2.refs_1_.refs_0_), channel_id=1, source_target_pairs={{8,0},{9,1},{10,2},{11,3},{12,4},{13,5},{14,6},{15,7},{0,8},{1,9},... | collective-permute-start | bytes 1440008 | tf_op jit(solution)/shard_map/ppermute | solution.py:61
  131.2 23.0 %collective-permute-start.20 = (bf16[408,600]{1,0:T(8,128)(2,1)S(1)}, bf16[408,600]{1,0:T(8,128)(2,1)S(1)}, u32[]{:S(2)}, u32[]{:S(2)}) collective-permute-start(bf16[408,600]{1,0:T(8,128)(2,1)S(1)} %collective-permute-done.19.refs_1_), channel_id=1, source_target_pairs={{8,0},{9,1},{10,2},{11,3},{12,4},{13,5},{14,6},{15,7},{0,8},{1,9},... | collective-permute-start | bytes 1468808 | tf_op jit(solution)/shard_map/ppermute | solution.py:61
  136.6 17.6 %collective-permute-start.18 = (bf16[400,600]{1,0:T(8,128)(2,1)S(1)}, bf16[400,600]{1,0:T(8,128)(2,1)S(1)}, u32[]{:S(2)}, u32[]{:S(2)}) collective-permute-start(bf16[400,600]{1,0:T(8,128)(2,1)S(1)} %collective-permute-done.17.refs_0_), channel_id=1, source_target_pairs={{8,0},{9,1},{10,2},{11,3},{12,4},{13,5},{14,6},{15,7},{0,8},{1,9},... | collective-permute-start | bytes 1440008 | tf_op jit(solution)/shard_map/ppermute | solution.py:61
  138.6 19.4 %collective-permute-start.15 = (bf16[408,600]{1,0:T(8,128)(2,1)S(1)}, bf16[408,600]{1,0:T(8,128)(2,1)S(1)}, u32[]{:S(2)}, u32[]{:S(2)}) collective-permute-start(bf16[408,600]{1,0:T(8,128)(2,1)S(1)} %collective-permute-done.14.refs_2_), channel_id=1, source_target_pairs={{8,0},{9,1},{10,2},{11,3},{12,4},{13,5},{14,6},{15,7},{0,8},{1,9},... | collective-permute-start | bytes 1468808 | tf_op jit(solution)/shard_map/ppermute | solution.py:61
  160.5 1.2 collective-permute-start.38
  161.6 4.0 %collective-permute-start.39 = (f32[8,128]{1,0:T(8,128)S(1)}, f32[8,128]{1,0:T(8,128)S(1)}, u32[]{:S(2)}, u32[]{:S(2)}) collective-permute-start(f32[8,128]{1,0:T(8,128)S(1)} %add.15), channel_id=1, source_target_pairs={{32,0},{33,1},{34,2},{35,3},{36,4},{37,5},{38,6},{39,7},{40,8},{41... | collective-permute-start | bytes 12296 | tf_op jit(solution)/shard_map/ppermute | solution.py:61
  161.6 5.0 %collective-permute-start.40 = (f32[8,128]{1,0:T(8,128)S(1)}, f32[8,128]{1,0:T(8,128)S(1)}, u32[]{:S(2)}, u32[]{:S(2)}) collective-permute-start(f32[8,128]{1,0:T(8,128)S(1)} %add.15), channel_id=1, source_target_pairs={{16,0},{17,1},{18,2},{19,3},{20,4},{21,5},{22,6},{23,7},{24,8},{25... | collective-permute-start | bytes 12296 | tf_op jit(solution)/shard_map/ppermute | solution.py:61
  165.1 3.7 %collective-permute-start.41 = (f32[8,128]{1,0:T(8,128)S(1)}, f32[8,128]{1,0:T(8,128)S(1)}, u32[]{:S(2)}, u32[]{:S(2)}) collective-permute-start(f32[8,128]{1,0:T(8,128)S(1)} %add.15), channel_id=1, source_target_pairs={{48,0},{49,1},{50,2},{51,3},{52,4},{53,5},{54,6},{55,7},{56,8},{57... | collective-permute-start | bytes 12296 | tf_op jit(solution)/shard_map/ppermute | solution.py:61
  168.7 4.2 %collective-permute-start.42 = (f32[8,128]{1,0:T(8,128)S(1)}, f32[8,128]{1,0:T(8,128)S(1)}, u32[]{:S(2)}, u32[]{:S(2)}) collective-permute-start(f32[8,128]{1,0:T(8,128)S(1)} %add_add_fusion), channel_id=1, source_target_pairs={{64,0},{65,1},{66,2},{67,3},{68,4},{69,5},{70,6},{71,7},{72,8},{73... | collective-permute-start | bytes 12296 | tf_op jit(solution)/shard_map/ppermute | solution.py:61

commit v2 on v1

--- a/solution.py
+++ b/solution.py
@@ -28,14 +28,10 @@
     return pl.BlockSpec(memory_space=pltpu.VMEM)
 
 
-def scalars():
-    return pl.BlockSpec(memory_space=pltpu.SMEM)
-
-
 def call(body, shapes, operands, mib, flops=0, **more):
     return pl.pallas_call(
         body,
-        in_specs=[scalars()] + [whole()] * (len(operands) - 1),
+        in_specs=[whole()] * len(operands),
         out_specs=jax.tree.map(lambda _: whole(), shapes),
         out_shape=shapes,
         cost_estimate=pl.CostEstimate(flops=flops, bytes_accessed=flops // 300, transcendentals=0),
@@ -76,9 +72,18 @@
     return from_device(block, source)
 
 
-def place(ids_ref):
-    here = ids_ref[0]
-    return here >> 3, (here >> 1) & 3, here & 1, ids_ref[1] & 3
+def onward(block, step, columns):
+    route = []
+    for a in range(PLANES):
+        for x in columns:
+            for c in range(CORES):
+                route.append((pts_id(a, x - step, c), pts_id(a, x, c)))
+    return lax.ppermute(block, AXES[0], route)
+
+
+def place():
+    here = lax.axis_index(AXES[0])
+    return here >> 3, (here >> 1) & 3, here & 1, lax.axis_index(AXES[1]) & 3
 
 
 def takes(slot, a, x, c, odd):
@@ -122,9 +127,9 @@
     )(array)
 
 
-def pick(ids, takes_second, one, two):
-    def body(ids_ref, one_ref, two_ref, o_ref):
-        second = takes_second(*place(ids_ref))
+def pick(takes_second, one, two):
+    def body(one_ref, two_ref, o_ref):
+        second = takes_second(*place())
 
         @pl.when(second == 0)
         def _():
@@ -134,29 +139,30 @@
         def _():
             o_ref[...] = two_ref[...]
 
-    return call(body, jax.ShapeDtypeStruct(one.shape, one.dtype), [ids, one, two], 4)
-
-
-def group_block(ids_ref, key):
-    zlo, y = ids_ref[1] >> 2, ids_ref[1] & 3
+    return call(body, jax.ShapeDtypeStruct(one.shape, one.dtype), [one, two], 4)
+
+
+def group_block(key):
+    group = lax.axis_index(AXES[1])
+    zlo, y = group >> 2, group & 3
     return ((zlo + key[0]) & (ZLO - 1)) * YS + ((y + key[1]) & (YS - 1))
 
 
-def theta_part(ids, green_cut, blocks, so_far=None, occ_t=None):
+def theta_part(green_cut, blocks, so_far=None, occ_t=None):
     keys = list(blocks)
     n = len(keys)
     rows = green_cut.shape[1]
     pts = blocks[keys[0]].shape[1]
     flops = 2 * rows * pts * green_cut.shape[2] * n
-    operands = [ids, green_cut, *blocks.values()]
+    operands = [green_cut, *blocks.values()]
     if so_far is not None:
         operands.append(so_far)
 
     if occ_t is None:
 
-        def part(ids_ref, g_ref, *refs):
+        def part(g_ref, *refs):
             cs, o_ref = refs[:n], refs[-1]
-            at = [group_block(ids_ref, key) for key in keys]
+            at = [group_block(key) for key in keys]
 
             @pl.loop(0, 2)
             def _(half):
@@ -171,10 +177,10 @@
 
     elec = occ_t.shape[0]
 
-    def last(ids_ref, g_ref, *refs):
+    def last(g_ref, *refs):
         cs = refs[:n]
         acc_ref, occ_ref, t0_ref, t1_ref, *pick_refs, dens_ref = refs[n:]
-        at = [group_block(ids_ref, key) for key in keys]
+        at = [group_block(key) for key in keys]
         th_refs = (t0_ref, t1_ref)
         occ = occ_ref[...].astype(F32)
         dens = []
@@ -193,12 +199,11 @@
         tail = jnp.where(row == 0, dens[0], jnp.where(row == 1, dens[1], 0.0)).astype(BF16)
         for w in range(2):
             th_refs[w][elec : elec + EXTRA, :] = tail
-        a, x, c, y = place(ids_ref)
+        a, x, c, y = place()
         odd = (y ^ c) & 1
         goes = (
             odd,
             1 - odd,
-            takes(FAR, a, x + 2, c, odd),
             takes(OWN, a, x, 1 - c, odd),
         )
         for w, o_ref in zip(goes, pick_refs):
@@ -212,11 +217,11 @@
                 o_ref[...] = t1_ref[...]
 
     slab = jax.ShapeDtypeStruct((elec + EXTRA, pts), BF16)
-    shapes = [slab] * 6 + [jax.ShapeDtypeStruct((2, pts), F32)]
+    shapes = [slab] * 5 + [jax.ShapeDtypeStruct((2, pts), F32)]
     return call(last, shapes, operands + [occ_t], 8, flops)
 
 
-def exchange(jobs, ids, own, kernel_cut, acc=None, density=None):
+def exchange(jobs, own, kernel_cut, acc=None, density=None):
     n = len(jobs)
     elec, pts = jobs[0][3][0].shape
     contract_last = (((1,), (1,)), ((), ()))
@@ -224,9 +229,9 @@
     n_occ = len(occ_blocks)
     first = acc is None
 
-    def body(ids_ref, k_ref, *refs):
+    def body(k_ref, *refs):
         os, ts, refs = refs[:n_occ], refs[n_occ : n_occ + n], refs[n_occ + n :]
-        a, x, c, y = place(ids_ref)
+        a, x, c, y = place()
         if first:
             ex_ref, pot_ref, own_ref, flip_ref = refs
             ex_ref[...] = jnp.zeros_like(ex_ref)
@@ -267,7 +272,7 @@
             vals_out[...] = vals
 
     shapes = [jax.ShapeDtypeStruct((2, 8, pts), F32), jax.ShapeDtypeStruct((EXTRA, pts), F32)]
-    operands = [ids, kernel_cut] + occ_blocks + [job[4] for job in jobs]
+    operands = [kernel_cut] + occ_blocks + [job[4] for job in jobs]
     scratch, alias = [], {}
     if first:
         shapes += [jax.ShapeDtypeStruct((3, pts, elec), BF16)]
@@ -294,7 +299,6 @@
 
 def local(green_half, collocation, occupied, kernel):
     walkers, elec, orb = green_half.shape
-    ids = jnp.stack([lax.axis_index(axis) for axis in AXES]).astype(jnp.int32)
     occ_t = occupied.T
 
     coll = {(0, 0): collocation}
@@ -308,7 +312,7 @@
     occ_right = from_column(occ_t, RIGHT)
     occ_plane = from_chip(occ_t, 1, 0)
     occ_side = from_column(occ_plane, SIDE)
-    occ_pick = pick(ids, lambda a, x, c, y: (y ^ c) & 1, occ_t, occ_plane)
+    occ_pick = pick(lambda a, x, c, y: (y ^ c) & 1, occ_t, occ_plane)
     occ_far = from_column(occ_pick, FAR)
 
     def from_y(block):
@@ -326,19 +330,30 @@
     def some(keys):
         return {k: coll[k] for k in keys}
 
-    so_far = theta_part(ids, green_cut, some([(0, 0), (1, 0), (0, 2)]))
-    middle = some([(0, 1), (0, 3), (1, 1), (1, 3)])
-    so_far = theta_part(ids, green_cut, middle, so_far)
-    t0, t1, t_first, t_second, t_far, t_sib, density = theta_part(
-        ids, green_cut, some([(1, 2)]), so_far, occ_t
-    )
+    so_far = theta_part(green_cut, some([(0, 0), (1, 0), (0, 2)]))
+    so_far = theta_part(green_cut, some([(0, 1), (0, 3)]), so_far)
+    so_far = theta_part(green_cut, some([(1, 1), (1, 3)]), so_far)
+    t0, t1, t_first, t_second, t_sib, density = theta_part(green_cut, some([(1, 2)]), so_far, occ_t)
     first = from_chip(t_first, 1, 0)
     second = from_chip(t_second, 1, 0)
-    plane = pick(ids, lambda a, x, c, y: a ^ (y ^ c) & 1, first, second)
-    far2 = pick(ids, lambda a, x, c, y: x >> 1 ^ (y ^ c) & 1, first, second)
-    sends = {LEFT: t0, RIGHT: t1, FAR: t_far, SIDE: first, SIDE2: second, FAR2: far2}
-    theta = {slot: from_column(sends[slot], slot) for slot in sends}
-    theta |= {OWN: t_sib, PLANE: plane}
+    theta = {OWN: t_sib}
+    sends = {LEFT: t0, RIGHT: t1, SIDE: first, SIDE2: second}
+    for slot, block in sends.items():
+        theta[slot] = from_column(block, slot)
+    theta[PLANE] = pick(lambda a, x, c, y: a ^ (y ^ c) & 1, first, second)
+
+    def right_half(a, x, c, y):
+        return x >> 1
+
+    right = onward(theta[LEFT], 1, (0, 1))
+    left = onward(theta[RIGHT], -1, (2, 3))
+    theta[FAR] = pick(right_half, right, left)
+    side, side2 = theta[SIDE], theta[SIDE2]
+    walker0 = pick(lambda a, x, c, y: (y ^ c) & 1, side, side2)
+    walker1 = pick(lambda a, x, c, y: (y ^ c) & 1, side2, side)
+    right = onward(walker0, 1, (2, 3))
+    left = onward(walker1, -1, (0, 1))
+    theta[FAR2] = pick(right_half, left, right)
     theta_sib = {slot: from_chip(theta[slot], 0, 0, 1) for slot in theta}
     occ_sib = {slot: [from_chip(occ[slot][0], 0, 0, 1)] for slot in occ}
     occ_sib[FAR] += [from_chip(occ_far2, 0, 0, 1)]
@@ -346,15 +361,15 @@
         known[FAR2] = known[FAR][::-1]
 
     own_jobs = [(OWN, 0, w, [occ_t], t, 1.0, w == 0) for w, t in enumerate((t0, t1))]
-    *acc, own = exchange(own_jobs, ids, None, kernel_cut)
+    *acc, own = exchange(own_jobs, None, kernel_cut)
 
     for slot in (OWN, *SLOTS):
         if slot != OWN:
             same = (slot, 0, None, occ[slot], theta[slot], 2.0, True)
-            acc = exchange([same], ids, own, kernel_cut, acc)
+            acc = exchange([same], own, kernel_cut, acc)
         sib = (slot, 1, None, occ_sib[slot], theta_sib[slot], 2.0, True)
         ending = density if slot == FAR2 else None
-        acc = exchange([sib], ids, own, kernel_cut, acc, ending)
+        acc = exchange([sib], own, kernel_cut, acc, ending)
     _, _, potential, energies = acc
     energies = everyone_total(energies)
     return potential, energies[0, :walkers], energies[0, walkers : 2 * walkers]

time: 175 us -> 163 us (0.931)
  Pallas kernels: 51.9 us -> 38.6 us
  starting transfers between devices: 58.9 us -> 66.4 us
  waiting for transfers between devices: 58.2 us -> 52.5 us
    pallas_call x22 -> x26, Pallas kernels: 42.7 us -> 29.4 us  [call(): pl.pallas_call(body, in_specs=[whole()] * len(operands), out_specs=jax.tr...]
    ppermute x43 -> x41, waiting for transfers between devices: 58.2 us -> 47.1 us  [from_device(): return lax.ppermute(block, AXES, route)]
    ppermute x0 -> x4, starting transfers between devices: none -> 5.48 us  [onward(): return lax.ppermute(block, AXES[0], route)]
    ppermute x0 -> x4, waiting for transfers between devices: none -> 5.42 us  [onward(): return lax.ppermute(block, AXES[0], route)]
    ppermute x43 -> x41, starting transfers between devices: 58.9 us -> 61 us  [from_device(): return lax.ppermute(block, AXES, route)]
  transfers between devices with their start and end apart: 43 -> 45, of which waited for: 14 -> 15; matrix products, arithmetic and copies ran while one was open for 0% -> 0% of each run, Pallas kernels for 28% -> 23%
where the time goes in v2:
time: 163 us; the launch traced here: 161 us
  starting transfers between devices  66.4 us (41%)
  waiting for transfers between devices  52.5 us (32%)
  Pallas kernels  38.6 us (24%)
  local copies, waits for them, and re-layouts  2.71 us (2%)
    ppermute x41, starting transfers between devices, from_device(): return lax.ppermute(block, AXES, route)  61 us
    ppermute x41, waiting for transfers between devices, from_device(): return lax.ppermute(block, AXES, route)  47.1 us
    pallas_call x26, Pallas kernels, call(): pl.pallas_call(body, in_specs=[whole()] * len(operands), out_specs=jax.tr...  29.4 us
    pallas_call x2, Pallas kernels, split_columns(): pl.pallas_call(body, grid=(steps,), in_specs=[pl.BlockSpec((tile, cols),...  9.18 us
    ppermute x4, starting transfers between devices, onward(): return lax.ppermute(block, AXES[0], route)  5.48 us
    ppermute x4, waiting for transfers between devices, onward(): return lax.ppermute(block, AXES[0], route)  5.42 us
  transfers between devices with their start and end apart: 45, of which 15 were waited for; matrix products, arithmetic and copies ran while one was open for 0% of the time, Pallas kernels for 23%

profile of v2, /device:TPU:1, one launch (start us, length us, event | category | flops | bytes accessed | tf_op | source)
XLA Modules:
  0.0 161.2 jit_solution(4874277703345440627)
XLA Ops:
  0.6 2.5 %collective-permute-start.7 = (bf16[300,600]{1,0:T(8,128)(2,1)}, bf16[300,600]{1,0:T(8,128)(2,1)S(1)}, u32[]{:S(2)}, u32[]{:S(2)}) collective-permute-start(bf16[300,600]{1,0:T(8,128)(2,1)} %refs_0_.1), channel_id=1, source_target_pairs={{4,0},{5,1},{6,2},{7,3},{0,4},{1,5},{2,6},{3,7},{12,8},{13,9},{14,... | collective-permute-start | bytes 1080008 | tf_op jit(solution)/shard_map/ppermute | solution.py:57
  3.2 2.9 %collective-permute-start.5 = (bf16[300,600]{1,0:T(8,128)(2,1)}, bf16[300,600]{1,0:T(8,128)(2,1)S(1)}, u32[]{:S(2)}, u32[]{:S(2)}) collective-permute-start(bf16[300,600]{1,0:T(8,128)(2,1)} %refs_0_.1), channel_id=1, source_target_pairs={{2,0},{3,1},{0,2},{1,3},{6,4},{7,5},{4,6},{5,7},{10,8},{11,9},{8,1... | collective-permute-start | bytes 1080008 | tf_op jit(solution)/shard_map/ppermute | solution.py:57
  6.9 1.5 collective-permute-start.38
  9.1 3.0 %collective-permute-done.7.refs_1_ = bf16[300,600]{1,0:T(8,128)(2,1)S(1)} collective-permute-done((bf16[300,600]{1,0:T(8,128)(2,1)}, bf16[300,600]{1,0:T(8,128)(2,1)S(1)}, u32[]{:S(2)}, u32[]{:S(2)}) %collective-permute-start.7) | collective-permute-done | bytes 360032 | tf_op jit(solution)/shard_map/ppermute | solution.py:57
  12.1 1.1 collective-permute-start.35
  13.2 1.4 collective-permute-done.5.refs_2_
  14.6 2.5 %collective-permute-start.32 = (bf16[400,600]{1,0:T(8,128)(2,1)}, bf16[400,600]{1,0:T(8,128)(2,1)S(1)}, u32[]{:S(2)}, u32[]{:S(2)}) collective-permute-start(bf16[400,600]{1,0:T(8,128)(2,1)} %bitcast.10), channel_id=1, source_target_pairs={{16,0},{17,1},{18,2},{19,3},{20,4},{21,5},{22,6},{23,7},{24,8},{25... | collective-permute-start | bytes 1440008 | tf_op jit(solution)/shard_map/ppermute | solution.py:57
  17.1 6.5 %collective-permute-done.10.refs_0_ = bf16[300,600]{1,0:T(8,128)(2,1)S(1)} collective-permute-done((bf16[300,600]{1,0:T(8,128)(2,1)}, bf16[300,600]{1,0:T(8,128)(2,1)S(1)}, u32[]{:S(2)}, u32[]{:S(2)}) %collective-permute-start.10) | collective-permute-done | bytes 360032 | tf_op jit(solution)/shard_map/ppermute | solution.py:57
  23.6 3.3 %collective-permute-start = (bf16[400,600]{1,0:T(8,128)(2,1)}, bf16[400,600]{1,0:T(8,128)(2,1)S(1)}, u32[]{:S(2)}, u32[]{:S(2)}) collective-permute-start(bf16[400,600]{1,0:T(8,128)(2,1)} %bitcast.11), channel_id=1, source_target_pairs={{64,0},{65,1},{66,2},{67,3},{68,4},{69,5},{70,6},{71,7},{72,8},{73... | collective-permute-start | bytes 1440008 | tf_op jit(solution)/shard_map/ppermute | solution.py:57
  26.9 3.3 %collective-permute-start.8 = (bf16[300,600]{1,0:T(8,128)(2,1)S(1)}, bf16[300,600]{1,0:T(8,128)(2,1)S(1)}, u32[]{:S(2)}, u32[]{:S(2)}) collective-permute-start(bf16[300,600]{1,0:T(8,128)(2,1)S(1)} %collective-permute-done.7.refs_1_), channel_id=1, source_target_pairs={{1,0},{2,1},{3,2},{0,3},{5,4},{6,5},{7,6},{4,7},{9,8},{10,9},{11,1... | collective-permute-start | bytes 1080008 | tf_op jit(solution)/shard_map/ppermute | solution.py:57
  30.2 1.1 collective-permute-start.36
  31.4 6.3 %collective-permute-done.two_ref.refs_0_ = bf16[400,600]{1,0:T(8,128)(2,1)S(1)} collective-permute-done((bf16[400,600]{1,0:T(8,128)(2,1)}, bf16[400,600]{1,0:T(8,128)(2,1)S(1)}, u32[]{:S(2)}, u32[]{:S(2)}) %collective-permute-start) | collective-permute-done | bytes 480032 | tf_op jit(solution)/shard_map/ppermute | solution.py:57
  37.7 3.7 %collective-permute-start.33 = (bf16[400,600]{1,0:T(8,128)(2,1)S(1)}, bf16[400,600]{1,0:T(8,128)(2,1)S(1)}, u32[]{:S(2)}, u32[]{:S(2)}) collective-permute-start(bf16[400,600]{1,0:T(8,128)(2,1)S(1)} %collective-permute-done.32.refs_0_), channel_id=1, source_target_pairs={{8,0},{9,1},{10,2},{11,3},{12,4},{13,5},{14,6},{15,7},{0,8},{1,9},... | collective-permute-start | bytes 1440008 | tf_op jit(solution)/shard_map/ppermute | solution.py:57
  41.4 2.5 %collective-permute-start.19 = (bf16[400,600]{1,0:T(8,128)(2,1)S(1)}, bf16[400,600]{1,0:T(8,128)(2,1)S(1)}, u32[]{:S(2)}, u32[]{:S(2)}) collective-permute-start(bf16[400,600]{1,0:T(8,128)(2,1)S(1)} %collective-permute-done.two_ref.refs_0_), channel_id=1, source_target_pairs={{48,0},{17,1},{50,2},{19,3},{52,4},{21,5},{54,6},{23,7},{24,8},{57... | collective-permute-start | bytes 1440008 | tf_op jit(solution)/shard_map/ppermute | solution.py:57
  43.8 2.1 %copy-done.1 = bf16[2,400,2400]{2,1,0:T(8,128)(2,1)S(1)} copy-done((bf16[2,400,2400]{2,1,0:T(8,128)(2,1)S(1)}, bf16[2,400,2400]{2,1,0:T(8,128)(2,1)}, u32[]{:S(2)}) %copy-start.1) | copy-done | bytes 3840024
  45.9 3.4 %shard_map.69.g_ref = bf16[8,800,300]{2,1,0:T(8,128)(2,1)S(1)} custom-call(bf16[800,2400]{1,0:T(8,128)(2,1)S(1)} %bitcast.16), custom_call_target="tpu_custom_call" | custom-call | tf_op jit(solution)/shard_map/pallas_call | solution.py:120
  49.4 2.2 %shard_map.70.refs_2_ = f32[800,600]{1,0:T(8,128)S(1)} custom-call(bf16[8,800,300]{2,1,0:T(8,128)(2,1)S(1)} %shard_map.69.g_ref, bf16[300,600]{1,0:T(8,128)(2,1)S(1)} %copy-done.2, bf16[300,600]{1,0:T(8,128)(2,1)S(1)} %collective-permute-done.7.refs_1_, bf16[300,600]{1,0:T(8,128)(2,1)S(1)} %collective-permute-done.5.refs_2_), custom_call_target="tpu_custom_call" | custom-call | flops 864000000 | bytes 2880000 | tf_op jit(solution)/shard_map/pallas_call | solution.py:32
  51.6 1.6 %shard_map.71.refs_2_ = f32[800,600]{1,0:T(8,128)S(1)} custom-call(bf16[8,800,300]{2,1,0:T(8,128)(2,1)S(1)} %shard_map.69.g_ref, bf16[300,600]{1,0:T(8,128)(2,1)S(1)} %collective-permute-done.10.refs_0_, bf16[300,600]{1,0:T(8,128)(2,1)S(1)} %collective-permute-done.11.refs_1_, f32[800,600]{1,0:T(8,128)S(1)} %shard_map.70.refs_2_), custom_call_target="tpu_custom_call" | custom-call | flops 576000000 | bytes 1920000 | tf_op jit(solution)/shard_map/pallas_call | solution.py:32
  53.3 1.8 %collective-permute-start.1 = (bf16[400,600]{1,0:T(8,128)(2,1)S(1)}, bf16[400,600]{1,0:T(8,128)(2,1)S(1)}, u32[]{:S(2)}, u32[]{:S(2)}) collective-permute-start(bf16[400,600]{1,0:T(8,128)(2,1)S(1)} %shard_map.68), channel_id=1, source_target_pairs={{32,0},{33,1},{34,2},{35,3},{36,4},{37,5},{38,6},{39,7},{40,8},{41... | collective-permute-start | bytes 1440008 | tf_op jit(solution)/shard_map/ppermute | solution.py:57
  55.2 1.6 shard_map.72.refs_1_
  56.8 1.0 shard_map.73
  58.5 2.4 %collective-permute-start.25 = (bf16[408,600]{1,0:T(8,128)(2,1)S(1)}, bf16[408,600]{1,0:T(8,128)(2,1)S(1)}, u32[]{:S(2)}, u32[]{:S(2)}) collective-permute-start(bf16[408,600]{1,0:T(8,128)(2,1)S(1)} %get-tuple-element.45.refs_3_), channel_id=1, source_target_pairs={{16,0},{17,1},{18,2},{19,3},{20,4},{21,5},{22,6},{23,7},{24,8},{25... | collective-permute-start | bytes 1468808 | tf_op jit(solution)/shard_map/ppermute | solution.py:57
  60.9 2.9 %collective-permute-start.14 = (bf16[408,600]{1,0:T(8,128)(2,1)S(1)}, bf16[408,600]{1,0:T(8,128)(2,1)S(1)}, u32[]{:S(2)}, u32[]{:S(2)}) collective-permute-start(bf16[408,600]{1,0:T(8,128)(2,1)S(1)} %get-tuple-element.43), channel_id=1, source_target_pairs={{64,0},{65,1},{66,2},{67,3},{68,4},{69,5},{70,6},{71,7},{72,8},{73... | collective-permute-start | bytes 1468808 | tf_op jit(solution)/shard_map/ppermute | solution.py:57
  63.8 3.9 %collective-permute-done.1.refs_0_.refs_1_ = bf16[400,600]{1,0:T(8,128)(2,1)S(1)} collective-permute-done((bf16[400,600]{1,0:T(8,128)(2,1)S(1)}, bf16[400,600]{1,0:T(8,128)(2,1)S(1)}, u32[]{:S(2)}, u32[]{:S(2)}) %collective-permute-start.1) | collective-permute-done | bytes 480032 | tf_op jit(solution)/shard_map/ppermute | solution.py:57
  67.7 3.2 %collective-permute-start.12 = (bf16[408,600]{1,0:T(8,128)(2,1)S(1)}, bf16[408,600]{1,0:T(8,128)(2,1)S(1)}, u32[]{:S(2)}, u32[]{:S(2)}) collective-permute-start(bf16[408,600]{1,0:T(8,128)(2,1)S(1)} %get-tuple-element.42), channel_id=1, source_target_pairs={{64,0},{65,1},{66,2},{67,3},{68,4},{69,5},{70,6},{71,7},{72,8},{73... | collective-permute-start | bytes 1468808 | tf_op jit(solution)/shard_map/ppermute | solution.py:57
  70.9 2.6 %collective-permute-start.30 = (bf16[400,600]{1,0:T(8,128)(2,1)S(1)}, bf16[400,600]{1,0:T(8,128)(2,1)S(1)}, u32[]{:S(2)}, u32[]{:S(2)}) collective-permute-start(bf16[400,600]{1,0:T(8,128)(2,1)S(1)} %collective-permute-done.19.refs_0_), channel_id=1, source_target_pairs={{8,0},{9,1},{10,2},{11,3},{12,4},{13,5},{14,6},{15,7},{0,8},{1,9},... | collective-permute-start | bytes 1440008 | tf_op jit(solution)/shard_map/ppermute | solution.py:57
  73.5 6.2 %collective-permute-done.23.refs_1_ = bf16[408,600]{1,0:T(8,128)(2,1)S(1)} collective-permute-done((bf16[408,600]{1,0:T(8,128)(2,1)S(1)}, bf16[408,600]{1,0:T(8,128)(2,1)S(1)}, u32[]{:S(2)}, u32[]{:S(2)}) %collective-permute-start.23) | collective-permute-done | bytes 489632 | tf_op jit(solution)/shard_map/ppermute | solution.py:57
  79.7 1.2 collective-permute-start.2
  81.9 4.3 %collective-permute-done.12.two_ref = bf16[408,600]{1,0:T(8,128)(2,1)S(1)} collective-permute-done((bf16[408,600]{1,0:T(8,128)(2,1)S(1)}, bf16[408,600]{1,0:T(8,128)(2,1)S(1)}, u32[]{:S(2)}, u32[]{:S(2)}) %collective-permute-start.12) | collective-permute-done | bytes 489632 | tf_op jit(solution)/shard_map/ppermute | solution.py:57
  86.6 1.1 collective-permute-start.13
  87.7 4.8 %collective-permute-done.2.refs_1_.refs_0_ = bf16[400,600]{1,0:T(8,128)(2,1)S(1)} collective-permute-done((bf16[400,600]{1,0:T(8,128)(2,1)S(1)}, bf16[400,600]{1,0:T(8,128)(2,1)S(1)}, u32[]{:S(2)}, u32[]{:S(2)}) %collective-permute-start.2) | collective-permute-done | bytes 480032 | tf_op jit(solution)/shard_map/ppermute | solution.py:57
  92.5 2.2 %collective-permute-start.37 = (bf16[408,600]{1,0:T(8,128)(2,1)S(1)}, bf16[408,600]{1,0:T(8,128)(2,1)S(1)}, u32[]{:S(2)}, u32[]{:S(2)}) collective-permute-start(bf16[408,600]{1,0:T(8,128)(2,1)S(1)} %collective-permute-done.23.refs_1_), channel_id=1, source_target_pairs={{8,0},{9,1},{10,2},{11,3},{12,4},{13,5},{14,6},{15,7},{0,8},{1,9},... | collective-permute-start | bytes 1468808 | tf_op jit(solution)/shard_map/ppermute | solution.py:57
  94.7 2.2 %collective-permute-start.24 = (bf16[408,600]{1,0:T(8,128)(2,1)S(1)}, bf16[408,600]{1,0:T(8,128)(2,1)S(1)}, u32[]{:S(2)}, u32[]{:S(2)}) collective-permute-start(bf16[408,600]{1,0:T(8,128)(2,1)S(1)} %collective-permute-done.23.refs_1_), channel_id=1, source_target_pairs={{48,0},{56,8},{0,16},{8,24},{112,64},{120,72},{64,80},{72,88},{49,... | collective-permute-start | bytes 1468808 | tf_op jit(solution)/shard_map/ppermute | solution.py:81
  96.9 6.5 %collective-permute-done.20.refs_0_ = bf16[400,600]{1,0:T(8,128)(2,1)S(1)} collective-permute-done((bf16[400,600]{1,0:T(8,128)(2,1)S(1)}, bf16[400,600]{1,0:T(8,128)(2,1)S(1)}, u32[]{:S(2)}, u32[]{:S(2)}) %collective-permute-start.20) | collective-permute-done | bytes 480032 | tf_op jit(solution)/shard_map/ppermute | solution.py:57
  103.5 1.3 collective-permute-start.26
  104.8 1.9 %collective-permute-start.34 = (bf16[408,600]{1,0:T(8,128)(2,1)S(1)}, bf16[408,600]{1,0:T(8,128)(2,1)S(1)}, u32[]{:S(2)}, u32[]{:S(2)}) collective-permute-start(bf16[408,600]{1,0:T(8,128)(2,1)S(1)} %collective-permute-done.25.refs_1_), channel_id=1, source_target_pairs={{8,0},{9,1},{10,2},{11,3},{12,4},{13,5},{14,6},{15,7},{0,8},{1,9},... | collective-permute-start | bytes 1468808 | tf_op jit(solution)/shard_map/ppermute | solution.py:57
  107.7 4.0 %collective-permute-done.24.one_ref = bf16[408,600]{1,0:T(8,128)(2,1)S(1)} collective-permute-done((bf16[408,600]{1,0:T(8,128)(2,1)S(1)}, bf16[408,600]{1,0:T(8,128)(2,1)S(1)}, u32[]{:S(2)}, u32[]{:S(2)}) %collective-permute-start.24) | collective-permute-done | bytes 489632 | tf_op jit(solution)/shard_map/ppermute | solution.py:81
  111.7 1.3 collective-permute-start.16
  113.0 1.4 collective-permute-done.26.two_ref
  114.4 2.4 %collective-permute-start.31 = (bf16[408,600]{1,0:T(8,128)(2,1)S(1)}, bf16[408,600]{1,0:T(8,128)(2,1)S(1)}, u32[]{:S(2)}, u32[]{:S(2)}) collective-permute-start(bf16[408,600]{1,0:T(8,128)(2,1)S(1)} %collective-permute-done.15.two_ref.one_ref.refs_1_), channel_id=1, source_target_pairs={{8,0},{9,1},{10,2},{11,3},{12,4},{13,5},{14,6},{15,7},{0,8},{1,9},... | collective-permute-start | bytes 1468808 | tf_op jit(solution)/shard_map/ppermute | solution.py:57
  116.8 5.8 %shard_map.67.k_ref = bf16[16,600,600]{2,1,0:T(8,128)(2,1)S(1)} custom-call(bf16[600,9600]{1,0:T(8,128)(2,1)S(1)} %bitcast.7), custom_call_target="tpu_custom_call" | custom-call | tf_op jit(solution)/shard_map/pallas_call | solution.py:120
  122.6 2.5 %shard_map.77 = (f32[2,8,600]{2,1,0:T(8,128)S(1)}, f32[8,600]{1,0:T(8,128)S(1)}, bf16[3,600,400]{2,1,0:T(8,128)(2,1)S(1)}) custom-call(bf16[16,600,600]{2,1,0:T(8,128)(2,1)S(1)} %shard_map.67.k_ref, bf16[400,600]{1,0:T(8,128)(2,1)S(1)} %bitcast.14, bf16[400,600]{1,0:T(8,128)(2,1)S(1)} %bitcast.15, bf16[408,600]{1,0:T(8,128)(2,1)S(1)} %get-tuple-element.44.refs_2_, ...), custom_call_target="tpu_custom_call" | custom-call | flops 1152000000 | bytes 3840000 | tf_op jit(solution)/shard_map/pallas_call | solution.py:32
  125.2 1.3 shard_map.80
  127.1 1.3 shard_map.81
  128.5 1.3 shard_map.82
  130.3 1.3 shard_map.83
  132.0 1.3 shard_map.84
  133.3 1.3 shard_map.85
  134.6 1.3 shard_map.86
  135.9 1.3 shard_map.87
  137.3 1.3 shard_map.88
  138.6 1.3 shard_map.89
  140.0 1.3 shard_map.90
  141.2 1.3 shard_map.91
  142.6 1.3 shard_map.92
  143.9 1.3 shard_map.93
  145.2 2.0 %shard_map.94 = (f32[2,8,600]{2,1,0:T(8,128)S(1)}, f32[8,600]{1,0:T(8,128)S(1)}, f32[2,600]{1,0:T(2,128)}, f32[8,128]{1,0:T(8,128)S(1)}) custom-call(bf16[16,600,600]{2,1,0:T(8,128)(2,1)S(1)} %shard_map.67.k_ref, bf16[400,600]{1,0:T(8,128)(2,1)S(1)} %collective-permute-done.3.refs_1_.refs_0_, ...), custom_call_target="tpu_custom_call", output_to_operand_aliasing={{0}: (5, {}), {1}: (6, {})} | custom-call | flops 576000000 | bytes 1920000 | tf_op jit(solution)/shard_map/pallas_call | solution.py:32
  147.6 0.8 collective-permute-done.40
  148.5 4.6 %collective-permute-start.41 = (f32[8,128]{1,0:T(8,128)S(1)}, f32[8,128]{1,0:T(8,128)S(1)}, u32[]{:S(2)}, u32[]{:S(2)}) collective-permute-start(f32[8,128]{1,0:T(8,128)S(1)} %add.15), channel_id=1, source_target_pairs={{32,0},{33,1},{34,2},{35,3},{36,4},{37,5},{38,6},{39,7},{40,8},{41... | collective-permute-start | bytes 12296 | tf_op jit(solution)/shard_map/ppermute | solution.py:57
  153.0 1.5 collective-permute-start.43
  154.5 1.0 collective-permute-done.42
  155.5 1.2 collective-permute-done.43
  156.7 2.9 %collective-permute-start.44 = (f32[8,128]{1,0:T(8,128)S(1)}, f32[8,128]{1,0:T(8,128)S(1)}, u32[]{:S(2)}, u32[]{:S(2)}) collective-permute-start(f32[8,128]{1,0:T(8,128)S(1)} %add_add_fusion), channel_id=1, source_target_pairs={{64,0},{65,1},{66,2},{67,3},{68,4},{69,5},{70,6},{71,7},{72,8},{73... | collective-permute-start | bytes 12296 | tf_op jit(solution)/shard_map/ppermute | solution.py:57
  159.6 1.0 collective-permute-done.44
  (71 shorter events, 7.5 us)
Async XLA Ops:
  0.6 11.5 %collective-permute-start.7 = (bf16[300,600]{1,0:T(8,128)(2,1)}, bf16[300,600]{1,0:T(8,128)(2,1)S(1)}, u32[]{:S(2)}, u32[]{:S(2)}) collective-permute-start(bf16[300,600]{1,0:T(8,128)(2,1)} %refs_0_.1), channel_id=1, source_target_pairs={{4,0},{5,1},{6,2},{7,3},{0,4},{1,5},{2,6},{3,7},{12,8},{13,9},{14,... | collective-permute-start | bytes 1080008 | tf_op jit(solution)/shard_map/ppermute | solution.py:57
  3.2 11.4 %collective-permute-start.5 = (bf16[300,600]{1,0:T(8,128)(2,1)}, bf16[300,600]{1,0:T(8,128)(2,1)S(1)}, u32[]{:S(2)}, u32[]{:S(2)}) collective-permute-start(bf16[300,600]{1,0:T(8,128)(2,1)} %refs_0_.1), channel_id=1, source_target_pairs={{2,0},{3,1},{0,2},{1,3},{6,4},{7,5},{4,6},{5,7},{10,8},{11,9},{8,1... | collective-permute-start | bytes 1080008 | tf_op jit(solution)/shard_map/ppermute | solution.py:57
  6.1 17.5 %collective-permute-start.10 = (bf16[300,600]{1,0:T(8,128)(2,1)}, bf16[300,600]{1,0:T(8,128)(2,1)S(1)}, u32[]{:S(2)}, u32[]{:S(2)}) collective-permute-start(bf16[300,600]{1,0:T(8,128)(2,1)} %refs_0_.1), channel_id=1, source_target_pairs={{1,0},{2,1},{3,2},{0,3},{5,4},{6,5},{7,6},{4,7},{9,8},{10,9},{11,1... | collective-permute-start | bytes 1080008 | tf_op jit(solution)/shard_map/ppermute | solution.py:57
  6.9 23.4 %collective-permute-start.38 = (bf16[400,600]{1,0:T(8,128)(2,1)}, bf16[400,600]{1,0:T(8,128)(2,1)S(1)}, u32[]{:S(2)}, u32[]{:S(2)}) collective-permute-start(bf16[400,600]{1,0:T(8,128)(2,1)} %bitcast.8), channel_id=1, source_target_pairs={{8,0},{9,1},{10,2},{11,3},{12,4},{13,5},{14,6},{15,7},{0,8},{1,9},... | collective-permute-start | bytes 1440008 | tf_op jit(solution)/shard_map/ppermute | solution.py:57
  8.4 18.5 %collective-permute-start.11 = (bf16[300,600]{1,0:T(8,128)(2,1)}, bf16[300,600]{1,0:T(8,128)(2,1)S(1)}, u32[]{:S(2)}, u32[]{:S(2)}) collective-permute-start(bf16[300,600]{1,0:T(8,128)(2,1)} %refs_0_.1), channel_id=1, source_target_pairs={{3,0},{0,1},{1,2},{2,3},{7,4},{4,5},{5,6},{6,7},{11,8},{8,9},{9,10... | collective-permute-start | bytes 1080008 | tf_op jit(solution)/shard_map/ppermute | solution.py:57
  12.1 18.1 %collective-permute-start.35 = (bf16[400,600]{1,0:T(8,128)(2,1)}, bf16[400,600]{1,0:T(8,128)(2,1)S(1)}, u32[]{:S(2)}, u32[]{:S(2)}) collective-permute-start(bf16[400,600]{1,0:T(8,128)(2,1)} %bitcast.9), channel_id=1, source_target_pairs={{48,0},{49,1},{50,2},{51,3},{52,4},{53,5},{54,6},{55,7},{56,8},{57... | collective-permute-start | bytes 1440008 | tf_op jit(solution)/shard_map/ppermute | solution.py:57
  14.6 16.8 %collective-permute-start.32 = (bf16[400,600]{1,0:T(8,128)(2,1)}, bf16[400,600]{1,0:T(8,128)(2,1)S(1)}, u32[]{:S(2)}, u32[]{:S(2)}) collective-permute-start(bf16[400,600]{1,0:T(8,128)(2,1)} %bitcast.10), channel_id=1, source_target_pairs={{16,0},{17,1},{18,2},{19,3},{20,4},{21,5},{22,6},{23,7},{24,8},{25... | collective-permute-start | bytes 1440008 | tf_op jit(solution)/shard_map/ppermute | solution.py:57
  23.6 14.1 %collective-permute-start = (bf16[400,600]{1,0:T(8,128)(2,1)}, bf16[400,600]{1,0:T(8,128)(2,1)S(1)}, u32[]{:S(2)}, u32[]{:S(2)}) collective-permute-start(bf16[400,600]{1,0:T(8,128)(2,1)} %bitcast.11), channel_id=1, source_target_pairs={{64,0},{65,1},{66,2},{67,3},{68,4},{69,5},{70,6},{71,7},{72,8},{73... | collective-permute-start | bytes 1440008 | tf_op jit(solution)/shard_map/ppermute | solution.py:57
  26.9 14.5 %collective-permute-start.8 = (bf16[300,600]{1,0:T(8,128)(2,1)S(1)}, bf16[300,600]{1,0:T(8,128)(2,1)S(1)}, u32[]{:S(2)}, u32[]{:S(2)}) collective-permute-start(bf16[300,600]{1,0:T(8,128)(2,1)S(1)} %collective-permute-done.7.refs_1_), channel_id=1, source_target_pairs={{1,0},{2,1},{3,2},{0,3},{5,4},{6,5},{7,6},{4,7},{9,8},{10,9},{11,1... | collective-permute-start | bytes 1080008 | tf_op jit(solution)/shard_map/ppermute | solution.py:57
  30.2 13.6 %collective-permute-start.9 = (bf16[300,600]{1,0:T(8,128)(2,1)S(1)}, bf16[300,600]{1,0:T(8,128)(2,1)S(1)}, u32[]{:S(2)}, u32[]{:S(2)}) collective-permute-start(bf16[300,600]{1,0:T(8,128)(2,1)S(1)} %collective-permute-done.7.refs_1_), channel_id=1, source_target_pairs={{3,0},{0,1},{1,2},{2,3},{7,4},{4,5},{5,6},{6,7},{11,8},{8,9},{9,10... | collective-permute-start | bytes 1080008 | tf_op jit(solution)/shard_map/ppermute | solution.py:57
  30.2 27.6 %collective-permute-start.36 = (bf16[400,600]{1,0:T(8,128)(2,1)S(1)}, bf16[400,600]{1,0:T(8,128)(2,1)S(1)}, u32[]{:S(2)}, u32[]{:S(2)}) collective-permute-start(bf16[400,600]{1,0:T(8,128)(2,1)S(1)} %collective-permute-done.35.refs_0_), channel_id=1, source_target_pairs={{8,0},{9,1},{10,2},{11,3},{12,4},{13,5},{14,6},{15,7},{0,8},{1,9},... | collective-permute-start | bytes 1440008 | tf_op jit(solution)/shard_map/ppermute | solution.py:57
  31.4 22.0 %collective-permute-start.6 = (bf16[300,600]{1,0:T(8,128)(2,1)S(1)}, bf16[300,600]{1,0:T(8,128)(2,1)S(1)}, u32[]{:S(2)}, u32[]{:S(2)}) collective-permute-start(bf16[300,600]{1,0:T(8,128)(2,1)S(1)} %collective-permute-done.5.refs_2_), channel_id=1, source_target_pairs={{4,0},{5,1},{6,2},{7,3},{0,4},{1,5},{2,6},{3,7},{12,8},{13,9},{14,... | collective-permute-start | bytes 1080008 | tf_op jit(solution)/shard_map/ppermute | solution.py:57
  37.7 20.5 %collective-permute-start.33 = (bf16[400,600]{1,0:T(8,128)(2,1)S(1)}, bf16[400,600]{1,0:T(8,128)(2,1)S(1)}, u32[]{:S(2)}, u32[]{:S(2)}) collective-permute-start(bf16[400,600]{1,0:T(8,128)(2,1)S(1)} %collective-permute-done.32.refs_0_), channel_id=1, source_target_pairs={{8,0},{9,1},{10,2},{11,3},{12,4},{13,5},{14,6},{15,7},{0,8},{1,9},... | collective-permute-start | bytes 1440008 | tf_op jit(solution)/shard_map/ppermute | solution.py:57
  41.4 17.1 %collective-permute-start.19 = (bf16[400,600]{1,0:T(8,128)(2,1)S(1)}, bf16[400,600]{1,0:T(8,128)(2,1)S(1)}, u32[]{:S(2)}, u32[]{:S(2)}) collective-permute-start(bf16[400,600]{1,0:T(8,128)(2,1)S(1)} %collective-permute-done.two_ref.refs_0_), channel_id=1, source_target_pairs={{48,0},{17,1},{50,2},{19,3},{52,4},{21,5},{54,6},{23,7},{24,8},{57... | collective-permute-start | bytes 1440008 | tf_op jit(solution)/shard_map/ppermute | solution.py:57
  43.8 17.0 %collective-permute-start.28 = (bf16[400,600]{1,0:T(8,128)(2,1)S(1)}, bf16[400,600]{1,0:T(8,128)(2,1)S(1)}, u32[]{:S(2)}, u32[]{:S(2)}) collective-permute-start(bf16[400,600]{1,0:T(8,128)(2,1)S(1)} %collective-permute-done.two_ref.refs_0_), channel_id=1, source_target_pairs={{8,0},{9,1},{10,2},{11,3},{12,4},{13,5},{14,6},{15,7},{0,8},{1,9},... | collective-permute-start | bytes 1440008 | tf_op jit(solution)/shard_map/ppermute | solution.py:57
  43.8 2.1 %copy-start.1 = (bf16[2,400,2400]{2,1,0:T(8,128)(2,1)S(1)}, bf16[2,400,2400]{2,1,0:T(8,128)(2,1)}, u32[]{:S(2)}) copy-start(bf16[2,400,2400]{2,1,0:T(8,128)(2,1)} %param.4) | copy-start | bytes 11520004
  45.9 3.4 %copy-start.2 = (bf16[300,600]{1,0:T(8,128)(2,1)S(1)}, bf16[300,600]{1,0:T(8,128)(2,1)}, u32[]{:S(2)}) copy-start(bf16[300,600]{1,0:T(8,128)(2,1)} %refs_0_.1) | copy-start | bytes 1080004
  51.6 1.6 %copy-start = (bf16[600,400]{0,1:T(8,128)(2,1)S(1)}, bf16[600,400]{0,1:T(8,128)(2,1)}, u32[]{:S(2)}) copy-start(bf16[600,400]{0,1:T(8,128)(2,1)} %param.6) | copy-start | bytes 1440004
  53.3 14.3 %collective-permute-start.1 = (bf16[400,600]{1,0:T(8,128)(2,1)S(1)}, bf16[400,600]{1,0:T(8,128)(2,1)S(1)}, u32[]{:S(2)}, u32[]{:S(2)}) collective-permute-start(bf16[400,600]{1,0:T(8,128)(2,1)S(1)} %shard_map.68), channel_id=1, source_target_pairs={{32,0},{33,1},{34,2},{35,3},{36,4},{37,5},{38,6},{39,7},{40,8},{41... | collective-permute-start | bytes 1440008 | tf_op jit(solution)/shard_map/ppermute | solution.py:57
  55.2 61.7 %slice-start = ((s8[11520000]{0:T(1024)(128)(4,1)}), s8[4194304]{0:T(1024)(128)(4,1)S(1)}, s32[]{:S(2)}) async-start(s8[11520000]{0:T(1024)(128)(4,1)} %bitcast.6), calls=%async_computation | async-start | bytes 8388608
  55.2 61.7 %slice-start.1 = ((s8[11520000]{0:T(1024)(128)(4,1)}), s8[4194304]{0:T(1024)(128)(4,1)S(1)}, s32[]{:S(2)}) async-start(s8[11520000]{0:T(1024)(128)(4,1)} %bitcast.6), calls=%async_computation.1 | async-start | bytes 8388608
  56.8 60.1 %slice-start.2 = ((s8[11520000]{0:T(1024)(128)(4,1)}), s8[3131392]{0:T(1024)(128)(4,1)S(1)}, s32[]{:S(2)}) async-start(s8[11520000]{0:T(1024)(128)(4,1)} %bitcast.6), calls=%async_computation.2 | async-start | bytes 6262784
  57.8 13.1 %collective-permute-start.39 = (bf16[408,600]{1,0:T(8,128)(2,1)S(1)}, bf16[408,600]{1,0:T(8,128)(2,1)S(1)}, u32[]{:S(2)}, u32[]{:S(2)}) collective-permute-start(bf16[408,600]{1,0:T(8,128)(2,1)S(1)} %get-tuple-element.47), channel_id=1, source_target_pairs={{8,0},{9,1},{10,2},{11,3},{12,4},{13,5},{14,6},{15,7},{0,8},{1,9},... | collective-permute-start | bytes 1468808 | tf_op jit(solution)/shard_map/ppermute | solution.py:57
  58.2 21.5 %collective-permute-start.23 = (bf16[408,600]{1,0:T(8,128)(2,1)S(1)}, bf16[408,600]{1,0:T(8,128)(2,1)S(1)}, u32[]{:S(2)}, u32[]{:S(2)}) collective-permute-start(bf16[408,600]{1,0:T(8,128)(2,1)S(1)} %get-tuple-element.44.refs_2_), channel_id=1, source_target_pairs={{48,0},{49,1},{50,2},{51,3},{52,4},{53,5},{54,6},{55,7},{56,8},{57... | collective-permute-start | bytes 1468808 | tf_op jit(solution)/shard_map/ppermute | solution.py:57
  58.5 22.4 %collective-permute-start.25 = (bf16[408,600]{1,0:T(8,128)(2,1)S(1)}, bf16[408,600]{1,0:T(8,128)(2,1)S(1)}, u32[]{:S(2)}, u32[]{:S(2)}) collective-permute-start(bf16[408,600]{1,0:T(8,128)(2,1)S(1)} %get-tuple-element.45.refs_3_), channel_id=1, source_target_pairs={{16,0},{17,1},{18,2},{19,3},{20,4},{21,5},{22,6},{23,7},{24,8},{25... | collective-permute-start | bytes 1468808 | tf_op jit(solution)/shard_map/ppermute | solution.py:57
  60.9 20.8 %collective-permute-start.14 = (bf16[408,600]{1,0:T(8,128)(2,1)S(1)}, bf16[408,600]{1,0:T(8,128)(2,1)S(1)}, u32[]{:S(2)}, u32[]{:S(2)}) collective-permute-start(bf16[408,600]{1,0:T(8,128)(2,1)S(1)} %get-tuple-element.43), channel_id=1, source_target_pairs={{64,0},{65,1},{66,2},{67,3},{68,4},{69,5},{70,6},{71,7},{72,8},{73... | collective-permute-start | bytes 1468808 | tf_op jit(solution)/shard_map/ppermute | solution.py:57
  67.7 18.5 %collective-permute-start.12 = (bf16[408,600]{1,0:T(8,128)(2,1)S(1)}, bf16[408,600]{1,0:T(8,128)(2,1)S(1)}, u32[]{:S(2)}, u32[]{:S(2)}) collective-permute-start(bf16[408,600]{1,0:T(8,128)(2,1)S(1)} %get-tuple-element.42), channel_id=1, source_target_pairs={{64,0},{65,1},{66,2},{67,3},{68,4},{69,5},{70,6},{71,7},{72,8},{73... | collective-permute-start | bytes 1468808 | tf_op jit(solution)/shard_map/ppermute | solution.py:57
  70.9 15.6 %collective-permute-start.30 = (bf16[400,600]{1,0:T(8,128)(2,1)S(1)}, bf16[400,600]{1,0:T(8,128)(2,1)S(1)}, u32[]{:S(2)}, u32[]{:S(2)}) collective-permute-start(bf16[400,600]{1,0:T(8,128)(2,1)S(1)} %collective-permute-done.19.refs_0_), channel_id=1, source_target_pairs={{8,0},{9,1},{10,2},{11,3},{12,4},{13,5},{14,6},{15,7},{0,8},{1,9},... | collective-permute-start | bytes 1440008 | tf_op jit(solution)/shard_map/ppermute | solution.py:57
  79.7 12.8 %collective-permute-start.2 = (bf16[400,600]{1,0:T(8,128)(2,1)S(1)}, bf16[400,600]{1,0:T(8,128)(2,1)S(1)}, u32[]{:S(2)}, u32[]{:S(2)}) collective-permute-start(bf16[400,600]{1,0:T(8,128)(2,1)S(1)} %collective-permute-done.1.refs_0_.refs_1_), channel_id=1, source_target_pairs={{1,0},{0,1},{3,2},{2,3},{5,4},{4,5},{7,6},{6,7},{9,8},{8,9},{11,10... | collective-permute-start | bytes 1440008 | tf_op jit(solution)/shard_map/ppermute | solution.py:57
  80.9 13.8 %collective-permute-start.4 = (bf16[400,600]{1,0:T(8,128)(2,1)S(1)}, bf16[400,600]{1,0:T(8,128)(2,1)S(1)}, u32[]{:S(2)}, u32[]{:S(2)}) collective-permute-start(bf16[400,600]{1,0:T(8,128)(2,1)S(1)} %collective-permute-done.1.refs_0_.refs_1_), channel_id=1, source_target_pairs={{8,0},{9,1},{10,2},{11,3},{12,4},{13,5},{14,6},{15,7},{0,8},{1,9},... | collective-permute-start | bytes 1440008 | tf_op jit(solution)/shard_map/ppermute | solution.py:57
  81.6 21.8 %collective-permute-start.20 = (bf16[400,600]{1,0:T(8,128)(2,1)S(1)}, bf16[400,600]{1,0:T(8,128)(2,1)S(1)}, u32[]{:S(2)}, u32[]{:S(2)}) collective-permute-start(bf16[400,600]{1,0:T(8,128)(2,1)S(1)} %collective-permute-done.19.refs_0_), channel_id=1, source_target_pairs={{1,0},{0,1},{3,2},{2,3},{5,4},{4,5},{7,6},{6,7},{9,8},{8,9},{11,10... | collective-permute-start | bytes 1440008 | tf_op jit(solution)/shard_map/ppermute | solution.py:57
  86.2 18.6 %collective-permute-start.15 = (bf16[408,600]{1,0:T(8,128)(2,1)S(1)}, bf16[408,600]{1,0:T(8,128)(2,1)S(1)}, u32[]{:S(2)}, u32[]{:S(2)}) collective-permute-start(bf16[408,600]{1,0:T(8,128)(2,1)S(1)} %collective-permute-done.14.one_ref), channel_id=1, source_target_pairs={{48,0},{17,1},{50,2},{19,3},{52,4},{21,5},{54,6},{23,7},{24,8},{57... | collective-permute-start | bytes 1468808 | tf_op jit(solution)/shard_map/ppermute | solution.py:57
  86.6 20.2 %collective-permute-start.13 = (bf16[408,600]{1,0:T(8,128)(2,1)S(1)}, bf16[408,600]{1,0:T(8,128)(2,1)S(1)}, u32[]{:S(2)}, u32[]{:S(2)}) collective-permute-start(bf16[408,600]{1,0:T(8,128)(2,1)S(1)} %collective-permute-done.12.two_ref), channel_id=1, source_target_pairs={{16,0},{49,1},{18,2},{51,3},{20,4},{53,5},{22,6},{55,7},{56,8},{25... | collective-permute-start | bytes 1468808 | tf_op jit(solution)/shard_map/ppermute | solution.py:57
  92.5 14.4 %collective-permute-start.37 = (bf16[408,600]{1,0:T(8,128)(2,1)S(1)}, bf16[408,600]{1,0:T(8,128)(2,1)S(1)}, u32[]{:S(2)}, u32[]{:S(2)}) collective-permute-start(bf16[408,600]{1,0:T(8,128)(2,1)S(1)} %collective-permute-done.23.refs_1_), channel_id=1, source_target_pairs={{8,0},{9,1},{10,2},{11,3},{12,4},{13,5},{14,6},{15,7},{0,8},{1,9},... | collective-permute-start | bytes 1468808 | tf_op jit(solution)/shard_map/ppermute | solution.py:57
  94.7 17.0 %collective-permute-start.24 = (bf16[408,600]{1,0:T(8,128)(2,1)S(1)}, bf16[408,600]{1,0:T(8,128)(2,1)S(1)}, u32[]{:S(2)}, u32[]{:S(2)}) collective-permute-start(bf16[408,600]{1,0:T(8,128)(2,1)S(1)} %collective-permute-done.23.refs_1_), channel_id=1, source_target_pairs={{48,0},{56,8},{0,16},{8,24},{112,64},{120,72},{64,80},{72,88},{49,... | collective-permute-start | bytes 1468808 | tf_op jit(solution)/shard_map/ppermute | solution.py:81
  103.5 10.9 %collective-permute-start.26 = (bf16[408,600]{1,0:T(8,128)(2,1)S(1)}, bf16[408,600]{1,0:T(8,128)(2,1)S(1)}, u32[]{:S(2)}, u32[]{:S(2)}) collective-permute-start(bf16[408,600]{1,0:T(8,128)(2,1)S(1)} %collective-permute-done.25.refs_1_), channel_id=1, source_target_pairs={{48,32},{56,40},{0,48},{8,56},{112,96},{120,104},{64,112},{72,120}... | collective-permute-start | bytes 1468808 | tf_op jit(solution)/shard_map/ppermute | solution.py:81
  104.8 20.4 %collective-permute-start.34 = (bf16[408,600]{1,0:T(8,128)(2,1)S(1)}, bf16[408,600]{1,0:T(8,128)(2,1)S(1)}, u32[]{:S(2)}, u32[]{:S(2)}) collective-permute-start(bf16[408,600]{1,0:T(8,128)(2,1)S(1)} %collective-permute-done.25.refs_1_), channel_id=1, source_target_pairs={{8,0},{9,1},{10,2},{11,3},{12,4},{13,5},{14,6},{15,7},{0,8},{1,9},... | collective-permute-start | bytes 1468808 | tf_op jit(solution)/shard_map/ppermute | solution.py:57
  106.8 19.8 %collective-permute-start.29 = (bf16[408,600]{1,0:T(8,128)(2,1)S(1)}, bf16[408,600]{1,0:T(8,128)(2,1)S(1)}, u32[]{:S(2)}, u32[]{:S(2)}) collective-permute-start(bf16[408,600]{1,0:T(8,128)(2,1)S(1)} %shard_map.79.refs_1_), channel_id=1, source_target_pairs={{8,0},{9,1},{10,2},{11,3},{12,4},{13,5},{14,6},{15,7},{0,8},{1,9},... | collective-permute-start | bytes 1468808 | tf_op jit(solution)/shard_map/ppermute | solution.py:57
  106.9 21.5 %collective-permute-start.17 = (bf16[408,600]{1,0:T(8,128)(2,1)S(1)}, bf16[408,600]{1,0:T(8,128)(2,1)S(1)}, u32[]{:S(2)}, u32[]{:S(2)}) collective-permute-start(bf16[408,600]{1,0:T(8,128)(2,1)S(1)} %shard_map.75), channel_id=1, source_target_pairs={{16,32},{24,40},{32,48},{40,56},{80,96},{88,104},{96,112},{104,120... | collective-permute-start | bytes 1468808 | tf_op jit(solution)/shard_map/ppermute | solution.py:81
  111.7 18.1 %collective-permute-start.16 = (bf16[408,600]{1,0:T(8,128)(2,1)S(1)}, bf16[408,600]{1,0:T(8,128)(2,1)S(1)}, u32[]{:S(2)}, u32[]{:S(2)}) collective-permute-start(bf16[408,600]{1,0:T(8,128)(2,1)S(1)} %shard_map.74), channel_id=1, source_target_pairs={{16,0},{24,8},{32,16},{40,24},{80,64},{88,72},{96,80},{104,88},{17... | collective-permute-start | bytes 1468808 | tf_op jit(solution)/shard_map/ppermute | solution.py:81
  114.4 17.3 %collective-permute-start.31 = (bf16[408,600]{1,0:T(8,128)(2,1)S(1)}, bf16[408,600]{1,0:T(8,128)(2,1)S(1)}, u32[]{:S(2)}, u32[]{:S(2)}) collective-permute-start(bf16[408,600]{1,0:T(8,128)(2,1)S(1)} %collective-permute-done.15.two_ref.one_ref.refs_1_), channel_id=1, source_target_pairs={{8,0},{9,1},{10,2},{11,3},{12,4},{13,5},{14,6},{15,7},{0,8},{1,9},... | collective-permute-start | bytes 1468808 | tf_op jit(solution)/shard_map/ppermute | solution.py:57
  125.1 14.8 %collective-permute-start.27 = (bf16[408,600]{1,0:T(8,128)(2,1)S(1)}, bf16[408,600]{1,0:T(8,128)(2,1)S(1)}, u32[]{:S(2)}, u32[]{:S(2)}) collective-permute-start(bf16[408,600]{1,0:T(8,128)(2,1)S(1)} %shard_map.78.refs_2_), channel_id=1, source_target_pairs={{8,0},{9,1},{10,2},{11,3},{12,4},{13,5},{14,6},{15,7},{0,8},{1,9},... | collective-permute-start | bytes 1468808 | tf_op jit(solution)/shard_map/ppermute | solution.py:57
  126.5 13.4 %collective-permute-start.3 = (bf16[400,600]{1,0:T(8,128)(2,1)S(1)}, bf16[400,600]{1,0:T(8,128)(2,1)S(1)}, u32[]{:S(2)}, u32[]{:S(2)}) collective-permute-start(bf16[400,600]{1,0:T(8,128)(2,1)S(1)} %collective-permute-done.2.refs_1_.refs_0_), channel_id=1, source_target_pairs={{8,0},{9,1},{10,2},{11,3},{12,4},{13,5},{14,6},{15,7},{0,8},{1,9},... | collective-permute-start | bytes 1440008 | tf_op jit(solution)/shard_map/ppermute | solution.py:57
  128.4 14.2 %collective-permute-start.22 = (bf16[408,600]{1,0:T(8,128)(2,1)S(1)}, bf16[408,600]{1,0:T(8,128)(2,1)S(1)}, u32[]{:S(2)}, u32[]{:S(2)}) collective-permute-start(bf16[408,600]{1,0:T(8,128)(2,1)S(1)} %collective-permute-done.13.one_ref.two_ref.refs_1_), channel_id=1, source_target_pairs={{8,0},{9,1},{10,2},{11,3},{12,4},{13,5},{14,6},{15,7},{0,8},{1,9},... | collective-permute-start | bytes 1468808 | tf_op jit(solution)/shard_map/ppermute | solution.py:57
  129.8 12.8 %collective-permute-start.21 = (bf16[400,600]{1,0:T(8,128)(2,1)S(1)}, bf16[400,600]{1,0:T(8,128)(2,1)S(1)}, u32[]{:S(2)}, u32[]{:S(2)}) collective-permute-start(bf16[400,600]{1,0:T(8,128)(2,1)S(1)} %collective-permute-done.20.refs_0_), channel_id=1, source_target_pairs={{8,0},{9,1},{10,2},{11,3},{12,4},{13,5},{14,6},{15,7},{0,8},{1,9},... | collective-permute-start | bytes 1440008 | tf_op jit(solution)/shard_map/ppermute | solution.py:57
  131.7 13.5 %collective-permute-start.18 = (bf16[408,600]{1,0:T(8,128)(2,1)S(1)}, bf16[408,600]{1,0:T(8,128)(2,1)S(1)}, u32[]{:S(2)}, u32[]{:S(2)}) collective-permute-start(bf16[408,600]{1,0:T(8,128)(2,1)S(1)} %shard_map.76.refs_2_), channel_id=1, source_target_pairs={{8,0},{9,1},{10,2},{11,3},{12,4},{13,5},{14,6},{15,7},{0,8},{1,9},... | collective-permute-start | bytes 1468808 | tf_op jit(solution)/shard_map/ppermute | solution.py:57
  147.2 1.3 collective-permute-start.40
  148.5 6.0 %collective-permute-start.41 = (f32[8,128]{1,0:T(8,128)S(1)}, f32[8,128]{1,0:T(8,128)S(1)}, u32[]{:S(2)}, u32[]{:S(2)}) collective-permute-start(f32[8,128]{1,0:T(8,128)S(1)} %add.15), channel_id=1, source_target_pairs={{32,0},{33,1},{34,2},{35,3},{36,4},{37,5},{38,6},{39,7},{40,8},{41... | collective-permute-start | bytes 12296 | tf_op jit(solution)/shard_map/ppermute | solution.py:57
  153.0 2.5 %collective-permute-start.42 = (f32[8,128]{1,0:T(8,128)S(1)}, f32[8,128]{1,0:T(8,128)S(1)}, u32[]{:S(2)}, u32[]{:S(2)}) collective-permute-start(f32[8,128]{1,0:T(8,128)S(1)} %add.15), channel_id=1, source_target_pairs={{16,0},{17,1},{18,2},{19,3},{20,4},{21,5},{22,6},{23,7},{24,8},{25... | collective-permute-start | bytes 12296 | tf_op jit(solution)/shard_map/ppermute | solution.py:57
  153.0 3.7 %collective-permute-start.43 = (f32[8,128]{1,0:T(8,128)S(1)}, f32[8,128]{1,0:T(8,128)S(1)}, u32[]{:S(2)}, u32[]{:S(2)}) collective-permute-start(f32[8,128]{1,0:T(8,128)S(1)} %add.15), channel_id=1, source_target_pairs={{48,0},{49,1},{50,2},{51,3},{52,4},{53,5},{54,6},{55,7},{56,8},{57... | collective-permute-start | bytes 12296 | tf_op jit(solution)/shard_map/ppermute | solution.py:57
  156.7 4.0 %collective-permute-start.44 = (f32[8,128]{1,0:T(8,128)S(1)}, f32[8,128]{1,0:T(8,128)S(1)}, u32[]{:S(2)}, u32[]{:S(2)}) collective-permute-start(f32[8,128]{1,0:T(8,128)S(1)} %add_add_fusion), channel_id=1, source_target_pairs={{64,0},{65,1},{66,2},{67,3},{68,4},{69,5},{70,6},{71,7},{72,8},{73... | collective-permute-start | bytes 12296 | tf_op jit(solution)/shard_map/ppermute | solution.py:57

commit v3 on v2

--- a/solution.py
+++ b/solution.py
@@ -79,6 +79,21 @@
             for c in range(CORES):
                 route.append((pts_id(a, x - step, c), pts_id(a, x, c)))
     return lax.ppermute(block, AXES[0], route)
+
+
+def onward_by_parity(block, rightward):
+    route = []
+    for a in range(PLANES):
+        for x in range(COLS):
+            for c in range(CORES):
+                for z in range(ZLO):
+                    for y in range(YS):
+                        step = 1 if (y ^ c) & 1 == rightward else -1
+                        if (x >= COLS // 2) == (step == 1):
+                            at = z * YS + y
+                            start = pts_id(a, x - step, c) * ZLO * YS + at
+                            route.append((start, pts_id(a, x, c) * ZLO * YS + at))
+    return lax.ppermute(block, AXES, route)
 
 
 def place():
@@ -348,12 +363,9 @@
     right = onward(theta[LEFT], 1, (0, 1))
     left = onward(theta[RIGHT], -1, (2, 3))
     theta[FAR] = pick(right_half, right, left)
-    side, side2 = theta[SIDE], theta[SIDE2]
-    walker0 = pick(lambda a, x, c, y: (y ^ c) & 1, side, side2)
-    walker1 = pick(lambda a, x, c, y: (y ^ c) & 1, side2, side)
-    right = onward(walker0, 1, (2, 3))
-    left = onward(walker1, -1, (0, 1))
-    theta[FAR2] = pick(right_half, left, right)
+    one = onward_by_parity(theta[SIDE], 0)
+    two = onward_by_parity(theta[SIDE2], 1)
+    theta[FAR2] = pick(lambda a, x, c, y: 1 ^ x >> 1 ^ (y ^ c) & 1, one, two)
     theta_sib = {slot: from_chip(theta[slot], 0, 0, 1) for slot in theta}
     occ_sib = {slot: [from_chip(occ[slot][0], 0, 0, 1)] for slot in occ}
     occ_sib[FAR] += [from_chip(occ_far2, 0, 0, 1)]

time: 163 us -> 163 us (level)
  waiting for transfers between devices: 52.5 us -> 56.7 us
  starting transfers between devices: 66.4 us -> 62.7 us
    ppermute x41, waiting for transfers between devices: 47.1 us -> 55.8 us  [from_device(): return lax.ppermute(block, AXES, route)]
    ppermute x4 -> x2, waiting for transfers between devices: 5.42 us -> 0.95 us  [onward(): return lax.ppermute(block, AXES[0], route)]
    ppermute x41, starting transfers between devices: 61 us -> 57.5 us  [from_device(): return lax.ppermute(block, AXES, route)]
    ppermute x4 -> x2, starting transfers between devices: 5.48 us -> 3.22 us  [onward(): return lax.ppermute(block, AXES[0], route)]
    ppermute x0 -> x2, starting transfers between devices: none -> 1.96 us  [onward_by_parity(): return lax.ppermute(block, AXES, route)]
    pallas_call x26 -> x24, Pallas kernels: 29.4 us -> 29.4 us  [call(): pl.pallas_call(body, in_specs=[whole()] * len(operands), out_specs=jax.tr...]
where the time goes in v3:
time: 163 us; the launch traced here: 162 us
  starting transfers between devices  62.7 us (38%)
  waiting for transfers between devices  56.7 us (35%)
  Pallas kernels  38.6 us (24%)
  local copies, waits for them, and re-layouts  2.72 us (2%)
    ppermute x41, starting transfers between devices, from_device(): return lax.ppermute(block, AXES, route)  57.5 us
    ppermute x41, waiting for transfers between devices, from_device(): return lax.ppermute(block, AXES, route)  55.8 us
    pallas_call x24, Pallas kernels, call(): pl.pallas_call(body, in_specs=[whole()] * len(operands), out_specs=jax.tr...  29.4 us
    pallas_call x2, Pallas kernels, split_columns(): pl.pallas_call(body, grid=(steps,), in_specs=[pl.BlockSpec((tile, cols),...  9.18 us
  transfers between devices with their start and end apart: 45, of which 15 were waited for; matrix products, arithmetic and copies ran while one was open for 0% of the time, Pallas kernels for 23%

profile of v3, /device:TPU:1, one launch (start us, length us, event | category | flops | bytes accessed | tf_op | source)
XLA Modules:
  0.0 161.7 jit_solution(10464324412490741535)
XLA Ops:
  0.6 2.5 %collective-permute-start.7 = (bf16[300,600]{1,0:T(8,128)(2,1)}, bf16[300,600]{1,0:T(8,128)(2,1)S(1)}, u32[]{:S(2)}, u32[]{:S(2)}) collective-permute-start(bf16[300,600]{1,0:T(8,128)(2,1)} %refs_0_.1), channel_id=1, source_target_pairs={{4,0},{5,1},{6,2},{7,3},{0,4},{1,5},{2,6},{3,7},{12,8},{13,9},{14,... | collective-permute-start | bytes 1080008 | tf_op jit(solution)/shard_map/ppermute | solution.py:57
  3.2 2.9 %collective-permute-start.5 = (bf16[300,600]{1,0:T(8,128)(2,1)}, bf16[300,600]{1,0:T(8,128)(2,1)S(1)}, u32[]{:S(2)}, u32[]{:S(2)}) collective-permute-start(bf16[300,600]{1,0:T(8,128)(2,1)} %refs_0_.1), channel_id=1, source_target_pairs={{2,0},{3,1},{0,2},{1,3},{6,4},{7,5},{4,6},{5,7},{10,8},{11,9},{8,1... | collective-permute-start | bytes 1080008 | tf_op jit(solution)/shard_map/ppermute | solution.py:57
  6.1 0.8 collective-permute-start.10
  6.9 1.5 collective-permute-start.38
  9.1 3.0 %collective-permute-done.7.refs_1_ = bf16[300,600]{1,0:T(8,128)(2,1)S(1)} collective-permute-done((bf16[300,600]{1,0:T(8,128)(2,1)}, bf16[300,600]{1,0:T(8,128)(2,1)S(1)}, u32[]{:S(2)}, u32[]{:S(2)}) %collective-permute-start.7) | collective-permute-done | bytes 360032 | tf_op jit(solution)/shard_map/ppermute | solution.py:57
  12.1 1.1 collective-permute-start.35
  13.2 1.4 collective-permute-done.5.refs_2_
  14.6 2.5 %collective-permute-start.32 = (bf16[400,600]{1,0:T(8,128)(2,1)}, bf16[400,600]{1,0:T(8,128)(2,1)S(1)}, u32[]{:S(2)}, u32[]{:S(2)}) collective-permute-start(bf16[400,600]{1,0:T(8,128)(2,1)} %bitcast.10), channel_id=1, source_target_pairs={{16,0},{17,1},{18,2},{19,3},{20,4},{21,5},{22,6},{23,7},{24,8},{25... | collective-permute-start | bytes 1440008 | tf_op jit(solution)/shard_map/ppermute | solution.py:57
  17.1 6.5 %collective-permute-done.10.refs_0_ = bf16[300,600]{1,0:T(8,128)(2,1)S(1)} collective-permute-done((bf16[300,600]{1,0:T(8,128)(2,1)}, bf16[300,600]{1,0:T(8,128)(2,1)S(1)}, u32[]{:S(2)}, u32[]{:S(2)}) %collective-permute-start.10) | collective-permute-done | bytes 360032 | tf_op jit(solution)/shard_map/ppermute | solution.py:57
  23.6 3.3 %collective-permute-start = (bf16[400,600]{1,0:T(8,128)(2,1)}, bf16[400,600]{1,0:T(8,128)(2,1)S(1)}, u32[]{:S(2)}, u32[]{:S(2)}) collective-permute-start(bf16[400,600]{1,0:T(8,128)(2,1)} %bitcast.11), channel_id=1, source_target_pairs={{64,0},{65,1},{66,2},{67,3},{68,4},{69,5},{70,6},{71,7},{72,8},{73... | collective-permute-start | bytes 1440008 | tf_op jit(solution)/shard_map/ppermute | solution.py:57
  26.9 3.3 %collective-permute-start.8 = (bf16[300,600]{1,0:T(8,128)(2,1)S(1)}, bf16[300,600]{1,0:T(8,128)(2,1)S(1)}, u32[]{:S(2)}, u32[]{:S(2)}) collective-permute-start(bf16[300,600]{1,0:T(8,128)(2,1)S(1)} %collective-permute-done.7.refs_1_), channel_id=1, source_target_pairs={{1,0},{2,1},{3,2},{0,3},{5,4},{6,5},{7,6},{4,7},{9,8},{10,9},{11,1... | collective-permute-start | bytes 1080008 | tf_op jit(solution)/shard_map/ppermute | solution.py:57
  30.2 1.1 collective-permute-start.36
  31.4 6.3 %collective-permute-done.two_ref.refs_0_ = bf16[400,600]{1,0:T(8,128)(2,1)S(1)} collective-permute-done((bf16[400,600]{1,0:T(8,128)(2,1)}, bf16[400,600]{1,0:T(8,128)(2,1)S(1)}, u32[]{:S(2)}, u32[]{:S(2)}) %collective-permute-start) | collective-permute-done | bytes 480032 | tf_op jit(solution)/shard_map/ppermute | solution.py:57
  37.7 3.7 %collective-permute-start.33 = (bf16[400,600]{1,0:T(8,128)(2,1)S(1)}, bf16[400,600]{1,0:T(8,128)(2,1)S(1)}, u32[]{:S(2)}, u32[]{:S(2)}) collective-permute-start(bf16[400,600]{1,0:T(8,128)(2,1)S(1)} %collective-permute-done.32.refs_0_), channel_id=1, source_target_pairs={{8,0},{9,1},{10,2},{11,3},{12,4},{13,5},{14,6},{15,7},{0,8},{1,9},... | collective-permute-start | bytes 1440008 | tf_op jit(solution)/shard_map/ppermute | solution.py:57
  41.4 2.5 %collective-permute-start.19 = (bf16[400,600]{1,0:T(8,128)(2,1)S(1)}, bf16[400,600]{1,0:T(8,128)(2,1)S(1)}, u32[]{:S(2)}, u32[]{:S(2)}) collective-permute-start(bf16[400,600]{1,0:T(8,128)(2,1)S(1)} %collective-permute-done.two_ref.refs_0_), channel_id=1, source_target_pairs={{48,0},{17,1},{50,2},{19,3},{52,4},{21,5},{54,6},{23,7},{24,8},{57... | collective-permute-start | bytes 1440008 | tf_op jit(solution)/shard_map/ppermute | solution.py:57
  43.8 2.1 %copy-done.1 = bf16[2,400,2400]{2,1,0:T(8,128)(2,1)S(1)} copy-done((bf16[2,400,2400]{2,1,0:T(8,128)(2,1)S(1)}, bf16[2,400,2400]{2,1,0:T(8,128)(2,1)}, u32[]{:S(2)}) %copy-start.1) | copy-done | bytes 3840024
  45.9 3.4 %shard_map.69.g_ref = bf16[8,800,300]{2,1,0:T(8,128)(2,1)S(1)} custom-call(bf16[800,2400]{1,0:T(8,128)(2,1)S(1)} %bitcast.16), custom_call_target="tpu_custom_call" | custom-call | tf_op jit(solution)/shard_map/pallas_call | solution.py:135
  49.4 2.2 %shard_map.70.refs_2_ = f32[800,600]{1,0:T(8,128)S(1)} custom-call(bf16[8,800,300]{2,1,0:T(8,128)(2,1)S(1)} %shard_map.69.g_ref, bf16[300,600]{1,0:T(8,128)(2,1)S(1)} %copy-done.2, bf16[300,600]{1,0:T(8,128)(2,1)S(1)} %collective-permute-done.7.refs_1_, bf16[300,600]{1,0:T(8,128)(2,1)S(1)} %collective-permute-done.5.refs_2_), custom_call_target="tpu_custom_call" | custom-call | flops 864000000 | bytes 2880000 | tf_op jit(solution)/shard_map/pallas_call | solution.py:32
  51.6 1.6 %shard_map.71.refs_2_ = f32[800,600]{1,0:T(8,128)S(1)} custom-call(bf16[8,800,300]{2,1,0:T(8,128)(2,1)S(1)} %shard_map.69.g_ref, bf16[300,600]{1,0:T(8,128)(2,1)S(1)} %collective-permute-done.10.refs_0_, bf16[300,600]{1,0:T(8,128)(2,1)S(1)} %collective-permute-done.11.refs_1_, f32[800,600]{1,0:T(8,128)S(1)} %shard_map.70.refs_2_), custom_call_target="tpu_custom_call" | custom-call | flops 576000000 | bytes 1920000 | tf_op jit(solution)/shard_map/pallas_call | solution.py:32
  53.4 1.8 %collective-permute-start.1 = (bf16[400,600]{1,0:T(8,128)(2,1)S(1)}, bf16[400,600]{1,0:T(8,128)(2,1)S(1)}, u32[]{:S(2)}, u32[]{:S(2)}) collective-permute-start(bf16[400,600]{1,0:T(8,128)(2,1)S(1)} %shard_map.68), channel_id=1, source_target_pairs={{32,0},{33,1},{34,2},{35,3},{36,4},{37,5},{38,6},{39,7},{40,8},{41... | collective-permute-start | bytes 1440008 | tf_op jit(solution)/shard_map/ppermute | solution.py:57
  55.2 1.6 shard_map.72.refs_1_
  56.8 1.0 shard_map.73
  58.5 2.4 %collective-permute-start.25 = (bf16[408,600]{1,0:T(8,128)(2,1)S(1)}, bf16[408,600]{1,0:T(8,128)(2,1)S(1)}, u32[]{:S(2)}, u32[]{:S(2)}) collective-permute-start(bf16[408,600]{1,0:T(8,128)(2,1)S(1)} %get-tuple-element.45.refs_3_), channel_id=1, source_target_pairs={{16,0},{17,1},{18,2},{19,3},{20,4},{21,5},{22,6},{23,7},{24,8},{25... | collective-permute-start | bytes 1468808 | tf_op jit(solution)/shard_map/ppermute | solution.py:57
  60.9 2.9 %collective-permute-start.12 = (bf16[408,600]{1,0:T(8,128)(2,1)S(1)}, bf16[408,600]{1,0:T(8,128)(2,1)S(1)}, u32[]{:S(2)}, u32[]{:S(2)}) collective-permute-start(bf16[408,600]{1,0:T(8,128)(2,1)S(1)} %get-tuple-element.42), channel_id=1, source_target_pairs={{64,0},{65,1},{66,2},{67,3},{68,4},{69,5},{70,6},{71,7},{72,8},{73... | collective-permute-start | bytes 1468808 | tf_op jit(solution)/shard_map/ppermute | solution.py:57
  63.8 3.9 %collective-permute-done.1.refs_0_.refs_1_ = bf16[400,600]{1,0:T(8,128)(2,1)S(1)} collective-permute-done((bf16[400,600]{1,0:T(8,128)(2,1)S(1)}, bf16[400,600]{1,0:T(8,128)(2,1)S(1)}, u32[]{:S(2)}, u32[]{:S(2)}) %collective-permute-start.1) | collective-permute-done | bytes 480032 | tf_op jit(solution)/shard_map/ppermute | solution.py:57
  67.7 3.2 %collective-permute-start.15 = (bf16[408,600]{1,0:T(8,128)(2,1)S(1)}, bf16[408,600]{1,0:T(8,128)(2,1)S(1)}, u32[]{:S(2)}, u32[]{:S(2)}) collective-permute-start(bf16[408,600]{1,0:T(8,128)(2,1)S(1)} %get-tuple-element.43), channel_id=1, source_target_pairs={{64,0},{65,1},{66,2},{67,3},{68,4},{69,5},{70,6},{71,7},{72,8},{73... | collective-permute-start | bytes 1468808 | tf_op jit(solution)/shard_map/ppermute | solution.py:57
  70.9 2.6 %collective-permute-start.30 = (bf16[400,600]{1,0:T(8,128)(2,1)S(1)}, bf16[400,600]{1,0:T(8,128)(2,1)S(1)}, u32[]{:S(2)}, u32[]{:S(2)}) collective-permute-start(bf16[400,600]{1,0:T(8,128)(2,1)S(1)} %collective-permute-done.19.refs_0_), channel_id=1, source_target_pairs={{8,0},{9,1},{10,2},{11,3},{12,4},{13,5},{14,6},{15,7},{0,8},{1,9},... | collective-permute-start | bytes 1440008 | tf_op jit(solution)/shard_map/ppermute | solution.py:57
  73.5 6.2 %collective-permute-done.23.refs_1_ = bf16[408,600]{1,0:T(8,128)(2,1)S(1)} collective-permute-done((bf16[408,600]{1,0:T(8,128)(2,1)S(1)}, bf16[408,600]{1,0:T(8,128)(2,1)S(1)}, u32[]{:S(2)}, u32[]{:S(2)}) %collective-permute-start.23) | collective-permute-done | bytes 489632 | tf_op jit(solution)/shard_map/ppermute | solution.py:57
  79.7 1.2 collective-permute-start.2
  82.0 4.3 %collective-permute-done.15.two_ref = bf16[408,600]{1,0:T(8,128)(2,1)S(1)} collective-permute-done((bf16[408,600]{1,0:T(8,128)(2,1)S(1)}, bf16[408,600]{1,0:T(8,128)(2,1)S(1)}, u32[]{:S(2)}, u32[]{:S(2)}) %collective-permute-start.15) | collective-permute-done | bytes 489632 | tf_op jit(solution)/shard_map/ppermute | solution.py:57
  86.2 1.6 %collective-permute-start.37 = (bf16[408,600]{1,0:T(8,128)(2,1)S(1)}, bf16[408,600]{1,0:T(8,128)(2,1)S(1)}, u32[]{:S(2)}, u32[]{:S(2)}) collective-permute-start(bf16[408,600]{1,0:T(8,128)(2,1)S(1)} %collective-permute-done.23.refs_1_), channel_id=1, source_target_pairs={{8,0},{9,1},{10,2},{11,3},{12,4},{13,5},{14,6},{15,7},{0,8},{1,9},... | collective-permute-start | bytes 1468808 | tf_op jit(solution)/shard_map/ppermute | solution.py:57
  88.0 4.5 %collective-permute-done.2.refs_1_.refs_0_ = bf16[400,600]{1,0:T(8,128)(2,1)S(1)} collective-permute-done((bf16[400,600]{1,0:T(8,128)(2,1)S(1)}, bf16[400,600]{1,0:T(8,128)(2,1)S(1)}, u32[]{:S(2)}, u32[]{:S(2)}) %collective-permute-start.2) | collective-permute-done | bytes 480032 | tf_op jit(solution)/shard_map/ppermute | solution.py:57
  92.5 1.9 %collective-permute-start.24 = (bf16[408,600]{1,0:T(8,128)(2,1)S(1)}, bf16[408,600]{1,0:T(8,128)(2,1)S(1)}, u32[]{:S(2)}, u32[]{:S(2)}) collective-permute-start(bf16[408,600]{1,0:T(8,128)(2,1)S(1)} %collective-permute-done.23.refs_1_), channel_id=1, source_target_pairs={{48,0},{56,8},{0,16},{8,24},{112,64},{120,72},{64,80},{72,88},{49,... | collective-permute-start | bytes 1468808 | tf_op jit(solution)/shard_map/ppermute | solution.py:81
  94.7 8.8 %collective-permute-done.20.refs_0_ = bf16[400,600]{1,0:T(8,128)(2,1)S(1)} collective-permute-done((bf16[400,600]{1,0:T(8,128)(2,1)S(1)}, bf16[400,600]{1,0:T(8,128)(2,1)S(1)}, u32[]{:S(2)}, u32[]{:S(2)}) %collective-permute-start.20) | collective-permute-done | bytes 480032 | tf_op jit(solution)/shard_map/ppermute | solution.py:57
  103.5 1.3 collective-permute-start.26
  104.8 1.9 %collective-permute-start.34 = (bf16[408,600]{1,0:T(8,128)(2,1)S(1)}, bf16[408,600]{1,0:T(8,128)(2,1)S(1)}, u32[]{:S(2)}, u32[]{:S(2)}) collective-permute-start(bf16[408,600]{1,0:T(8,128)(2,1)S(1)} %collective-permute-done.25.refs_1_), channel_id=1, source_target_pairs={{8,0},{9,1},{10,2},{11,3},{12,4},{13,5},{14,6},{15,7},{0,8},{1,9},... | collective-permute-start | bytes 1468808 | tf_op jit(solution)/shard_map/ppermute | solution.py:57
  106.9 1.3 collective-permute-start.14
  108.2 6.6 %collective-permute-done.16.refs_1_ = bf16[408,600]{1,0:T(8,128)(2,1)S(1)} collective-permute-done((bf16[408,600]{1,0:T(8,128)(2,1)S(1)}, bf16[408,600]{1,0:T(8,128)(2,1)S(1)}, u32[]{:S(2)}, u32[]{:S(2)}) %collective-permute-start.16) | collective-permute-done | bytes 489632 | tf_op jit(solution)/shard_map/ppermute | solution.py:57
  115.5 1.0 collective-permute-done.26.two_ref
  116.4 1.6 collective-permute-start.31
  118.0 5.8 %shard_map.67.k_ref = bf16[16,600,600]{2,1,0:T(8,128)(2,1)S(1)} custom-call(bf16[600,9600]{1,0:T(8,128)(2,1)S(1)} %bitcast.7), custom_call_target="tpu_custom_call" | custom-call | tf_op jit(solution)/shard_map/pallas_call | solution.py:135
  123.8 2.5 %shard_map.75 = (f32[2,8,600]{2,1,0:T(8,128)S(1)}, f32[8,600]{1,0:T(8,128)S(1)}, bf16[3,600,400]{2,1,0:T(8,128)(2,1)S(1)}) custom-call(bf16[16,600,600]{2,1,0:T(8,128)(2,1)S(1)} %shard_map.67.k_ref, bf16[400,600]{1,0:T(8,128)(2,1)S(1)} %bitcast.14, bf16[400,600]{1,0:T(8,128)(2,1)S(1)} %bitcast.15, bf16[408,600]{1,0:T(8,128)(2,1)S(1)} %get-tuple-element.44.refs_2_, ...), custom_call_target="tpu_custom_call" | custom-call | flops 1152000000 | bytes 3840000 | tf_op jit(solution)/shard_map/pallas_call | solution.py:32
  126.5 1.3 shard_map.78
  128.4 1.3 shard_map.79
  129.8 1.3 shard_map.80
  131.6 1.3 shard_map.81
  133.3 1.3 shard_map.82
  134.6 1.3 shard_map.83
  135.9 1.3 shard_map.84
  137.2 1.3 shard_map.85
  138.5 1.3 shard_map.86
  139.9 1.3 shard_map.87
  141.2 1.3 shard_map.88
  142.5 1.3 shard_map.89
  143.9 1.3 shard_map.90
  145.2 1.3 shard_map.91
  146.5 2.0 %shard_map.92 = (f32[2,8,600]{2,1,0:T(8,128)S(1)}, f32[8,600]{1,0:T(8,128)S(1)}, f32[2,600]{1,0:T(2,128)}, f32[8,128]{1,0:T(8,128)S(1)}) custom-call(bf16[16,600,600]{2,1,0:T(8,128)(2,1)S(1)} %shard_map.67.k_ref, bf16[400,600]{1,0:T(8,128)(2,1)S(1)} %collective-permute-done.3.refs_1_.refs_0_, ...), custom_call_target="tpu_custom_call", output_to_operand_aliasing={{0}: (5, {}), {1}: (6, {})} | custom-call | flops 576000000 | bytes 1920000 | tf_op jit(solution)/shard_map/pallas_call | solution.py:32
  148.9 0.8 collective-permute-done.40
  149.8 3.4 %collective-permute-start.41 = (f32[8,128]{1,0:T(8,128)S(1)}, f32[8,128]{1,0:T(8,128)S(1)}, u32[]{:S(2)}, u32[]{:S(2)}) collective-permute-start(f32[8,128]{1,0:T(8,128)S(1)} %add.15), channel_id=1, source_target_pairs={{32,0},{33,1},{34,2},{35,3},{36,4},{37,5},{38,6},{39,7},{40,8},{41... | collective-permute-start | bytes 12296 | tf_op jit(solution)/shard_map/ppermute | solution.py:57
  153.2 1.4 collective-permute-start.43
  154.6 1.0 collective-permute-done.42
  155.6 1.3 collective-permute-done.43
  156.9 3.2 %collective-permute-start.44 = (f32[8,128]{1,0:T(8,128)S(1)}, f32[8,128]{1,0:T(8,128)S(1)}, u32[]{:S(2)}, u32[]{:S(2)}) collective-permute-start(f32[8,128]{1,0:T(8,128)S(1)} %add_add_fusion), channel_id=1, source_target_pairs={{64,0},{65,1},{66,2},{67,3},{68,4},{69,5},{70,6},{71,7},{72,8},{73... | collective-permute-start | bytes 12296 | tf_op jit(solution)/shard_map/ppermute | solution.py:57
  160.1 1.0 collective-permute-done.44
  (69 shorter events, 6.7 us)
Async XLA Ops:
  0.6 11.5 %collective-permute-start.7 = (bf16[300,600]{1,0:T(8,128)(2,1)}, bf16[300,600]{1,0:T(8,128)(2,1)S(1)}, u32[]{:S(2)}, u32[]{:S(2)}) collective-permute-start(bf16[300,600]{1,0:T(8,128)(2,1)} %refs_0_.1), channel_id=1, source_target_pairs={{4,0},{5,1},{6,2},{7,3},{0,4},{1,5},{2,6},{3,7},{12,8},{13,9},{14,... | collective-permute-start | bytes 1080008 | tf_op jit(solution)/shard_map/ppermute | solution.py:57
  3.2 11.4 %collective-permute-start.5 = (bf16[300,600]{1,0:T(8,128)(2,1)}, bf16[300,600]{1,0:T(8,128)(2,1)S(1)}, u32[]{:S(2)}, u32[]{:S(2)}) collective-permute-start(bf16[300,600]{1,0:T(8,128)(2,1)} %refs_0_.1), channel_id=1, source_target_pairs={{2,0},{3,1},{0,2},{1,3},{6,4},{7,5},{4,6},{5,7},{10,8},{11,9},{8,1... | collective-permute-start | bytes 1080008 | tf_op jit(solution)/shard_map/ppermute | solution.py:57
  6.1 17.5 %collective-permute-start.10 = (bf16[300,600]{1,0:T(8,128)(2,1)}, bf16[300,600]{1,0:T(8,128)(2,1)S(1)}, u32[]{:S(2)}, u32[]{:S(2)}) collective-permute-start(bf16[300,600]{1,0:T(8,128)(2,1)} %refs_0_.1), channel_id=1, source_target_pairs={{1,0},{2,1},{3,2},{0,3},{5,4},{6,5},{7,6},{4,7},{9,8},{10,9},{11,1... | collective-permute-start | bytes 1080008 | tf_op jit(solution)/shard_map/ppermute | solution.py:57
  6.9 23.4 %collective-permute-start.38 = (bf16[400,600]{1,0:T(8,128)(2,1)}, bf16[400,600]{1,0:T(8,128)(2,1)S(1)}, u32[]{:S(2)}, u32[]{:S(2)}) collective-permute-start(bf16[400,600]{1,0:T(8,128)(2,1)} %bitcast.8), channel_id=1, source_target_pairs={{8,0},{9,1},{10,2},{11,3},{12,4},{13,5},{14,6},{15,7},{0,8},{1,9},... | collective-permute-start | bytes 1440008 | tf_op jit(solution)/shard_map/ppermute | solution.py:57
  8.4 18.5 %collective-permute-start.11 = (bf16[300,600]{1,0:T(8,128)(2,1)}, bf16[300,600]{1,0:T(8,128)(2,1)S(1)}, u32[]{:S(2)}, u32[]{:S(2)}) collective-permute-start(bf16[300,600]{1,0:T(8,128)(2,1)} %refs_0_.1), channel_id=1, source_target_pairs={{3,0},{0,1},{1,2},{2,3},{7,4},{4,5},{5,6},{6,7},{11,8},{8,9},{9,10... | collective-permute-start | bytes 1080008 | tf_op jit(solution)/shard_map/ppermute | solution.py:57
  12.1 18.1 %collective-permute-start.35 = (bf16[400,600]{1,0:T(8,128)(2,1)}, bf16[400,600]{1,0:T(8,128)(2,1)S(1)}, u32[]{:S(2)}, u32[]{:S(2)}) collective-permute-start(bf16[400,600]{1,0:T(8,128)(2,1)} %bitcast.9), channel_id=1, source_target_pairs={{48,0},{49,1},{50,2},{51,3},{52,4},{53,5},{54,6},{55,7},{56,8},{57... | collective-permute-start | bytes 1440008 | tf_op jit(solution)/shard_map/ppermute | solution.py:57
  14.6 16.8 %collective-permute-start.32 = (bf16[400,600]{1,0:T(8,128)(2,1)}, bf16[400,600]{1,0:T(8,128)(2,1)S(1)}, u32[]{:S(2)}, u32[]{:S(2)}) collective-permute-start(bf16[400,600]{1,0:T(8,128)(2,1)} %bitcast.10), channel_id=1, source_target_pairs={{16,0},{17,1},{18,2},{19,3},{20,4},{21,5},{22,6},{23,7},{24,8},{25... | collective-permute-start | bytes 1440008 | tf_op jit(solution)/shard_map/ppermute | solution.py:57
  23.6 14.1 %collective-permute-start = (bf16[400,600]{1,0:T(8,128)(2,1)}, bf16[400,600]{1,0:T(8,128)(2,1)S(1)}, u32[]{:S(2)}, u32[]{:S(2)}) collective-permute-start(bf16[400,600]{1,0:T(8,128)(2,1)} %bitcast.11), channel_id=1, source_target_pairs={{64,0},{65,1},{66,2},{67,3},{68,4},{69,5},{70,6},{71,7},{72,8},{73... | collective-permute-start | bytes 1440008 | tf_op jit(solution)/shard_map/ppermute | solution.py:57
  26.9 14.5 %collective-permute-start.8 = (bf16[300,600]{1,0:T(8,128)(2,1)S(1)}, bf16[300,600]{1,0:T(8,128)(2,1)S(1)}, u32[]{:S(2)}, u32[]{:S(2)}) collective-permute-start(bf16[300,600]{1,0:T(8,128)(2,1)S(1)} %collective-permute-done.7.refs_1_), channel_id=1, source_target_pairs={{1,0},{2,1},{3,2},{0,3},{5,4},{6,5},{7,6},{4,7},{9,8},{10,9},{11,1... | collective-permute-start | bytes 1080008 | tf_op jit(solution)/shard_map/ppermute | solution.py:57
  30.2 13.6 %collective-permute-start.9 = (bf16[300,600]{1,0:T(8,128)(2,1)S(1)}, bf16[300,600]{1,0:T(8,128)(2,1)S(1)}, u32[]{:S(2)}, u32[]{:S(2)}) collective-permute-start(bf16[300,600]{1,0:T(8,128)(2,1)S(1)} %collective-permute-done.7.refs_1_), channel_id=1, source_target_pairs={{3,0},{0,1},{1,2},{2,3},{7,4},{4,5},{5,6},{6,7},{11,8},{8,9},{9,10... | collective-permute-start | bytes 1080008 | tf_op jit(solution)/shard_map/ppermute | solution.py:57
  30.2 27.6 %collective-permute-start.36 = (bf16[400,600]{1,0:T(8,128)(2,1)S(1)}, bf16[400,600]{1,0:T(8,128)(2,1)S(1)}, u32[]{:S(2)}, u32[]{:S(2)}) collective-permute-start(bf16[400,600]{1,0:T(8,128)(2,1)S(1)} %collective-permute-done.35.refs_0_), channel_id=1, source_target_pairs={{8,0},{9,1},{10,2},{11,3},{12,4},{13,5},{14,6},{15,7},{0,8},{1,9},... | collective-permute-start | bytes 1440008 | tf_op jit(solution)/shard_map/ppermute | solution.py:57
  31.4 22.0 %collective-permute-start.6 = (bf16[300,600]{1,0:T(8,128)(2,1)S(1)}, bf16[300,600]{1,0:T(8,128)(2,1)S(1)}, u32[]{:S(2)}, u32[]{:S(2)}) collective-permute-start(bf16[300,600]{1,0:T(8,128)(2,1)S(1)} %collective-permute-done.5.refs_2_), channel_id=1, source_target_pairs={{4,0},{5,1},{6,2},{7,3},{0,4},{1,5},{2,6},{3,7},{12,8},{13,9},{14,... | collective-permute-start | bytes 1080008 | tf_op jit(solution)/shard_map/ppermute | solution.py:57
  37.7 20.5 %collective-permute-start.33 = (bf16[400,600]{1,0:T(8,128)(2,1)S(1)}, bf16[400,600]{1,0:T(8,128)(2,1)S(1)}, u32[]{:S(2)}, u32[]{:S(2)}) collective-permute-start(bf16[400,600]{1,0:T(8,128)(2,1)S(1)} %collective-permute-done.32.refs_0_), channel_id=1, source_target_pairs={{8,0},{9,1},{10,2},{11,3},{12,4},{13,5},{14,6},{15,7},{0,8},{1,9},... | collective-permute-start | bytes 1440008 | tf_op jit(solution)/shard_map/ppermute | solution.py:57
  41.4 17.1 %collective-permute-start.19 = (bf16[400,600]{1,0:T(8,128)(2,1)S(1)}, bf16[400,600]{1,0:T(8,128)(2,1)S(1)}, u32[]{:S(2)}, u32[]{:S(2)}) collective-permute-start(bf16[400,600]{1,0:T(8,128)(2,1)S(1)} %collective-permute-done.two_ref.refs_0_), channel_id=1, source_target_pairs={{48,0},{17,1},{50,2},{19,3},{52,4},{21,5},{54,6},{23,7},{24,8},{57... | collective-permute-start | bytes 1440008 | tf_op jit(solution)/shard_map/ppermute | solution.py:57
  43.8 17.1 %collective-permute-start.28 = (bf16[400,600]{1,0:T(8,128)(2,1)S(1)}, bf16[400,600]{1,0:T(8,128)(2,1)S(1)}, u32[]{:S(2)}, u32[]{:S(2)}) collective-permute-start(bf16[400,600]{1,0:T(8,128)(2,1)S(1)} %collective-permute-done.two_ref.refs_0_), channel_id=1, source_target_pairs={{8,0},{9,1},{10,2},{11,3},{12,4},{13,5},{14,6},{15,7},{0,8},{1,9},... | collective-permute-start | bytes 1440008 | tf_op jit(solution)/shard_map/ppermute | solution.py:57
  43.8 2.1 %copy-start.1 = (bf16[2,400,2400]{2,1,0:T(8,128)(2,1)S(1)}, bf16[2,400,2400]{2,1,0:T(8,128)(2,1)}, u32[]{:S(2)}) copy-start(bf16[2,400,2400]{2,1,0:T(8,128)(2,1)} %param.4) | copy-start | bytes 11520004
  45.9 3.4 %copy-start.2 = (bf16[300,600]{1,0:T(8,128)(2,1)S(1)}, bf16[300,600]{1,0:T(8,128)(2,1)}, u32[]{:S(2)}) copy-start(bf16[300,600]{1,0:T(8,128)(2,1)} %refs_0_.1) | copy-start | bytes 1080004
  51.6 1.6 %copy-start = (bf16[600,400]{0,1:T(8,128)(2,1)S(1)}, bf16[600,400]{0,1:T(8,128)(2,1)}, u32[]{:S(2)}) copy-start(bf16[600,400]{0,1:T(8,128)(2,1)} %param.6) | copy-start | bytes 1440004
  53.3 64.8 %slice-start = ((s8[11520000]{0:T(1024)(128)(4,1)}), s8[4194304]{0:T(1024)(128)(4,1)S(1)}, s32[]{:S(2)}) async-start(s8[11520000]{0:T(1024)(128)(4,1)} %bitcast.6), calls=%async_computation | async-start | bytes 8388608
  53.3 64.7 %slice-start.1 = ((s8[11520000]{0:T(1024)(128)(4,1)}), s8[4194304]{0:T(1024)(128)(4,1)S(1)}, s32[]{:S(2)}) async-start(s8[11520000]{0:T(1024)(128)(4,1)} %bitcast.6), calls=%async_computation.1 | async-start | bytes 8388608
  53.4 14.3 %collective-permute-start.1 = (bf16[400,600]{1,0:T(8,128)(2,1)S(1)}, bf16[400,600]{1,0:T(8,128)(2,1)S(1)}, u32[]{:S(2)}, u32[]{:S(2)}) collective-permute-start(bf16[400,600]{1,0:T(8,128)(2,1)S(1)} %shard_map.68), channel_id=1, source_target_pairs={{32,0},{33,1},{34,2},{35,3},{36,4},{37,5},{38,6},{39,7},{40,8},{41... | collective-permute-start | bytes 1440008 | tf_op jit(solution)/shard_map/ppermute | solution.py:57
  56.8 61.2 %slice-start.2 = ((s8[11520000]{0:T(1024)(128)(4,1)}), s8[3131392]{0:T(1024)(128)(4,1)S(1)}, s32[]{:S(2)}) async-start(s8[11520000]{0:T(1024)(128)(4,1)} %bitcast.6), calls=%async_computation.2 | async-start | bytes 6262784
  57.8 13.1 %collective-permute-start.39 = (bf16[408,600]{1,0:T(8,128)(2,1)S(1)}, bf16[408,600]{1,0:T(8,128)(2,1)S(1)}, u32[]{:S(2)}, u32[]{:S(2)}) collective-permute-start(bf16[408,600]{1,0:T(8,128)(2,1)S(1)} %get-tuple-element.47), channel_id=1, source_target_pairs={{8,0},{9,1},{10,2},{11,3},{12,4},{13,5},{14,6},{15,7},{0,8},{1,9},... | collective-permute-start | bytes 1468808 | tf_op jit(solution)/shard_map/ppermute | solution.py:57
  58.2 21.5 %collective-permute-start.23 = (bf16[408,600]{1,0:T(8,128)(2,1)S(1)}, bf16[408,600]{1,0:T(8,128)(2,1)S(1)}, u32[]{:S(2)}, u32[]{:S(2)}) collective-permute-start(bf16[408,600]{1,0:T(8,128)(2,1)S(1)} %get-tuple-element.44.refs_2_), channel_id=1, source_target_pairs={{48,0},{49,1},{50,2},{51,3},{52,4},{53,5},{54,6},{55,7},{56,8},{57... | collective-permute-start | bytes 1468808 | tf_op jit(solution)/shard_map/ppermute | solution.py:57
  58.5 22.4 %collective-permute-start.25 = (bf16[408,600]{1,0:T(8,128)(2,1)S(1)}, bf16[408,600]{1,0:T(8,128)(2,1)S(1)}, u32[]{:S(2)}, u32[]{:S(2)}) collective-permute-start(bf16[408,600]{1,0:T(8,128)(2,1)S(1)} %get-tuple-element.45.refs_3_), channel_id=1, source_target_pairs={{16,0},{17,1},{18,2},{19,3},{20,4},{21,5},{22,6},{23,7},{24,8},{25... | collective-permute-start | bytes 1468808 | tf_op jit(solution)/shard_map/ppermute | solution.py:57
  60.9 20.8 %collective-permute-start.12 = (bf16[408,600]{1,0:T(8,128)(2,1)S(1)}, bf16[408,600]{1,0:T(8,128)(2,1)S(1)}, u32[]{:S(2)}, u32[]{:S(2)}) collective-permute-start(bf16[408,600]{1,0:T(8,128)(2,1)S(1)} %get-tuple-element.42), channel_id=1, source_target_pairs={{64,0},{65,1},{66,2},{67,3},{68,4},{69,5},{70,6},{71,7},{72,8},{73... | collective-permute-start | bytes 1468808 | tf_op jit(solution)/shard_map/ppermute | solution.py:57
  67.7 18.5 %collective-permute-start.15 = (bf16[408,600]{1,0:T(8,128)(2,1)S(1)}, bf16[408,600]{1,0:T(8,128)(2,1)S(1)}, u32[]{:S(2)}, u32[]{:S(2)}) collective-permute-start(bf16[408,600]{1,0:T(8,128)(2,1)S(1)} %get-tuple-element.43), channel_id=1, source_target_pairs={{64,0},{65,1},{66,2},{67,3},{68,4},{69,5},{70,6},{71,7},{72,8},{73... | collective-permute-start | bytes 1468808 | tf_op jit(solution)/shard_map/ppermute | solution.py:57
  70.9 16.9 %collective-permute-start.30 = (bf16[400,600]{1,0:T(8,128)(2,1)S(1)}, bf16[400,600]{1,0:T(8,128)(2,1)S(1)}, u32[]{:S(2)}, u32[]{:S(2)}) collective-permute-start(bf16[400,600]{1,0:T(8,128)(2,1)S(1)} %collective-permute-done.19.refs_0_), channel_id=1, source_target_pairs={{8,0},{9,1},{10,2},{11,3},{12,4},{13,5},{14,6},{15,7},{0,8},{1,9},... | collective-permute-start | bytes 1440008 | tf_op jit(solution)/shard_map/ppermute | solution.py:57
  79.7 12.8 %collective-permute-start.2 = (bf16[400,600]{1,0:T(8,128)(2,1)S(1)}, bf16[400,600]{1,0:T(8,128)(2,1)S(1)}, u32[]{:S(2)}, u32[]{:S(2)}) collective-permute-start(bf16[400,600]{1,0:T(8,128)(2,1)S(1)} %collective-permute-done.1.refs_0_.refs_1_), channel_id=1, source_target_pairs={{1,0},{0,1},{3,2},{2,3},{5,4},{4,5},{7,6},{6,7},{9,8},{8,9},{11,10... | collective-permute-start | bytes 1440008 | tf_op jit(solution)/shard_map/ppermute | solution.py:57
  80.9 13.5 %collective-permute-start.4 = (bf16[400,600]{1,0:T(8,128)(2,1)S(1)}, bf16[400,600]{1,0:T(8,128)(2,1)S(1)}, u32[]{:S(2)}, u32[]{:S(2)}) collective-permute-start(bf16[400,600]{1,0:T(8,128)(2,1)S(1)} %collective-permute-done.1.refs_0_.refs_1_), channel_id=1, source_target_pairs={{8,0},{9,1},{10,2},{11,3},{12,4},{13,5},{14,6},{15,7},{0,8},{1,9},... | collective-permute-start | bytes 1440008 | tf_op jit(solution)/shard_map/ppermute | solution.py:57
  81.7 21.8 %collective-permute-start.20 = (bf16[400,600]{1,0:T(8,128)(2,1)S(1)}, bf16[400,600]{1,0:T(8,128)(2,1)S(1)}, u32[]{:S(2)}, u32[]{:S(2)}) collective-permute-start(bf16[400,600]{1,0:T(8,128)(2,1)S(1)} %collective-permute-done.19.refs_0_), channel_id=1, source_target_pairs={{1,0},{0,1},{3,2},{2,3},{5,4},{4,5},{7,6},{6,7},{9,8},{8,9},{11,10... | collective-permute-start | bytes 1440008 | tf_op jit(solution)/shard_map/ppermute | solution.py:57
  86.2 18.6 %collective-permute-start.37 = (bf16[408,600]{1,0:T(8,128)(2,1)S(1)}, bf16[408,600]{1,0:T(8,128)(2,1)S(1)}, u32[]{:S(2)}, u32[]{:S(2)}) collective-permute-start(bf16[408,600]{1,0:T(8,128)(2,1)S(1)} %collective-permute-done.23.refs_1_), channel_id=1, source_target_pairs={{8,0},{9,1},{10,2},{11,3},{12,4},{13,5},{14,6},{15,7},{0,8},{1,9},... | collective-permute-start | bytes 1468808 | tf_op jit(solution)/shard_map/ppermute | solution.py:57
  87.9 18.9 %collective-permute-start.13 = (bf16[408,600]{1,0:T(8,128)(2,1)S(1)}, bf16[408,600]{1,0:T(8,128)(2,1)S(1)}, u32[]{:S(2)}, u32[]{:S(2)}) collective-permute-start(bf16[408,600]{1,0:T(8,128)(2,1)S(1)} %collective-permute-done.12.one_ref), channel_id=1, source_target_pairs={{48,0},{17,1},{50,2},{19,3},{52,4},{21,5},{54,6},{23,7},{24,8},{57... | collective-permute-start | bytes 1468808 | tf_op jit(solution)/shard_map/ppermute | solution.py:57
  92.5 14.4 %collective-permute-start.24 = (bf16[408,600]{1,0:T(8,128)(2,1)S(1)}, bf16[408,600]{1,0:T(8,128)(2,1)S(1)}, u32[]{:S(2)}, u32[]{:S(2)}) collective-permute-start(bf16[408,600]{1,0:T(8,128)(2,1)S(1)} %collective-permute-done.23.refs_1_), channel_id=1, source_target_pairs={{48,0},{56,8},{0,16},{8,24},{112,64},{120,72},{64,80},{72,88},{49,... | collective-permute-start | bytes 1468808 | tf_op jit(solution)/shard_map/ppermute | solution.py:81
  94.4 20.4 %collective-permute-start.16 = (bf16[408,600]{1,0:T(8,128)(2,1)S(1)}, bf16[408,600]{1,0:T(8,128)(2,1)S(1)}, u32[]{:S(2)}, u32[]{:S(2)}) collective-permute-start(bf16[408,600]{1,0:T(8,128)(2,1)S(1)} %collective-permute-done.15.two_ref), channel_id=1, source_target_pairs={{16,0},{49,1},{18,2},{51,3},{20,4},{53,5},{22,6},{55,7},{56,8},{25... | collective-permute-start | bytes 1468808 | tf_op jit(solution)/shard_map/ppermute | solution.py:57
  103.5 13.0 %collective-permute-start.26 = (bf16[408,600]{1,0:T(8,128)(2,1)S(1)}, bf16[408,600]{1,0:T(8,128)(2,1)S(1)}, u32[]{:S(2)}, u32[]{:S(2)}) collective-permute-start(bf16[408,600]{1,0:T(8,128)(2,1)S(1)} %collective-permute-done.25.refs_1_), channel_id=1, source_target_pairs={{48,32},{56,40},{0,48},{8,56},{112,96},{120,104},{64,112},{72,120}... | collective-permute-start | bytes 1468808 | tf_op jit(solution)/shard_map/ppermute | solution.py:81
  104.8 21.6 %collective-permute-start.34 = (bf16[408,600]{1,0:T(8,128)(2,1)S(1)}, bf16[408,600]{1,0:T(8,128)(2,1)S(1)}, u32[]{:S(2)}, u32[]{:S(2)}) collective-permute-start(bf16[408,600]{1,0:T(8,128)(2,1)S(1)} %collective-permute-done.25.refs_1_), channel_id=1, source_target_pairs={{8,0},{9,1},{10,2},{11,3},{12,4},{13,5},{14,6},{15,7},{0,8},{1,9},... | collective-permute-start | bytes 1468808 | tf_op jit(solution)/shard_map/ppermute | solution.py:57
  106.8 21.0 %collective-permute-start.29 = (bf16[408,600]{1,0:T(8,128)(2,1)S(1)}, bf16[408,600]{1,0:T(8,128)(2,1)S(1)}, u32[]{:S(2)}, u32[]{:S(2)}) collective-permute-start(bf16[408,600]{1,0:T(8,128)(2,1)S(1)} %shard_map.77.refs_1_), channel_id=1, source_target_pairs={{8,0},{9,1},{10,2},{11,3},{12,4},{13,5},{14,6},{15,7},{0,8},{1,9},... | collective-permute-start | bytes 1468808 | tf_op jit(solution)/shard_map/ppermute | solution.py:57
  106.9 22.8 %collective-permute-start.14 = (bf16[408,600]{1,0:T(8,128)(2,1)S(1)}, bf16[408,600]{1,0:T(8,128)(2,1)S(1)}, u32[]{:S(2)}, u32[]{:S(2)}) collective-permute-start(bf16[408,600]{1,0:T(8,128)(2,1)S(1)} %collective-permute-done.13.refs_1_), channel_id=1, source_target_pairs={{17,1},{19,3},{21,5},{23,7},{24,8},{26,10},{28,12},{30,14},{33,17}... | collective-permute-start | bytes 1468808 | tf_op jit(solution)/shard_map/ppermute | solution.py:96
  114.8 16.2 %collective-permute-start.17 = (bf16[408,600]{1,0:T(8,128)(2,1)S(1)}, bf16[408,600]{1,0:T(8,128)(2,1)S(1)}, u32[]{:S(2)}, u32[]{:S(2)}) collective-permute-start(bf16[408,600]{1,0:T(8,128)(2,1)S(1)} %collective-permute-done.16.refs_1_), channel_id=1, source_target_pairs={{16,0},{18,2},{20,4},{22,6},{25,9},{27,11},{29,13},{31,15},{32,16}... | collective-permute-start | bytes 1468808 | tf_op jit(solution)/shard_map/ppermute | solution.py:96
  116.4 16.5 %collective-permute-start.31 = (bf16[408,600]{1,0:T(8,128)(2,1)S(1)}, bf16[408,600]{1,0:T(8,128)(2,1)S(1)}, u32[]{:S(2)}, u32[]{:S(2)}) collective-permute-start(bf16[408,600]{1,0:T(8,128)(2,1)S(1)} %collective-permute-done.13.refs_1_), channel_id=1, source_target_pairs={{8,0},{9,1},{10,2},{11,3},{12,4},{13,5},{14,6},{15,7},{0,8},{1,9},... | collective-permute-start | bytes 1468808 | tf_op jit(solution)/shard_map/ppermute | solution.py:57
  126.4 14.8 %collective-permute-start.27 = (bf16[408,600]{1,0:T(8,128)(2,1)S(1)}, bf16[408,600]{1,0:T(8,128)(2,1)S(1)}, u32[]{:S(2)}, u32[]{:S(2)}) collective-permute-start(bf16[408,600]{1,0:T(8,128)(2,1)S(1)} %shard_map.76.refs_2_), channel_id=1, source_target_pairs={{8,0},{9,1},{10,2},{11,3},{12,4},{13,5},{14,6},{15,7},{0,8},{1,9},... | collective-permute-start | bytes 1468808 | tf_op jit(solution)/shard_map/ppermute | solution.py:57
  127.8 13.4 %collective-permute-start.3 = (bf16[400,600]{1,0:T(8,128)(2,1)S(1)}, bf16[400,600]{1,0:T(8,128)(2,1)S(1)}, u32[]{:S(2)}, u32[]{:S(2)}) collective-permute-start(bf16[400,600]{1,0:T(8,128)(2,1)S(1)} %collective-permute-done.2.refs_1_.refs_0_), channel_id=1, source_target_pairs={{8,0},{9,1},{10,2},{11,3},{12,4},{13,5},{14,6},{15,7},{0,8},{1,9},... | collective-permute-start | bytes 1440008 | tf_op jit(solution)/shard_map/ppermute | solution.py:57
  129.7 14.2 %collective-permute-start.22 = (bf16[408,600]{1,0:T(8,128)(2,1)S(1)}, bf16[408,600]{1,0:T(8,128)(2,1)S(1)}, u32[]{:S(2)}, u32[]{:S(2)}) collective-permute-start(bf16[408,600]{1,0:T(8,128)(2,1)S(1)} %collective-permute-done.16.refs_1_), channel_id=1, source_target_pairs={{8,0},{9,1},{10,2},{11,3},{12,4},{13,5},{14,6},{15,7},{0,8},{1,9},... | collective-permute-start | bytes 1468808 | tf_op jit(solution)/shard_map/ppermute | solution.py:57
  131.0 12.8 %collective-permute-start.21 = (bf16[400,600]{1,0:T(8,128)(2,1)S(1)}, bf16[400,600]{1,0:T(8,128)(2,1)S(1)}, u32[]{:S(2)}, u32[]{:S(2)}) collective-permute-start(bf16[400,600]{1,0:T(8,128)(2,1)S(1)} %collective-permute-done.20.refs_0_), channel_id=1, source_target_pairs={{8,0},{9,1},{10,2},{11,3},{12,4},{13,5},{14,6},{15,7},{0,8},{1,9},... | collective-permute-start | bytes 1440008 | tf_op jit(solution)/shard_map/ppermute | solution.py:57
  133.0 13.5 %collective-permute-start.18 = (bf16[408,600]{1,0:T(8,128)(2,1)S(1)}, bf16[408,600]{1,0:T(8,128)(2,1)S(1)}, u32[]{:S(2)}, u32[]{:S(2)}) collective-permute-start(bf16[408,600]{1,0:T(8,128)(2,1)S(1)} %shard_map.74.refs_2_), channel_id=1, source_target_pairs={{8,0},{9,1},{10,2},{11,3},{12,4},{13,5},{14,6},{15,7},{0,8},{1,9},... | collective-permute-start | bytes 1468808 | tf_op jit(solution)/shard_map/ppermute | solution.py:57
  148.5 1.3 collective-permute-start.40
  149.8 4.8 %collective-permute-start.41 = (f32[8,128]{1,0:T(8,128)S(1)}, f32[8,128]{1,0:T(8,128)S(1)}, u32[]{:S(2)}, u32[]{:S(2)}) collective-permute-start(f32[8,128]{1,0:T(8,128)S(1)} %add.15), channel_id=1, source_target_pairs={{32,0},{33,1},{34,2},{35,3},{36,4},{37,5},{38,6},{39,7},{40,8},{41... | collective-permute-start | bytes 12296 | tf_op jit(solution)/shard_map/ppermute | solution.py:57
  153.1 2.5 %collective-permute-start.42 = (f32[8,128]{1,0:T(8,128)S(1)}, f32[8,128]{1,0:T(8,128)S(1)}, u32[]{:S(2)}, u32[]{:S(2)}) collective-permute-start(f32[8,128]{1,0:T(8,128)S(1)} %add.15), channel_id=1, source_target_pairs={{16,0},{17,1},{18,2},{19,3},{20,4},{21,5},{22,6},{23,7},{24,8},{25... | collective-permute-start | bytes 12296 | tf_op jit(solution)/shard_map/ppermute | solution.py:57
  153.2 3.7 %collective-permute-start.43 = (f32[8,128]{1,0:T(8,128)S(1)}, f32[8,128]{1,0:T(8,128)S(1)}, u32[]{:S(2)}, u32[]{:S(2)}) collective-permute-start(f32[8,128]{1,0:T(8,128)S(1)} %add.15), channel_id=1, source_target_pairs={{48,0},{49,1},{50,2},{51,3},{52,4},{53,5},{54,6},{55,7},{56,8},{57... | collective-permute-start | bytes 12296 | tf_op jit(solution)/shard_map/ppermute | solution.py:57
  156.9 4.2 %collective-permute-start.44 = (f32[8,128]{1,0:T(8,128)S(1)}, f32[8,128]{1,0:T(8,128)S(1)}, u32[]{:S(2)}, u32[]{:S(2)}) collective-permute-start(f32[8,128]{1,0:T(8,128)S(1)} %add_add_fusion), channel_id=1, source_target_pairs={{64,0},{65,1},{66,2},{67,3},{68,4},{69,5},{70,6},{71,7},{72,8},{73... | collective-permute-start | bytes 12296 | tf_op jit(solution)/shard_map/ppermute | solution.py:57
